TPU v7x, 256 devices: a whole 4x4x8 slice. The times are simulated.
256 devices in a mesh: trial: 4 (over z_lo), ep: 4 (over y), fsdp: 16 (over z_hi, x, core).
Axes of the slice: x: 4, y: 4, z: 8 (z_hi: 2, z_lo: 4; z = z_hi * 4 + z_lo), core: 2. Of those that a mesh axis runs over, the one named last changes fastest.
Arguments:
- master_down: float32 [256, 1024, 2048], P(('trial', 'ep'), None, 'fsdp'), parts along dimension 0, may hold values from -0.25 to 0.25
- router_weight: float32 [8192, 64], P(('trial', 'fsdp'), 'ep'), parts along dimension 0, may hold values from -0.125 to 0.125
- router_gain: float32 [8192], P(('trial', 'fsdp')), parts along dimension 0, may hold values from 0.25 to 1.75
Outputs:
- final_down: bfloat16 [256, 1024, 2048], P(('trial', 'ep'), 'fsdp'), parts along dimension 0
- scale_down: float32 [256, 1024], P(('trial', 'ep'), 'fsdp'), parts along dimension 0
- serve_router: bfloat16 [8192, 64], P('trial'), parts along dimension 0
There are 4 independent parts, one for each index of `trial`. A program takes and returns all parts, laid end to end along the dimension named above; each array names one. Nothing has to cross between parts.
All inputs are finite; a program needn't handle non-finite values. Where the computation divides by a largest or mean magnitude, that divisor is 1e-20 or more.
Results may differ from a plain program's by a relative error of at most 0.001.
Values may be sent and summed in bfloat16 or wider, within the bound.
No kernel may reach another device: no remote copies, remote signals or barrier semaphores. Data moves between devices by JAX's collectives and lax.ppermute only.
A program may use at most 64 MiB of HBM per device.

v0:
```python
import jax
import jax.numpy as jnp
from jax import lax
from jax.sharding import PartitionSpec as P


def copy_for_each(shard, axis):
    copies = jnp.broadcast_to(shard, (lax.axis_size(axis), *shard.shape))
    return lax.all_to_all(copies, axis, split_axis=0, concat_axis=0, tiled=True)


def taken_together(shard, axis):
    return copy_for_each(shard, axis).max(axis=0)


def laid_out(blocks, dim):
    lengths = list(blocks.shape[1:])
    lengths[dim] *= blocks.shape[0]
    return jnp.moveaxis(blocks, 0, dim).reshape(lengths)


def gathered_copies(shard, axis, dim):
    blocks = copy_for_each(shard, axis)
    return laid_out(blocks, dim)


def shards(master_down, router_weight, router_gain):
    scale_down = taken_together(jnp.max(jnp.abs(master_down), axis=2), "fsdp")
    narrow_down = (master_down / jnp.expand_dims(scale_down, 2)).astype(jnp.bfloat16)
    final_down = lax.all_to_all(narrow_down, "fsdp", split_axis=1, concat_axis=2, tiled=True)
    scale_down = lax.dynamic_slice_in_dim(
        scale_down, lax.axis_index("fsdp") * final_down.shape[1], final_down.shape[1], axis=1
    )
    part_router = (router_weight * router_gain[:, None]).astype(jnp.bfloat16)
    row_router = gathered_copies(part_router, "fsdp", 0)
    serve_router = lax.all_gather(row_router, "ep", axis=1, tiled=True)
    return (final_down, scale_down, serve_router)


def solution(mesh):
    return jax.shard_map(
        shards,
        mesh=mesh,
        in_specs=(
            P(("trial", "ep"), None, "fsdp"),
            P(("trial", "fsdp"), "ep"),
            P(("trial", "fsdp")),
        ),
        out_specs=(P(("trial", "ep"), "fsdp", None), P(("trial", "ep"), "fsdp"), P("trial", None)),
        check_vma=False,
    )
```

profile of v0, /device:TPU:55, one launch (start us, length us, event | category | flops | bytes accessed | tf_op | source)
XLA Modules:
  0.0 194.5 jit_solution(12414777083532193542)
XLA Ops:
  0.6 0.0 copy-start
  0.6 0.0 copy-start.1
  0.7 5.6 %abs_reduce_fusion = f32[16,1024]{1,0:T(8,128)S(1)} fusion(f32[16,1024,128]{2,1,0:T(8,128)} %param.3), kind=kLoop, calls=%fused_computation.2 | loop fusion | flops 4177920 | bytes 8454144 | tf_op jit(solution)/shard_map/reduce_max | solution.py:28
  6.3 1.1 broadcast_in_dim.8
  7.4 10.8 %all-to-all-start = ((f32[16,16,1024]{2,1,0:T(8,128)}), f32[16,16,1024]{2,1,0:T(8,128)S(1)}, u32[]{:S(2)}, u32[]{:S(2)}) async-start(f32[16,16,1024]{2,1,0:T(8,128)} %broadcast_in_dim.8), calls=%async_computation | async-start | bytes 2097152 | tf_op jit(solution)/shard_map/all_to_all | solution.py:9
  18.2 0.0 copy-done
  18.2 0.0 copy-done.1
  18.2 30.0 %all-to-all-done = f32[16,16,1024]{2,1,0:T(8,128)S(1)} async-done(((f32[16,16,1024]{2,1,0:T(8,128)}), f32[16,16,1024]{2,1,0:T(8,128)S(1)}, u32[]{:S(2)}, u32[]{:S(2)}) %all-to-all-start) | async-done | bytes 1048608 | tf_op jit(solution)/shard_map/all_to_all | solution.py:9
  48.2 0.6 broadcast_in_dim.9
  48.8 5.0 %all-to-all-start.2 = ((bf16[16,128,16]{1,2,0:T(8,128)(2,1)}), bf16[16,128,16]{1,2,0:T(8,128)(2,1)S(1)}, u32[]{:S(2)}, u32[]{:S(2)}) async-start(bf16[16,128,16]{1,2,0:T(8,128)(2,1)} %broadcast_in_dim.9), calls=%async_computation.2 | async-start | bytes 131072 | tf_op jit(solution)/shard_map/all_to_all | solution.py:9
  53.8 0.1 reduce_max.19
  53.9 0.2 copy.14
  54.1 9.6 %fusion = bf16[16,1024,128]{2,0,1:T(8,128)(2,1)} fusion(f32[16,1024,128]{2,1,0:T(8,128)} %param.3, f32[16,1024]{0,1:T(8,128)S(1)} %copy.14), kind=kLoop, calls=%fused_computation.1 | loop fusion | flops 4194304 | bytes 12648448 | tf_op jit(solution)/shard_map/convert_element_type | solution.py:29
  63.7 0.0 all-to-all-done.2
  63.7 9.7 %all-to-all-start.1 = ((bf16[16,1024,128]{2,0,1:T(8,128)(2,1)}), bf16[16,1024,128]{2,0,1:T(8,128)(2,1)}, u32[]{:S(2)}, u32[]{:S(2)}) async-start(bf16[16,1024,128]{2,0,1:T(8,128)(2,1)} %fusion), calls=%async_computation.1 | async-start | bytes 8388608 | tf_op jit(solution)/shard_map/all_to_all | solution.py:30
  73.4 9.4 %all_gather.3 = bf16[2048,64]{0,1:T(8,128)(2,1)S(1)} all-gather(bf16[2048,16]{0,1:T(8,128)(2,1)S(1)} %copy_bitcast_fusion), channel_id=1, replica_groups=mesh['trial'=4,'ep'=4,'fsdp'=16] {'ep'}, dimensions={1}, use_global_device_ids=true | all-gather | bytes 327680 | tf_op jit(solution)/shard_map/all_gather | solution.py:36
  82.7 0.7 constant_dynamic-slice_fusion
  83.4 96.2 %all-to-all-done.1 = bf16[16,1024,128]{2,0,1:T(8,128)(2,1)} async-done(((bf16[16,1024,128]{2,0,1:T(8,128)(2,1)}), bf16[16,1024,128]{2,0,1:T(8,128)(2,1)}, u32[]{:S(2)}, u32[]{:S(2)}) %all-to-all-start.1) | async-done | bytes 4194336 | tf_op jit(solution)/shard_map/all_to_all | solution.py:30
  179.7 6.9 %copy.16 = bf16[16,64,16,128]{3,2,1,0:T(8,128)(2,1)} copy(bf16[16,64,16,128]{3,0,1,2:T(8,128)(2,1)} %bitcast.1) | data formatting | bytes 8388608 | tf_op jit(solution)/shard_map/all_to_all | solution.py:30
  186.5 7.3 %all_to_all.23 = bf16[16,64,2048]{2,1,0:T(8,128)(2,1)} reshape(bf16[16,64,16,128]{3,2,1,0:T(8,128)(2,1)} %copy.16) | data formatting | bytes 8388608 | tf_op jit(solution)/shard_map/all_to_all | solution.py:30
  193.8 0.7 copy.24
  (2 shorter events, 0.0 us)
Async XLA Ops:
  0.6 17.5 %copy-start = (f32[128,16]{0,1:T(8,128)S(1)}, f32[128,16]{0,1:T(8,128)}, u32[]{:S(2)}) copy-start(f32[128,16]{0,1:T(8,128)} %param.4) | copy-start | bytes 24580
  0.6 17.5 %copy-start.1 = (f32[128]{0:T(128)S(1)}, f32[128]{0:T(128)}, u32[]{:S(2)}) copy-start(f32[128]{0:T(128)} %param.5) | copy-start | bytes 1540
  7.4 40.8 %all-to-all-start = ((f32[16,16,1024]{2,1,0:T(8,128)}), f32[16,16,1024]{2,1,0:T(8,128)S(1)}, u32[]{:S(2)}, u32[]{:S(2)}) async-start(f32[16,16,1024]{2,1,0:T(8,128)} %broadcast_in_dim.8), calls=%async_computation | async-start | bytes 2097152 | tf_op jit(solution)/shard_map/all_to_all | solution.py:9
  48.8 14.9 %all-to-all-start.2 = ((bf16[16,128,16]{1,2,0:T(8,128)(2,1)}), bf16[16,128,16]{1,2,0:T(8,128)(2,1)S(1)}, u32[]{:S(2)}, u32[]{:S(2)}) async-start(bf16[16,128,16]{1,2,0:T(8,128)(2,1)} %broadcast_in_dim.9), calls=%async_computation.2 | async-start | bytes 131072 | tf_op jit(solution)/shard_map/all_to_all | solution.py:9
  63.7 115.9 %all-to-all-start.1 = ((bf16[16,1024,128]{2,0,1:T(8,128)(2,1)}), bf16[16,1024,128]{2,0,1:T(8,128)(2,1)}, u32[]{:S(2)}, u32[]{:S(2)}) async-start(bf16[16,1024,128]{2,0,1:T(8,128)(2,1)} %fusion), calls=%async_computation.1 | async-start | bytes 8388608 | tf_op jit(solution)/shard_map/all_to_all | solution.py:30
where the time goes:
time: 195 us; the launch traced here: 194 us
  waiting for transfers between devices  126 us (65%)
  starting transfers between devices  25.5 us (13%)
  local copies, waits for them, and re-layouts  17.4 us (9%)
  other arithmetic  15.3 us (8%)
  blocking collectives  9.36 us (5%)
    all_to_all x1, waiting for transfers between devices, shards(): lax.all_to_all(narrow_down, 'fsdp', split_axis=1, concat_axis=2, tiled=True)  96.2 us
    all_to_all x2, waiting for transfers between devices, copy_for_each(): return lax.all_to_all(copies, axis, split_axis=0, concat_axis=0, tiled=True)  30 us
    all_to_all x2, starting transfers between devices, copy_for_each(): return lax.all_to_all(copies, axis, split_axis=0, concat_axis=0, tiled=True)  15.8 us
    all_to_all x2, local copies, waits for them, and re-layouts, shards(): lax.all_to_all(narrow_down, 'fsdp', split_axis=1, concat_axis=2, tiled=True)  14.1 us
    all_to_all x1, starting transfers between devices, shards(): lax.all_to_all(narrow_down, 'fsdp', split_axis=1, concat_axis=2, tiled=True)  9.66 us
    convert_element_type x1, other arithmetic, shards(): (master_down / jnp.expand_dims(scale_down, 2)).astype(jnp.bfloat16)  9.63 us
    all_gather x1, blocking collectives, shards(): serve_router = lax.all_gather(row_router, 'ep', axis=1, tiled=True)  9.36 us
    reduce_max x1, other arithmetic, shards(): scale_down = taken_together(jnp.max(jnp.abs(master_down), axis=2), 'fsdp')  5.62 us
  transfers between devices with their start and end apart: 3, of which 2 were waited for; matrix products, arithmetic and copies ran while one was open for 5% of the time, Pallas kernels for 0%

commit v1 on v0

v1 whole, which is shorter than its diff:
```python
import functools

import jax
import jax.numpy as jnp
from jax import lax
from jax.experimental import pallas as pl
from jax.experimental.pallas import tpu as pltpu
from jax.sharding import PartitionSpec as P


EARLY = 1
BF16, F32 = jnp.bfloat16, jnp.float32
ANY = pl.BlockSpec(memory_space=pl.ANY)
VMEM = pl.BlockSpec(memory_space=pltpu.VMEM)
SMEM = pl.BlockSpec(memory_space=pltpu.SMEM)
HOPS = [(dx, dc) for dx in range(4) for dc in range(2)]


def params(mebibytes):
    return pltpu.CompilerParams(vmem_limit_bytes=mebibytes * 2**20)


def cost(read, written):
    return pl.CostEstimate(flops=(read + written) * 4, bytes_accessed=read + written, transcendentals=0)


def route(dz, dx, dc):
    pairs = []
    for f in range(16):
        z, x, c = f // 8, f // 2 % 4, f % 2
        pairs.append((f, (z ^ dz) * 8 + (x + dx) % 4 * 2 + (c ^ dc)))
    return pairs


def partner(f, dz, dx, dc):
    z, x, c = f // 8, f // 2 % 4, f % 2
    z = z if dz == 0 else 1 - z
    c = c if dc == 0 else 1 - c
    return z * 8 + (x + dx) % 4 * 2 + c


def lanes(position):
    return pl.ds(pl.multiple_of(position * 128, 128), 128)


def local_kernel(w_ref, router_ref, gain_ref, out_ref, taken, sems):
    blocks, experts = taken.shape[:2]
    reads = []
    for b in range(blocks):
        reads.append(pltpu.make_async_copy(w_ref.at[:, pl.ds(128 * b, 128), :], taken.at[b], sems.at[b]))
        reads[-1].start()
    out_ref[:, 128 * blocks :] = router_ref[...] * gain_ref[...]
    lane = lax.broadcasted_iota(jnp.int32, (128, 128), 1)
    for b in range(blocks):
        reads[b].wait()
        total = jnp.zeros((128, 128), F32)
        for e in range(experts):
            row = jnp.max(jnp.abs(taken[b, e]), axis=1, keepdims=True)
            total = jnp.where(lane == e, row, total)
        out_ref[:, pl.ds(128 * b, 128)] = total.T[:experts]


def local_maxima(w, router, gain):
    experts, rows, _ = w.shape
    blocks = rows // 128
    return pl.pallas_call(
        local_kernel,
        out_shape=jax.ShapeDtypeStruct((experts, rows + 128), F32),
        in_specs=[ANY, VMEM, VMEM],
        out_specs=VMEM,
        scratch_shapes=[pltpu.VMEM((blocks, experts, 128, 128), F32), pltpu.SemaphoreType.DMA((blocks,))],
        compiler_params=params(56),
        cost_estimate=cost(8 * 2**20, 2**16),
        name="local_maxima",
    )(w, router, gain)


def inverse_columns(scale_ref, inverse, slot, block):
    inverse[pl.ds(128 * slot, 128), :] = jnp.concatenate([1.0 / scale_ref[:, lanes(block)]] * 8, axis=0).T


def across_kernel(hops, f_ref, w_ref, scale_ref, *refs):
    outs, (taken, inverse, made, in_sems, out_sems) = refs[: len(hops)], refs[len(hops) :]
    count = taken.shape[1]
    f = f_ref[0]
    targets = [partner(f, 1, *hop) for hop in hops]
    reads = []
    for k, target in enumerate(targets):
        rows = pl.ds(pl.multiple_of(target * 64, 64), 64)
        reads.append(pltpu.make_async_copy(w_ref.at[pl.ds(0, count), rows, :], taken.at[k], in_sems.at[k]))
        reads[-1].start()
    for dx in sorted({dx for dx, _ in hops}):
        inverse_columns(scale_ref, inverse, dx, partner(f, 1, dx, 0) // 2)
    writes = []
    for k, target in enumerate(targets):
        columns = inverse[pl.ds(pl.multiple_of(hops[k][0] * 128 + target % 2 * 64, 64), 64), :]
        reads[k].wait()
        for e in range(count):
            made[k, e] = (taken[k, e] * columns[:, e : e + 1]).astype(BF16)
        writes.append(pltpu.make_async_copy(made.at[k], outs[k], out_sems.at[k]))
        writes[-1].start()
    for write in writes:
        write.wait()


def across_pieces(hops, f, w, scale, count):
    n = len(hops)
    return pl.pallas_call(
        functools.partial(across_kernel, hops),
        out_shape=[jax.ShapeDtypeStruct((count, 64, 128), BF16)] * n,
        in_specs=[SMEM, ANY, VMEM],
        out_specs=[ANY] * n,
        scratch_shapes=[
            pltpu.VMEM((n, count, 64, 128), F32),
            pltpu.VMEM((512, 128), F32),
            pltpu.VMEM((n, count, 64, 128), BF16),
            pltpu.SemaphoreType.DMA((n,)),
            pltpu.SemaphoreType.DMA((n,)),
        ],
        compiler_params=params(56),
        cost_estimate=cost(n * 2**19, n * 2**18),
        name="across_pieces",
    )(f, w, scale)


def plane_kernel(f_ref, y_ref, w_ref, scale_ref, relay_ref, near_ref, r1_ref, r2_ref, r3_ref, *refs):
    outs, (final_ref, router_ref), (taken, inverse, made, in_sems, out_sems) = refs[:7], refs[7:9], refs[9:]
    experts, early = w_ref.shape[0], relay_ref.shape[0]
    f, y = f_ref[0], y_ref[0]
    reads = []
    for k, (dx, dc) in enumerate(HOPS):
        rows = pl.ds(pl.multiple_of(partner(f, 0, dx, dc) * 64, 64), 64)
        reads.append(pltpu.make_async_copy(w_ref.at[:, rows, :], taken.at[k], in_sems.at[k]))
        reads[-1].start()
    for dx in range(4):
        inverse_columns(scale_ref, inverse, dx, partner(f, 0, dx, 0) // 2)
    for k, (dx, dc) in enumerate(HOPS):
        target = partner(f, 0, dx, dc)
        local = pl.ds(pl.multiple_of(target % 8 * 64, 64), 64)
        columns = inverse[pl.ds(pl.multiple_of(dx * 128 + target % 2 * 64, 64), 64), :]
        reads[k].wait()
        for e in range(experts):
            made[k, e] = (taken[k, e] * columns[:, e : e + 1]).astype(BF16)
        for q in range(early):
            e = experts - early + q
            made[k, experts + q] = (relay_ref[q, local, :] * columns[:, e : e + 1]).astype(BF16)
        for plane in range(2):
            for dy, piece in enumerate((near_ref, r1_ref, r2_ref, r3_ref)):
                at = pl.multiple_of((y - dy + 4) % 4 * 16, 16)
                made[k, experts + early + plane, pl.ds(at, 16), :] = piece[plane]
    other = f + 8 - f // 8 * 16
    here = made.at[0]
    writes = [
        pltpu.make_async_copy(here.at[pl.ds(0, experts)], final_ref.at[:, :, lanes(f)], out_sems.at[0]),
        pltpu.make_async_copy(here.at[experts + early], router_ref.at[:, lanes(f)], out_sems.at[8]),
        pltpu.make_async_copy(here.at[experts + early + 1], router_ref.at[:, lanes(other)], out_sems.at[9]),
    ]
    if early:
        writes.append(
            pltpu.make_async_copy(
                here.at[pl.ds(experts, early)],
                final_ref.at[pl.ds(experts - early, early), :, lanes(other)],
                out_sems.at[10],
            )
        )
    for k in range(1, 8):
        writes.append(pltpu.make_async_copy(made.at[k], outs[k - 1], out_sems.at[k]))
    for write in writes:
        write.start()
    for write in writes:
        write.wait()


def plane_pieces(f, y, w, scale, relay, near, *received):
    experts, _, _ = w.shape
    blocks = experts + relay.shape[0] + 2
    return pl.pallas_call(
        plane_kernel,
        out_shape=[jax.ShapeDtypeStruct((blocks, 64, 128), BF16)] * 7
        + [jax.ShapeDtypeStruct((experts, 64, 2048), BF16), jax.ShapeDtypeStruct((64, 2048), BF16)],
        in_specs=[SMEM, SMEM, ANY] + [VMEM] * 6,
        out_specs=[ANY] * 9,
        scratch_shapes=[
            pltpu.VMEM((8, experts, 64, 128), F32),
            pltpu.VMEM((512, 128), F32),
            pltpu.VMEM((8, blocks, 64, 128), BF16),
            pltpu.SemaphoreType.DMA((8,)),
            pltpu.SemaphoreType.DMA((11,)),
        ],
        compiler_params=params(56),
        cost_estimate=cost(5 * 2**20, 3 * 2**20),
        name="plane_pieces",
    )(f, y, w, scale, relay, near, *received)


def place_across_kernel(hop, f_ref, piece_ref, _, final_ref, sem):
    source = partner(f_ref[0], 1, 4 - hop[0], hop[1])
    copy = pltpu.make_async_copy(piece_ref, final_ref.at[pl.ds(0, piece_ref.shape[0]), :, lanes(source)], sem)
    copy.start()
    copy.wait()


def place_across(hop, f, piece, final):
    return pl.pallas_call(
        functools.partial(place_across_kernel, hop),
        out_shape=jax.ShapeDtypeStruct(final.shape, final.dtype),
        in_specs=[SMEM, VMEM, ANY],
        out_specs=ANY,
        scratch_shapes=[pltpu.SemaphoreType.DMA],
        input_output_aliases={2: 0},
        compiler_params=params(2),
        cost_estimate=cost(2**18, 2**18),
        name="place_across",
    )(f, piece, final)


def place_plane_kernel(hop, early, f_ref, piece_ref, _, __, final_ref, router_ref, sems):
    experts = final_ref.shape[0]
    source = partner(f_ref[0], 0, 4 - hop[0], hop[1])
    other = source + 8 - source // 8 * 16
    copies = [
        pltpu.make_async_copy(piece_ref.at[pl.ds(0, experts)], final_ref.at[:, :, lanes(source)], sems.at[0]),
        pltpu.make_async_copy(piece_ref.at[experts + early], router_ref.at[:, lanes(source)], sems.at[1]),
        pltpu.make_async_copy(piece_ref.at[experts + early + 1], router_ref.at[:, lanes(other)], sems.at[2]),
    ]
    if early:
        copies.append(
            pltpu.make_async_copy(
                piece_ref.at[pl.ds(experts, early)],
                final_ref.at[pl.ds(experts - early, early), :, lanes(other)],
                sems.at[3],
            )
        )
    for copy in copies:
        copy.start()
    for copy in copies:
        copy.wait()


def place_plane(hop, early, f, piece, final, router):
    return pl.pallas_call(
        functools.partial(place_plane_kernel, hop, early),
        out_shape=[jax.ShapeDtypeStruct(final.shape, BF16), jax.ShapeDtypeStruct(router.shape, BF16)],
        in_specs=[SMEM, VMEM, ANY, ANY],
        out_specs=[ANY, ANY],
        scratch_shapes=[pltpu.SemaphoreType.DMA((4,))],
        input_output_aliases={2: 0, 3: 1},
        compiler_params=params(2),
        cost_estimate=cost(2**18, 2**18),
        name="place_plane",
    )(f, piece, final, router)


def send(piece, dz, dx, dc):
    return lax.ppermute(piece, "fsdp", route(dz, dx, dc))


def served(master_down, router_weight, router_gain):
    experts, rows, _ = master_down.shape
    position = lax.axis_index("fsdp")
    f = position.reshape(1)
    y = lax.axis_index("ep").reshape(1)

    local = local_maxima(master_down, router_weight.T, router_gain.reshape(1, -1))
    peer = send(local, 1, 0, 0)
    early = lax.dynamic_slice(
        master_down, (experts - EARLY, (1 - position // 8) * 512, 0), (EARLY, 512, 128)
    )
    relay = send(early, 1, 0, 0)
    scale = jnp.maximum(local[:, :rows], peer[:, :rows])
    near = jnp.stack([local[:, rows:], peer[:, rows:]]).astype(BF16)
    scale = jnp.maximum(scale, send(scale, 0, 0, 1))
    scale = functools.reduce(jnp.maximum, [scale] + [send(scale, 0, dx, 0) for dx in (1, 3, 2)])

    pieces = across_pieces(HOPS[:1], f, master_down, scale, experts - EARLY)
    pieces += across_pieces(HOPS[1:], f, master_down, scale, experts - EARLY)
    across = [send(piece, 1, *HOPS[k]) for k, piece in enumerate(pieces)]
    received = []
    for d in (1, 2, 3):
        received.append(lax.ppermute(near, "ep", [(i, (i + d) % 4) for i in range(4)]))
    *pieces, final, router = plane_pieces(f, y, master_down, scale, relay, near, *received)
    plane = [send(piece, 0, *HOPS[k + 1]) for k, piece in enumerate(pieces)]
    for k in range(2):
        final = place_across(HOPS[k], f, across[k], final)
    for k in range(7):
        final, router = place_plane(HOPS[k + 1], EARLY, f, plane[k], final, router)
    for k in range(2, 8):
        final = place_across(HOPS[k], f, across[k], final)
    own = lax.dynamic_slice_in_dim(scale, position * 64, 64, axis=1)
    return final, own, router.T


def solution(mesh):
    return jax.shard_map(
        served,
        mesh=mesh,
        in_specs=(
            P(("trial", "ep"), None, "fsdp"),
            P(("trial", "fsdp"), "ep"),
            P(("trial", "fsdp")),
        ),
        out_specs=(P(("trial", "ep"), "fsdp", None), P(("trial", "ep"), "fsdp"), P("trial", None)),
        check_vma=False,
    )
```

time: 195 us -> 158 us (0.81)
  the two profiles are of different devices: /device:TPU:55 before, /device:TPU:1 now
where the time goes in v1:
time: 158 us; the launch traced here: 157 us
  waiting for transfers between devices  79.2 us (50%)
  starting transfers between devices  39.3 us (25%)
  Pallas kernels  31.2 us (20%)
  local copies, waits for them, and re-layouts  4.82 us (3%)
    ppermute x21, waiting for transfers between devices, send(): return lax.ppermute(piece, 'fsdp', route(dz, dx, dc))  78 us
    ppermute x21, starting transfers between devices, send(): return lax.ppermute(piece, 'fsdp', route(dz, dx, dc))  34.3 us
    pallas_call x8, Pallas kernels, place_across(): pl.pallas_call(functools.partial(place_across_kernel, hop), out_shape=jax...  7.56 us
    pallas_call x2, Pallas kernels, across_pieces(): pl.pallas_call(functools.partial(across_kernel, hops), out_shape=[jax.Sha...  7.08 us
    pallas_call x1, Pallas kernels, local_maxima(): pl.pallas_call(local_kernel, out_shape=jax.ShapeDtypeStruct((experts, row...  5.7 us
    pallas_call x1, Pallas kernels, plane_pieces(): pl.pallas_call(plane_kernel, out_shape=[jax.ShapeDtypeStruct((blocks, 64,...  5.48 us
    pallas_call x7, Pallas kernels, place_plane(): pl.pallas_call(functools.partial(place_plane_kernel, hop, early), out_sha...  5.38 us
    ppermute x3, starting transfers between devices, served(): lax.ppermute(near, 'ep', [(i, (i + d) % 4) for i in range(4)])  4.99 us
  transfers between devices with their start and end apart: 24, of which 12 were waited for; matrix products, arithmetic and copies ran while one was open for 2% of the time, Pallas kernels for 15%

profile of v1, /device:TPU:1, one launch (start us, length us, event | category | flops | bytes accessed | tf_op | source)
XLA Modules:
  0.0 157.0 jit_solution(2895117746136641892)
XLA Ops:
  0.7 1.0 constant_dynamic-slice_fusion.1
  1.6 7.8 %collective-permute-start.11 = (f32[1,512,128]{2,1,0:T(8,128)S(1)}, f32[1,512,128]{2,1,0:T(8,128)S(1)}, u32[]{:S(2)}, u32[]{:S(2)}) collective-permute-start(f32[1,512,128]{2,1,0:T(8,128)S(1)} %constant_dynamic-slice_fusion.1), channel_id=1, source_target_pairs={{0,8},{1,9},{2,10},{3,11},{4,12},{5,13},{6,14},{7,15},{8,0},{9,1},... | collective-permute-start | bytes 786440 | tf_op jit(solution)/shard_map/ppermute | solution.py:255
  9.4 5.7 %local_maxima.1 = f32[16,1152]{1,0:T(8,128)} custom-call(f32[16,1024,128]{2,1,0:T(8,128)} %w_ref.7, f32[16,128]{1,0:T(8,128)} %bitcast.10, f32[1,128]{1,0:T(1,128)} %bitcast.11), custom_call_target="tpu_custom_call" | custom-call | flops 33816576 | bytes 8454144 | tf_op jit(solution)/shard_map/local_maxima/pallas_call | solution.py:66
  15.3 0.7 fusion
  16.0 11.8 %collective-permute-done = f32[16,1152]{1,0:T(8,128)S(1)} collective-permute-done((f32[16,1152]{1,0:T(8,128)}, f32[16,1152]{1,0:T(8,128)S(1)}, u32[]{:S(2)}, u32[]{:S(2)}) %collective-permute-start) | collective-permute-done | bytes 73760 | tf_op jit(solution)/shard_map/ppermute | solution.py:255
  27.8 0.8 slice_maximum_fusion
  28.6 1.5 collective-permute-start.1
  30.1 0.9 collective-permute-done.1
  31.0 1.3 collective-permute-start.2
  32.3 1.5 collective-permute-start.3
  33.8 1.5 collective-permute-start.4
  35.3 1.3 collective-permute-start.12
  36.6 2.6 %collective-permute-start.13 = (bf16[2,16,128]{2,1,0:T(8,128)(2,1)S(1)}, bf16[2,16,128]{2,1,0:T(8,128)(2,1)S(1)}, u32[]{:S(2)}, u32[]{:S(2)}) collective-permute-start(bf16[2,16,128]{2,1,0:T(8,128)(2,1)S(1)} %pad_maximum_fusion.near_ref), channel_id=1, source_target_pairs={{0,32},{16,48},{32,0},{48,16},{1,33},{17,49},{33,1},{49,17},{2,34}... | collective-permute-start | bytes 24584 | tf_op jit(solution)/shard_map/ppermute | solution.py:280
  39.2 1.1 collective-permute-start.14
  41.0 1.2 collective-permute-done.14.r3_ref
  42.8 5.5 %plane_pieces.1 = (bf16[19,64,128]{2,1,0:T(8,128)(2,1)}, bf16[19,64,128]{2,1,0:T(8,128)(2,1)}, bf16[19,64,128]{2,1,0:T(8,128)(2,1)}, bf16[19,64,128]{2,1,0:T(8,1...) custom-call(s32[1]{0:T(128)} %bitcast.f_ref, ...), custom_call_target="tpu_custom_call" | custom-call | flops 33554432 | bytes 8388608 | tf_op jit(solution)/shard_map/plane_pieces/pallas_call | solution.py:177
  48.3 2.6 %collective-permute-start.21 = (bf16[19,64,128]{2,1,0:T(8,128)(2,1)}, bf16[19,64,128]{2,1,0:T(8,128)(2,1)S(1)}, u32[]{:S(2)}, u32[]{:S(2)}) collective-permute-start(bf16[19,64,128]{2,1,0:T(8,128)(2,1)} %get-tuple-element.45), channel_id=1, source_target_pairs={{0,1},{1,0},{2,3},{3,2},{4,5},{5,4},{6,7},{7,6},{8,9},{9,8},{10,11... | collective-permute-start | bytes 933896 | tf_op jit(solution)/shard_map/ppermute | solution.py:255
  51.3 2.8 %across_pieces.3 = bf16[15,64,128]{2,1,0:T(8,128)(2,1)} custom-call(s32[1]{0:T(128)} %bitcast.f_ref, f32[16,1024,128]{2,1,0:T(8,128)} %w_ref.7, f32[16,1024]{1,0:T(8,128)} %maximum_maximum_fusion.scale_ref), custom_call_target="tpu_custom_call" | custom-call | flops 3145728 | bytes 786432 | tf_op jit(solution)/shard_map/across_pieces/pallas_call | solution.py:108
  54.1 1.3 collective-permute-start.23
  55.4 4.3 %across_pieces.2 = (bf16[15,64,128]{2,1,0:T(8,128)(2,1)}, bf16[15,64,128]{2,1,0:T(8,128)(2,1)}, bf16[15,64,128]{2,1,0:T(8,128)(2,1)}, bf16[15,64,128]{2,1,0:T(8,...) custom-call(s32[1]{0:T(128)} %bitcast.f_ref, ...), custom_call_target="tpu_custom_call" | custom-call | flops 22020096 | bytes 5505024 | tf_op jit(solution)/shard_map/across_pieces/pallas_call | solution.py:108
  59.7 5.0 %collective-permute-start.22 = (bf16[15,64,128]{2,1,0:T(8,128)(2,1)}, bf16[15,64,128]{2,1,0:T(8,128)(2,1)S(1)}, u32[]{:S(2)}, u32[]{:S(2)}) collective-permute-start(bf16[15,64,128]{2,1,0:T(8,128)(2,1)} %get-tuple-element.46), channel_id=1, source_target_pairs={{0,9},{1,8},{2,11},{3,10},{4,13},{5,12},{6,15},{7,14},{8,1},{9,0},... | collective-permute-start | bytes 737288 | tf_op jit(solution)/shard_map/ppermute | solution.py:255
  64.7 1.5 collective-permute-start.10
  66.2 5.6 %collective-permute-done.23.piece_ref = bf16[15,64,128]{2,1,0:T(8,128)(2,1)S(1)} collective-permute-done((bf16[15,64,128]{2,1,0:T(8,128)(2,1)}, bf16[15,64,128]{2,1,0:T(8,128)(2,1)S(1)}, u32[]{:S(2)}, u32[]{:S(2)}) %collective-permute-start.23) | collective-permute-done | bytes 245792 | tf_op jit(solution)/shard_map/ppermute | solution.py:255
  71.8 1.2 collective-permute-start.19
  73.0 4.4 %collective-permute-done.22.piece_ref = bf16[15,64,128]{2,1,0:T(8,128)(2,1)S(1)} collective-permute-done((bf16[15,64,128]{2,1,0:T(8,128)(2,1)}, bf16[15,64,128]{2,1,0:T(8,128)(2,1)S(1)}, u32[]{:S(2)}, u32[]{:S(2)}) %collective-permute-start.22) | collective-permute-done | bytes 245792 | tf_op jit(solution)/shard_map/ppermute | solution.py:255
  78.1 1.7 %collective-permute-start.18 = (bf16[19,64,128]{2,1,0:T(8,128)(2,1)S(1)}, bf16[19,64,128]{2,1,0:T(8,128)(2,1)S(1)}, u32[]{:S(2)}, u32[]{:S(2)}) collective-permute-start(bf16[19,64,128]{2,1,0:T(8,128)(2,1)S(1)} %copy-done.10), channel_id=1, source_target_pairs={{0,4},{1,5},{2,6},{3,7},{4,0},{5,1},{6,2},{7,3},{8,12},{9,13},{10,... | collective-permute-start | bytes 933896 | tf_op jit(solution)/shard_map/ppermute | solution.py:255
  79.8 5.3 %collective-permute-done.10.piece_ref = bf16[15,64,128]{2,1,0:T(8,128)(2,1)S(1)} collective-permute-done((bf16[15,64,128]{2,1,0:T(8,128)(2,1)}, bf16[15,64,128]{2,1,0:T(8,128)(2,1)S(1)}, u32[]{:S(2)}, u32[]{:S(2)}) %collective-permute-start.10) | collective-permute-done | bytes 245792 | tf_op jit(solution)/shard_map/ppermute | solution.py:255
  85.7 1.3 collective-permute-start.16
  87.0 1.9 %collective-permute-start.15 = (bf16[19,64,128]{2,1,0:T(8,128)(2,1)S(1)}, bf16[19,64,128]{2,1,0:T(8,128)(2,1)S(1)}, u32[]{:S(2)}, u32[]{:S(2)}) collective-permute-start(bf16[19,64,128]{2,1,0:T(8,128)(2,1)S(1)} %copy-done.7), channel_id=1, source_target_pairs={{0,7},{1,6},{2,1},{3,0},{4,3},{5,2},{6,5},{7,4},{8,15},{9,14},{10,... | collective-permute-start | bytes 933896 | tf_op jit(solution)/shard_map/ppermute | solution.py:255
  88.9 6.6 %collective-permute-done.18.piece_ref = bf16[19,64,128]{2,1,0:T(8,128)(2,1)S(1)} collective-permute-done((bf16[19,64,128]{2,1,0:T(8,128)(2,1)S(1)}, bf16[19,64,128]{2,1,0:T(8,128)(2,1)S(1)}, u32[]{:S(2)}, u32[]{:S(2)}) %collective-permute-start.18) | collective-permute-done | bytes 311328 | tf_op jit(solution)/shard_map/ppermute | solution.py:255
  95.8 17.9 %collective-permute-done.17.piece_ref = bf16[19,64,128]{2,1,0:T(8,128)(2,1)S(1)} collective-permute-done((bf16[19,64,128]{2,1,0:T(8,128)(2,1)S(1)}, bf16[19,64,128]{2,1,0:T(8,128)(2,1)S(1)}, u32[]{:S(2)}, u32[]{:S(2)}) %collective-permute-start.17) | collective-permute-done | bytes 311328 | tf_op jit(solution)/shard_map/ppermute | solution.py:255
  113.7 5.7 %collective-permute-done.15.piece_ref = bf16[19,64,128]{2,1,0:T(8,128)(2,1)S(1)} collective-permute-done((bf16[19,64,128]{2,1,0:T(8,128)(2,1)S(1)}, bf16[19,64,128]{2,1,0:T(8,128)(2,1)S(1)}, u32[]{:S(2)}, u32[]{:S(2)}) %collective-permute-start.15) | collective-permute-done | bytes 311328 | tf_op jit(solution)/shard_map/ppermute | solution.py:255
  119.4 2.8 %collective-permute-start.5 = (bf16[15,64,128]{2,1,0:T(8,128)(2,1)}, bf16[15,64,128]{2,1,0:T(8,128)(2,1)}, u32[]{:S(2)}, u32[]{:S(2)}) collective-permute-start(bf16[15,64,128]{2,1,0:T(8,128)(2,1)} %get-tuple-element.33), channel_id=1, source_target_pairs={{0,15},{1,14},{2,9},{3,8},{4,11},{5,10},{6,13},{7,12},{8,7},{9,6},... | collective-permute-start | bytes 737288 | tf_op jit(solution)/shard_map/ppermute | solution.py:255
  122.2 1.4 constant_dynamic-slice_fusion
  125.3 0.8 place_plane.7
  126.1 0.8 place_plane.8
  126.9 0.8 place_plane.9
  127.7 0.8 place_plane.10
  128.4 0.8 place_plane.11
  129.2 0.8 place_plane.12
  130.0 0.8 place_plane.13
  130.8 0.7 place_across.10._
  132.2 0.7 place_across.12._
  133.0 11.6 %collective-permute-done.7.piece_ref = bf16[15,64,128]{2,1,0:T(8,128)(2,1)S(1)} collective-permute-done((bf16[15,64,128]{2,1,0:T(8,128)(2,1)}, bf16[15,64,128]{2,1,0:T(8,128)(2,1)S(1)}, u32[]{:S(2)}, u32[]{:S(2)}) %collective-permute-start.7) | collective-permute-done | bytes 245792 | tf_op jit(solution)/shard_map/ppermute | solution.py:255
  145.3 4.7 %collective-permute-done.6.piece_ref = bf16[15,64,128]{2,1,0:T(8,128)(2,1)} collective-permute-done((bf16[15,64,128]{2,1,0:T(8,128)(2,1)}, bf16[15,64,128]{2,1,0:T(8,128)(2,1)}, u32[]{:S(2)}, u32[]{:S(2)}) %collective-permute-start.6) | collective-permute-done | bytes 245792 | tf_op jit(solution)/shard_map/ppermute | solution.py:255
  150.0 1.6 %place_across.14._ = bf16[16,64,2048]{2,1,0:T(8,128)(2,1)} custom-call(s32[1]{0:T(128)} %bitcast.f_ref, bf16[15,64,128]{2,1,0:T(8,128)(2,1)} %collective-permute-done.6.piece_ref, bf16[16,64,2048]{2,1,0:T(8,128)(2,1)} %place_across.13._), custom_call_target="tpu_custom_call", output_to_operand_aliasing={{}: (2, {})} | custom-call | flops 2097152 | bytes 524288 | tf_op jit(solution)/shard_map/place_across/pallas_call | solution.py:204
  151.6 3.6 %collective-permute-done.5.piece_ref = bf16[15,64,128]{2,1,0:T(8,128)(2,1)} collective-permute-done((bf16[15,64,128]{2,1,0:T(8,128)(2,1)}, bf16[15,64,128]{2,1,0:T(8,128)(2,1)}, u32[]{:S(2)}, u32[]{:S(2)}) %collective-permute-start.5) | collective-permute-done | bytes 245792 | tf_op jit(solution)/shard_map/ppermute | solution.py:255
  155.2 1.6 %place_across.15 = bf16[16,64,2048]{2,1,0:T(8,128)(2,1)} custom-call(s32[1]{0:T(128)} %bitcast.f_ref, bf16[15,64,128]{2,1,0:T(8,128)(2,1)} %collective-permute-done.5.piece_ref, bf16[16,64,2048]{2,1,0:T(8,128)(2,1)} %place_across.14._), custom_call_target="tpu_custom_call", output_to_operand_aliasing={{}: (2, {})} | custom-call | flops 2097152 | bytes 524288 | tf_op jit(solution)/shard_map/place_across/pallas_call | solution.py:204
  (51 shorter events, 6.6 us)
Async XLA Ops:
  1.6 40.5 %collective-permute-start.11 = (f32[1,512,128]{2,1,0:T(8,128)S(1)}, f32[1,512,128]{2,1,0:T(8,128)S(1)}, u32[]{:S(2)}, u32[]{:S(2)}) collective-permute-start(f32[1,512,128]{2,1,0:T(8,128)S(1)} %constant_dynamic-slice_fusion.1), channel_id=1, source_target_pairs={{0,8},{1,9},{2,10},{3,11},{4,12},{5,13},{6,14},{7,15},{8,0},{9,1},... | collective-permute-start | bytes 786440 | tf_op jit(solution)/shard_map/ppermute | solution.py:255
  15.1 12.6 %collective-permute-start = (f32[16,1152]{1,0:T(8,128)}, f32[16,1152]{1,0:T(8,128)S(1)}, u32[]{:S(2)}, u32[]{:S(2)}) collective-permute-start(f32[16,1152]{1,0:T(8,128)} %local_maxima.1), channel_id=1, source_target_pairs={{0,8},{1,9},{2,10},{3,11},{4,12},{5,13},{6,14},{7,15},{8,0},{9,1},... | collective-permute-start | bytes 221192 | tf_op jit(solution)/shard_map/ppermute | solution.py:255
  28.6 2.4 %collective-permute-start.1 = (f32[16,1024]{1,0:T(8,128)S(1)}, f32[16,1024]{1,0:T(8,128)S(1)}, u32[]{:S(2)}, u32[]{:S(2)}) collective-permute-start(f32[16,1024]{1,0:T(8,128)S(1)} %slice_maximum_fusion), channel_id=1, source_target_pairs={{0,1},{1,0},{2,3},{3,2},{4,5},{5,4},{6,7},{7,6},{8,9},{9,8},{10,11... | collective-permute-start | bytes 196616 | tf_op jit(solution)/shard_map/ppermute | solution.py:255
  31.0 5.6 %collective-permute-start.2 = (f32[16,1024]{1,0:T(8,128)S(1)}, f32[16,1024]{1,0:T(8,128)S(1)}, u32[]{:S(2)}, u32[]{:S(2)}) collective-permute-start(f32[16,1024]{1,0:T(8,128)S(1)} %max.16), channel_id=1, source_target_pairs={{0,2},{1,3},{2,4},{3,5},{4,6},{5,7},{6,0},{7,1},{8,10},{9,11},{10,... | collective-permute-start | bytes 196616 | tf_op jit(solution)/shard_map/ppermute | solution.py:255
  32.3 6.9 %collective-permute-start.3 = (f32[16,1024]{1,0:T(8,128)S(1)}, f32[16,1024]{1,0:T(8,128)S(1)}, u32[]{:S(2)}, u32[]{:S(2)}) collective-permute-start(f32[16,1024]{1,0:T(8,128)S(1)} %max.16), channel_id=1, source_target_pairs={{0,6},{1,7},{2,0},{3,1},{4,2},{5,3},{6,4},{7,5},{8,14},{9,15},{10,... | collective-permute-start | bytes 196616 | tf_op jit(solution)/shard_map/ppermute | solution.py:255
  33.8 6.5 %collective-permute-start.4 = (f32[16,1024]{1,0:T(8,128)S(1)}, f32[16,1024]{1,0:T(8,128)S(1)}, u32[]{:S(2)}, u32[]{:S(2)}) collective-permute-start(f32[16,1024]{1,0:T(8,128)S(1)} %max.16), channel_id=1, source_target_pairs={{0,4},{1,5},{2,6},{3,7},{4,0},{5,1},{6,2},{7,3},{8,12},{9,13},{10,... | collective-permute-start | bytes 196616 | tf_op jit(solution)/shard_map/ppermute | solution.py:255
  35.3 6.8 %copy-start.3 = (bf16[2,16,128]{2,1,0:T(8,128)(2,1)}, bf16[2,16,128]{2,1,0:T(8,128)(2,1)S(1)}, u32[]{:S(2)}) copy-start(bf16[2,16,128]{2,1,0:T(8,128)(2,1)S(1)} %pad_maximum_fusion.near_ref) | copy-start | bytes 24580
  35.3 5.6 %collective-permute-start.12 = (bf16[2,16,128]{2,1,0:T(8,128)(2,1)S(1)}, bf16[2,16,128]{2,1,0:T(8,128)(2,1)S(1)}, u32[]{:S(2)}, u32[]{:S(2)}) collective-permute-start(bf16[2,16,128]{2,1,0:T(8,128)(2,1)S(1)} %pad_maximum_fusion.near_ref), channel_id=1, source_target_pairs={{0,16},{16,32},{32,48},{48,0},{1,17},{17,33},{33,49},{49,1},{2,18}... | collective-permute-start | bytes 24584 | tf_op jit(solution)/shard_map/ppermute | solution.py:280
  36.6 4.3 %collective-permute-start.13 = (bf16[2,16,128]{2,1,0:T(8,128)(2,1)S(1)}, bf16[2,16,128]{2,1,0:T(8,128)(2,1)S(1)}, u32[]{:S(2)}, u32[]{:S(2)}) collective-permute-start(bf16[2,16,128]{2,1,0:T(8,128)(2,1)S(1)} %pad_maximum_fusion.near_ref), channel_id=1, source_target_pairs={{0,32},{16,48},{32,0},{48,16},{1,33},{17,49},{33,1},{49,17},{2,34}... | collective-permute-start | bytes 24584 | tf_op jit(solution)/shard_map/ppermute | solution.py:280
  39.2 2.9 %collective-permute-start.14 = (bf16[2,16,128]{2,1,0:T(8,128)(2,1)S(1)}, bf16[2,16,128]{2,1,0:T(8,128)(2,1)S(1)}, u32[]{:S(2)}, u32[]{:S(2)}) collective-permute-start(bf16[2,16,128]{2,1,0:T(8,128)(2,1)S(1)} %pad_maximum_fusion.near_ref), channel_id=1, source_target_pairs={{0,48},{16,0},{32,16},{48,32},{1,49},{17,1},{33,17},{49,33},{2,50}... | collective-permute-start | bytes 24584 | tf_op jit(solution)/shard_map/ppermute | solution.py:280
  40.9 1.2 copy-start.4
  41.0 1.2 copy-start.5
  42.1 0.6 copy-start.6
  42.1 0.7 copy-start.2
  48.3 37.4 %collective-permute-start.21 = (bf16[19,64,128]{2,1,0:T(8,128)(2,1)}, bf16[19,64,128]{2,1,0:T(8,128)(2,1)S(1)}, u32[]{:S(2)}, u32[]{:S(2)}) collective-permute-start(bf16[19,64,128]{2,1,0:T(8,128)(2,1)} %get-tuple-element.45), channel_id=1, source_target_pairs={{0,1},{1,0},{2,3},{3,2},{4,5},{5,4},{6,7},{7,6},{8,9},{9,8},{10,11... | collective-permute-start | bytes 933896 | tf_op jit(solution)/shard_map/ppermute | solution.py:255
  50.9 36.0 %collective-permute-start.20 = (bf16[19,64,128]{2,1,0:T(8,128)(2,1)}, bf16[19,64,128]{2,1,0:T(8,128)(2,1)S(1)}, u32[]{:S(2)}, u32[]{:S(2)}) collective-permute-start(bf16[19,64,128]{2,1,0:T(8,128)(2,1)} %get-tuple-element.44), channel_id=1, source_target_pairs={{0,2},{1,3},{2,4},{3,5},{4,6},{5,7},{6,0},{7,1},{8,10},{9,11},{10,... | collective-permute-start | bytes 933896 | tf_op jit(solution)/shard_map/ppermute | solution.py:255
  54.1 17.7 %copy-start.11 = (bf16[19,64,128]{2,1,0:T(8,128)(2,1)S(1)}, bf16[19,64,128]{2,1,0:T(8,128)(2,1)}, u32[]{:S(2)}) copy-start(bf16[19,64,128]{2,1,0:T(8,128)(2,1)} %get-tuple-element.43) | copy-start | bytes 933892
  54.1 24.0 %copy-start.10 = (bf16[19,64,128]{2,1,0:T(8,128)(2,1)S(1)}, bf16[19,64,128]{2,1,0:T(8,128)(2,1)}, u32[]{:S(2)}) copy-start(bf16[19,64,128]{2,1,0:T(8,128)(2,1)} %get-tuple-element.42) | copy-start | bytes 933892
  54.1 31.0 %copy-start.9 = (bf16[19,64,128]{2,1,0:T(8,128)(2,1)S(1)}, bf16[19,64,128]{2,1,0:T(8,128)(2,1)}, u32[]{:S(2)}) copy-start(bf16[19,64,128]{2,1,0:T(8,128)(2,1)} %get-tuple-element.41) | copy-start | bytes 933892
  54.1 31.6 %copy-start.8 = (bf16[19,64,128]{2,1,0:T(8,128)(2,1)S(1)}, bf16[19,64,128]{2,1,0:T(8,128)(2,1)}, u32[]{:S(2)}) copy-start(bf16[19,64,128]{2,1,0:T(8,128)(2,1)} %get-tuple-element.40) | copy-start | bytes 933892
  54.1 32.9 %copy-start.7 = (bf16[19,64,128]{2,1,0:T(8,128)(2,1)S(1)}, bf16[19,64,128]{2,1,0:T(8,128)(2,1)}, u32[]{:S(2)}) copy-start(bf16[19,64,128]{2,1,0:T(8,128)(2,1)} %get-tuple-element.39) | copy-start | bytes 933892
  54.1 17.6 %collective-permute-start.23 = (bf16[15,64,128]{2,1,0:T(8,128)(2,1)}, bf16[15,64,128]{2,1,0:T(8,128)(2,1)S(1)}, u32[]{:S(2)}, u32[]{:S(2)}) collective-permute-start(bf16[15,64,128]{2,1,0:T(8,128)(2,1)} %across_pieces.3), channel_id=1, source_target_pairs={{0,8},{1,9},{2,10},{3,11},{4,12},{5,13},{6,14},{7,15},{8,0},{9,1},... | collective-permute-start | bytes 737288 | tf_op jit(solution)/shard_map/ppermute | solution.py:255
  59.7 17.7 %collective-permute-start.22 = (bf16[15,64,128]{2,1,0:T(8,128)(2,1)}, bf16[15,64,128]{2,1,0:T(8,128)(2,1)S(1)}, u32[]{:S(2)}, u32[]{:S(2)}) collective-permute-start(bf16[15,64,128]{2,1,0:T(8,128)(2,1)} %get-tuple-element.46), channel_id=1, source_target_pairs={{0,9},{1,8},{2,11},{3,10},{4,13},{5,12},{6,15},{7,14},{8,1},{9,0},... | collective-permute-start | bytes 737288 | tf_op jit(solution)/shard_map/ppermute | solution.py:255
  64.7 20.4 %collective-permute-start.10 = (bf16[15,64,128]{2,1,0:T(8,128)(2,1)}, bf16[15,64,128]{2,1,0:T(8,128)(2,1)S(1)}, u32[]{:S(2)}, u32[]{:S(2)}) collective-permute-start(bf16[15,64,128]{2,1,0:T(8,128)(2,1)} %get-tuple-element.38), channel_id=1, source_target_pairs={{0,10},{1,11},{2,12},{3,13},{4,14},{5,15},{6,8},{7,9},{8,2},{9,3},... | collective-permute-start | bytes 737288 | tf_op jit(solution)/shard_map/ppermute | solution.py:255
  71.8 17.1 %collective-permute-start.19 = (bf16[19,64,128]{2,1,0:T(8,128)(2,1)S(1)}, bf16[19,64,128]{2,1,0:T(8,128)(2,1)S(1)}, u32[]{:S(2)}, u32[]{:S(2)}) collective-permute-start(bf16[19,64,128]{2,1,0:T(8,128)(2,1)S(1)} %copy-done.11), channel_id=1, source_target_pairs={{0,3},{1,2},{2,5},{3,4},{4,7},{5,6},{6,1},{7,0},{8,11},{9,10},{10,... | collective-permute-start | bytes 933896 | tf_op jit(solution)/shard_map/ppermute | solution.py:255
  77.4 0.7 copy-start
  78.1 17.4 %collective-permute-start.18 = (bf16[19,64,128]{2,1,0:T(8,128)(2,1)S(1)}, bf16[19,64,128]{2,1,0:T(8,128)(2,1)S(1)}, u32[]{:S(2)}, u32[]{:S(2)}) collective-permute-start(bf16[19,64,128]{2,1,0:T(8,128)(2,1)S(1)} %copy-done.10), channel_id=1, source_target_pairs={{0,4},{1,5},{2,6},{3,7},{4,0},{5,1},{6,2},{7,3},{8,12},{9,13},{10,... | collective-permute-start | bytes 933896 | tf_op jit(solution)/shard_map/ppermute | solution.py:255
  85.1 28.6 %collective-permute-start.17 = (bf16[19,64,128]{2,1,0:T(8,128)(2,1)S(1)}, bf16[19,64,128]{2,1,0:T(8,128)(2,1)S(1)}, u32[]{:S(2)}, u32[]{:S(2)}) collective-permute-start(bf16[19,64,128]{2,1,0:T(8,128)(2,1)S(1)} %copy-done.9), channel_id=1, source_target_pairs={{0,5},{1,4},{2,7},{3,6},{4,1},{5,0},{6,3},{7,2},{8,13},{9,12},{10,... | collective-permute-start | bytes 933896 | tf_op jit(solution)/shard_map/ppermute | solution.py:255
  85.7 28.0 %collective-permute-start.16 = (bf16[19,64,128]{2,1,0:T(8,128)(2,1)S(1)}, bf16[19,64,128]{2,1,0:T(8,128)(2,1)S(1)}, u32[]{:S(2)}, u32[]{:S(2)}) collective-permute-start(bf16[19,64,128]{2,1,0:T(8,128)(2,1)S(1)} %copy-done.8), channel_id=1, source_target_pairs={{0,6},{1,7},{2,0},{3,1},{4,2},{5,3},{6,4},{7,5},{8,14},{9,15},{10,... | collective-permute-start | bytes 933896 | tf_op jit(solution)/shard_map/ppermute | solution.py:255
  87.0 32.4 %collective-permute-start.15 = (bf16[19,64,128]{2,1,0:T(8,128)(2,1)S(1)}, bf16[19,64,128]{2,1,0:T(8,128)(2,1)S(1)}, u32[]{:S(2)}, u32[]{:S(2)}) collective-permute-start(bf16[19,64,128]{2,1,0:T(8,128)(2,1)S(1)} %copy-done.7), channel_id=1, source_target_pairs={{0,7},{1,6},{2,1},{3,0},{4,3},{5,2},{6,5},{7,4},{8,15},{9,14},{10,... | collective-permute-start | bytes 933896 | tf_op jit(solution)/shard_map/ppermute | solution.py:255
  88.9 42.6 %collective-permute-start.9 = (bf16[15,64,128]{2,1,0:T(8,128)(2,1)}, bf16[15,64,128]{2,1,0:T(8,128)(2,1)S(1)}, u32[]{:S(2)}, u32[]{:S(2)}) collective-permute-start(bf16[15,64,128]{2,1,0:T(8,128)(2,1)} %get-tuple-element.37), channel_id=1, source_target_pairs={{0,11},{1,10},{2,13},{3,12},{4,15},{5,14},{6,9},{7,8},{8,3},{9,2},... | collective-permute-start | bytes 737288 | tf_op jit(solution)/shard_map/ppermute | solution.py:255
  95.5 36.8 %collective-permute-start.8 = (bf16[15,64,128]{2,1,0:T(8,128)(2,1)}, bf16[15,64,128]{2,1,0:T(8,128)(2,1)S(1)}, u32[]{:S(2)}, u32[]{:S(2)}) collective-permute-start(bf16[15,64,128]{2,1,0:T(8,128)(2,1)} %get-tuple-element.36), channel_id=1, source_target_pairs={{0,12},{1,13},{2,14},{3,15},{4,8},{5,9},{6,10},{7,11},{8,4},{9,5},... | collective-permute-start | bytes 737288 | tf_op jit(solution)/shard_map/ppermute | solution.py:255
  113.7 30.9 %collective-permute-start.7 = (bf16[15,64,128]{2,1,0:T(8,128)(2,1)}, bf16[15,64,128]{2,1,0:T(8,128)(2,1)S(1)}, u32[]{:S(2)}, u32[]{:S(2)}) collective-permute-start(bf16[15,64,128]{2,1,0:T(8,128)(2,1)} %get-tuple-element.35), channel_id=1, source_target_pairs={{0,13},{1,12},{2,15},{3,14},{4,9},{5,8},{6,11},{7,10},{8,5},{9,4},... | collective-permute-start | bytes 737288 | tf_op jit(solution)/shard_map/ppermute | solution.py:255
  113.7 36.3 %collective-permute-start.6 = (bf16[15,64,128]{2,1,0:T(8,128)(2,1)}, bf16[15,64,128]{2,1,0:T(8,128)(2,1)}, u32[]{:S(2)}, u32[]{:S(2)}) collective-permute-start(bf16[15,64,128]{2,1,0:T(8,128)(2,1)} %get-tuple-element.34), channel_id=1, source_target_pairs={{0,14},{1,15},{2,8},{3,9},{4,10},{5,11},{6,12},{7,13},{8,6},{9,7},... | collective-permute-start | bytes 737288 | tf_op jit(solution)/shard_map/ppermute | solution.py:255
  119.4 35.9 %collective-permute-start.5 = (bf16[15,64,128]{2,1,0:T(8,128)(2,1)}, bf16[15,64,128]{2,1,0:T(8,128)(2,1)}, u32[]{:S(2)}, u32[]{:S(2)}) collective-permute-start(bf16[15,64,128]{2,1,0:T(8,128)(2,1)} %get-tuple-element.33), channel_id=1, source_target_pairs={{0,15},{1,14},{2,9},{3,8},{4,11},{5,10},{6,13},{7,12},{8,7},{9,6},... | collective-permute-start | bytes 737288 | tf_op jit(solution)/shard_map/ppermute | solution.py:255
  123.6 1.0 copy-start.1

commit v2 on v1

--- a/solution.py
+++ b/solution.py
@@ -8,6 +8,7 @@
 from jax.sharding import PartitionSpec as P
 
 
+RELAY = 7
 EARLY = 1
 BF16, F32 = jnp.bfloat16, jnp.float32
 ANY = pl.BlockSpec(memory_space=pl.ANY)
@@ -17,7 +18,7 @@
 
 
 def params(mebibytes):
-    return pltpu.CompilerParams(vmem_limit_bytes=mebibytes * 2**20)
+    return pltpu.CompilerParams(vmem_limit_bytes=int(mebibytes * 2**20))
 
 
 def cost(read, written):
@@ -43,13 +44,12 @@
     return pl.ds(pl.multiple_of(position * 128, 128), 128)
 
 
-def local_kernel(w_ref, router_ref, gain_ref, out_ref, taken, sems):
+def local_kernel(w_ref, out_ref, taken, sems):
     blocks, experts = taken.shape[:2]
     reads = []
     for b in range(blocks):
         reads.append(pltpu.make_async_copy(w_ref.at[:, pl.ds(128 * b, 128), :], taken.at[b], sems.at[b]))
         reads[-1].start()
-    out_ref[:, 128 * blocks :] = router_ref[...] * gain_ref[...]
     lane = lax.broadcasted_iota(jnp.int32, (128, 128), 1)
     for b in range(blocks):
         reads[b].wait()
@@ -60,26 +60,99 @@
         out_ref[:, pl.ds(128 * b, 128)] = total.T[:experts]
 
 
-def local_maxima(w, router, gain):
+def local_maxima(w):
     experts, rows, _ = w.shape
     blocks = rows // 128
     return pl.pallas_call(
         local_kernel,
-        out_shape=jax.ShapeDtypeStruct((experts, rows + 128), F32),
-        in_specs=[ANY, VMEM, VMEM],
+        out_shape=jax.ShapeDtypeStruct((experts, rows), F32),
+        in_specs=[ANY],
         out_specs=VMEM,
         scratch_shapes=[pltpu.VMEM((blocks, experts, 128, 128), F32), pltpu.SemaphoreType.DMA((blocks,))],
-        compiler_params=params(56),
+        compiler_params=params(50),
         cost_estimate=cost(8 * 2**20, 2**16),
         name="local_maxima",
-    )(w, router, gain)
+    )(w)
 
 
 def inverse_columns(scale_ref, inverse, slot, block):
     inverse[pl.ds(128 * slot, 128), :] = jnp.concatenate([1.0 / scale_ref[:, lanes(block)]] * 8, axis=0).T
 
 
-def across_kernel(hops, f_ref, w_ref, scale_ref, *refs):
+def chunk_kernel(f_ref, w_ref, scale_ref, out_ref, taken, inverse, made, in_sems, out_sems):
+    count = taken.shape[1]
+    plane = 1 - f_ref[0] // 8
+    reads = []
+    for b in range(4):
+        rows = pl.ds(pl.multiple_of(plane * 512 + 128 * b, 128), 128)
+        reads.append(pltpu.make_async_copy(w_ref.at[pl.ds(0, count), rows, :], taken.at[b], in_sems.at[b]))
+        reads[-1].start()
+    writes = []
+    for b in range(4):
+        inverse_columns(scale_ref, inverse, b, 4 * plane + b)
+        columns = inverse[pl.ds(128 * b, 128), :]
+        reads[b].wait()
+        for e in range(count):
+            made[b, e] = (taken[b, e] * columns[:, e : e + 1]).astype(BF16)
+        writes.append(pltpu.make_async_copy(made.at[b], out_ref.at[:, pl.ds(128 * b, 128), :], out_sems.at[b]))
+        writes[-1].start()
+    for write in writes:
+        write.wait()
+
+
+def chunk(f, w, scale, count):
+    return pl.pallas_call(
+        chunk_kernel,
+        out_shape=jax.ShapeDtypeStruct((count, 512, 128), BF16),
+        in_specs=[SMEM, ANY, VMEM],
+        out_specs=ANY,
+        scratch_shapes=[
+            pltpu.VMEM((4, count, 128, 128), F32),
+            pltpu.VMEM((512, 128), F32),
+            pltpu.VMEM((4, count, 128, 128), BF16),
+            pltpu.SemaphoreType.DMA((4,)),
+            pltpu.SemaphoreType.DMA((4,)),
+        ],
+        compiler_params=params(50),
+        cost_estimate=cost(4 * 2**20, 2 * 2**20),
+        name="chunk",
+    )(f, w, scale)
+
+
+def split_kernel(f_ref, chunk_ref, _, *refs):
+    outs, final_ref, sems = refs[:7], refs[7], refs[8]
+    f = f_ref[0]
+    copies = []
+    for k, hop in enumerate(HOPS):
+        rows = pl.ds(pl.multiple_of(partner(f, 0, *hop) % 8 * 64, 64), 64)
+        piece = chunk_ref.at[:, rows, :]
+        if k == 0:
+            target = final_ref.at[pl.ds(0, chunk_ref.shape[0]), :, lanes(partner(f, 1, 0, 0))]
+        else:
+            target = outs[k - 1]
+        copies.append(pltpu.make_async_copy(piece, target, sems.at[k]))
+        copies[-1].start()
+    for copy in copies:
+        copy.wait()
+
+
+def split(f, chunk, final):
+    count = chunk.shape[0]
+    return pl.pallas_call(
+        split_kernel,
+        out_shape=[jax.ShapeDtypeStruct((count, 64, 128), BF16)] * 7
+        + [jax.ShapeDtypeStruct(final.shape, BF16)],
+        in_specs=[SMEM, VMEM, ANY],
+        out_specs=[ANY] * 8,
+        scratch_shapes=[pltpu.SemaphoreType.DMA((8,))],
+        input_output_aliases={2: 7},
+        compiler_params=params(50),
+        cost_estimate=cost(2**20, 2**20),
+        name="split",
+    )(f, chunk, final)
+
+
+def across_kernel(hops, first, f_ref, w_ref, scale_ref, *refs):
     outs, (taken, inverse, made, in_sems, out_sems) = refs[: len(hops)], refs[len(hops) :]
     count = taken.shape[1]
     f = f_ref[0]
@@ -87,7 +160,7 @@
     reads = []
     for k, target in enumerate(targets):
         rows = pl.ds(pl.multiple_of(target * 64, 64), 64)
-        reads.append(pltpu.make_async_copy(w_ref.at[pl.ds(0, count), rows, :], taken.at[k], in_sems.at[k]))
+        reads.append(pltpu.make_async_copy(w_ref.at[pl.ds(first, count), rows, :], taken.at[k], in_sems.at[k]))
         reads[-1].start()
     for dx in sorted({dx for dx, _ in hops}):
         inverse_columns(scale_ref, inverse, dx, partner(f, 1, dx, 0) // 2)
@@ -96,17 +169,17 @@
         columns = inverse[pl.ds(pl.multiple_of(hops[k][0] * 128 + target % 2 * 64, 64), 64), :]
         reads[k].wait()
         for e in range(count):
-            made[k, e] = (taken[k, e] * columns[:, e : e + 1]).astype(BF16)
+            made[k, e] = (taken[k, e] * columns[:, first + e : first + e + 1]).astype(BF16)
         writes.append(pltpu.make_async_copy(made.at[k], outs[k], out_sems.at[k]))
         writes[-1].start()
     for write in writes:
         write.wait()
 
 
-def across_pieces(hops, f, w, scale, count):
+def across_pieces(hops, f, w, scale, first, count):
     n = len(hops)
     return pl.pallas_call(
-        functools.partial(across_kernel, hops),
+        functools.partial(across_kernel, hops, first),
         out_shape=[jax.ShapeDtypeStruct((count, 64, 128), BF16)] * n,
         in_specs=[SMEM, ANY, VMEM],
         out_specs=[ANY] * n,
@@ -117,7 +190,7 @@
             pltpu.SemaphoreType.DMA((n,)),
             pltpu.SemaphoreType.DMA((n,)),
         ],
-        compiler_params=params(56),
+        compiler_params=params(50),
         cost_estimate=cost(n * 2**19, n * 2**18),
         name="across_pieces",
     )(f, w, scale)
@@ -125,7 +198,7 @@
 
 def plane_kernel(f_ref, y_ref, w_ref, scale_ref, relay_ref, near_ref, r1_ref, r2_ref, r3_ref, *refs):
     outs, (final_ref, router_ref), (taken, inverse, made, in_sems, out_sems) = refs[:7], refs[7:9], refs[9:]
-    experts, early = w_ref.shape[0], relay_ref.shape[0]
+    experts, early = w_ref.shape[0], EARLY
     f, y = f_ref[0], y_ref[0]
     reads = []
     for k, (dx, dc) in enumerate(HOPS):
@@ -136,14 +209,13 @@
         inverse_columns(scale_ref, inverse, dx, partner(f, 0, dx, 0) // 2)
     for k, (dx, dc) in enumerate(HOPS):
         target = partner(f, 0, dx, dc)
-        local = pl.ds(pl.multiple_of(target % 8 * 64, 64), 64)
         columns = inverse[pl.ds(pl.multiple_of(dx * 128 + target % 2 * 64, 64), 64), :]
         reads[k].wait()
         for e in range(experts):
             made[k, e] = (taken[k, e] * columns[:, e : e + 1]).astype(BF16)
         for q in range(early):
             e = experts - early + q
-            made[k, experts + q] = (relay_ref[q, local, :] * columns[:, e : e + 1]).astype(BF16)
+            made[k, experts + q] = (relay_ref[pl.ds(pl.multiple_of(512 * q + target % 8 * 64, 64), 64), :] * columns[:, e : e + 1]).astype(BF16)
         for plane in range(2):
             for dy, piece in enumerate((near_ref, r1_ref, r2_ref, r3_ref)):
                 at = pl.multiple_of((y - dy + 4) % 4 * 16, 16)
@@ -173,7 +245,7 @@
 
 def plane_pieces(f, y, w, scale, relay, near, *received):
     experts, _, _ = w.shape
-    blocks = experts + relay.shape[0] + 2
+    blocks = experts + EARLY + 2
     return pl.pallas_call(
         plane_kernel,
         out_shape=[jax.ShapeDtypeStruct((blocks, 64, 128), BF16)] * 7
@@ -187,22 +259,24 @@
             pltpu.SemaphoreType.DMA((8,)),
             pltpu.SemaphoreType.DMA((11,)),
         ],
-        compiler_params=params(56),
+        compiler_params=params(50),
         cost_estimate=cost(5 * 2**20, 3 * 2**20),
         name="plane_pieces",
     )(f, y, w, scale, relay, near, *received)
 
 
-def place_across_kernel(hop, f_ref, piece_ref, _, final_ref, sem):
-    source = partner(f_ref[0], 1, 4 - hop[0], hop[1])
-    copy = pltpu.make_async_copy(piece_ref, final_ref.at[pl.ds(0, piece_ref.shape[0]), :, lanes(source)], sem)
+def place_far_kernel(hop, first, f_ref, piece_ref, _, final_ref, sem):
+    dx, dc = hop
+    source = partner(f_ref[0], 1, 4 - dx, dc)
+    experts = pl.ds(first, piece_ref.shape[0])
+    copy = pltpu.make_async_copy(piece_ref, final_ref.at[experts, :, lanes(source)], sem)
     copy.start()
     copy.wait()
 
 
-def place_across(hop, f, piece, final):
-    return pl.pallas_call(
-        functools.partial(place_across_kernel, hop),
+def place_far(hop, first, f, piece, final):
+    return pl.pallas_call(
+        functools.partial(place_far_kernel, hop, first),
         out_shape=jax.ShapeDtypeStruct(final.shape, final.dtype),
         in_specs=[SMEM, VMEM, ANY],
         out_specs=ANY,
@@ -210,7 +284,7 @@
         input_output_aliases={2: 0},
         compiler_params=params(2),
         cost_estimate=cost(2**18, 2**18),
-        name="place_across",
+        name="place_far",
     )(f, piece, final)
 
 
@@ -256,36 +330,42 @@
 
 
 def served(master_down, router_weight, router_gain):
-    experts, rows, _ = master_down.shape
+    experts, _, _ = master_down.shape
+    direct = experts - RELAY - EARLY
     position = lax.axis_index("fsdp")
     f = position.reshape(1)
     y = lax.axis_index("ep").reshape(1)
 
-    local = local_maxima(master_down, router_weight.T, router_gain.reshape(1, -1))
-    peer = send(local, 1, 0, 0)
+    scale = local_maxima(master_down)
+    peer = send(scale, 1, 0, 0)
+    product = router_weight.T * router_gain.reshape(1, -1)
     early = lax.dynamic_slice(
         master_down, (experts - EARLY, (1 - position // 8) * 512, 0), (EARLY, 512, 128)
     )
+    early = jnp.concatenate([early.reshape(EARLY * 512, 128), product])
     relay = send(early, 1, 0, 0)
-    scale = jnp.maximum(local[:, :rows], peer[:, :rows])
-    near = jnp.stack([local[:, rows:], peer[:, rows:]]).astype(BF16)
+    scale = jnp.maximum(scale, peer)
     scale = jnp.maximum(scale, send(scale, 0, 0, 1))
     scale = functools.reduce(jnp.maximum, [scale] + [send(scale, 0, dx, 0) for dx in (1, 3, 2)])
 
-    pieces = across_pieces(HOPS[:1], f, master_down, scale, experts - EARLY)
-    pieces += across_pieces(HOPS[1:], f, master_down, scale, experts - EARLY)
-    across = [send(piece, 1, *HOPS[k]) for k, piece in enumerate(pieces)]
+    forward = send(chunk(f, master_down, scale, RELAY), 1, 0, 0)
+    near = jnp.stack([product, relay[EARLY * 512 :]]).astype(BF16)
     received = []
     for d in (1, 2, 3):
         received.append(lax.ppermute(near, "ep", [(i, (i + d) % 4) for i in range(4)]))
     *pieces, final, router = plane_pieces(f, y, master_down, scale, relay, near, *received)
     plane = [send(piece, 0, *HOPS[k + 1]) for k, piece in enumerate(pieces)]
-    for k in range(2):
-        final = place_across(HOPS[k], f, across[k], final)
+    pieces = across_pieces(HOPS, f, master_down, scale, RELAY, direct)
+    across = [send(piece, 1, *HOPS[k]) for k, piece in enumerate(pieces)]
+    *pieces, final = split(f, forward, final)
+    relayed = [send(piece, 0, *HOPS[k + 1]) for k, piece in enumerate(pieces)]
+
     for k in range(7):
         final, router = place_plane(HOPS[k + 1], EARLY, f, plane[k], final, router)
-    for k in range(2, 8):
-        final = place_across(HOPS[k], f, across[k], final)
+    for k in range(7):
+        final = place_far(HOPS[k + 1], 0, f, relayed[k], final)
+    for k in range(8):
+        final = place_far(HOPS[k], RELAY, f, across[k], final)
     own = lax.dynamic_slice_in_dim(scale, position * 64, 64, axis=1)
     return final, own, router.T
 

time: 158 us -> 173 us (1.095)
  the two profiles are of different devices: /device:TPU:1 before, /device:TPU:55 now
where the time goes in v2:
time: 173 us; the launch traced here: 170 us
  starting transfers between devices  99.7 us (58%)
  waiting for transfers between devices  33.6 us (19%)
  Pallas kernels  30.3 us (18%)
  local copies, waits for them, and re-layouts  5.11 us (3%)
    ppermute x29, starting transfers between devices, send(): return lax.ppermute(piece, 'fsdp', route(dz, dx, dc))  97.4 us
    ppermute x29, waiting for transfers between devices, send(): return lax.ppermute(piece, 'fsdp', route(dz, dx, dc))  30.6 us
    pallas_call x15, Pallas kernels, place_far(): pl.pallas_call(functools.partial(place_far_kernel, hop, first), out_shape...  10.2 us
    pallas_call x7, Pallas kernels, place_plane(): pl.pallas_call(functools.partial(place_plane_kernel, hop, early), out_sha...  5.35 us
    pallas_call x1, Pallas kernels, local_maxima(): pl.pallas_call(local_kernel, out_shape=jax.ShapeDtypeStruct((experts, row...  4.38 us
    pallas_call x1, Pallas kernels, plane_pieces(): pl.pallas_call(plane_kernel, out_shape=[jax.ShapeDtypeStruct((blocks, 64,...  3.79 us
    unnamed x20, local copies, waits for them, and re-layouts  3.47 us
  transfers between devices with their start and end apart: 32, of which 6 were waited for; matrix products, arithmetic and copies ran while one was open for 1% of the time, Pallas kernels for 15%

profile of v2, /device:TPU:55, one launch (start us, length us, event | category | flops | bytes accessed | tf_op | source)
XLA Modules:
  0.0 169.9 jit_solution(12819705543524653078)
XLA Ops:
  0.7 4.4 %local_maxima.1 = f32[16,1024]{1,0:T(8,128)S(1)} custom-call(f32[16,1024,128]{2,1,0:T(8,128)} %w_ref.7), custom_call_target="tpu_custom_call" | custom-call | flops 33816576 | bytes 8454144 | tf_op jit(solution)/shard_map/local_maxima/pallas_call | solution.py:66
  5.0 6.1 %collective-permute-start = (f32[16,1024]{1,0:T(8,128)S(1)}, f32[16,1024]{1,0:T(8,128)S(1)}, u32[]{:S(2)}, u32[]{:S(2)}) collective-permute-start(f32[16,1024]{1,0:T(8,128)S(1)} %local_maxima.1), channel_id=1, source_target_pairs={{0,8},{1,9},{2,10},{3,11},{4,12},{5,13},{6,14},{7,15},{8,0},{9,1},... | collective-permute-start | bytes 196616 | tf_op jit(solution)/shard_map/ppermute | solution.py:329
  11.2 1.6 collective-permute-done
  12.8 2.6 %collective-permute-start.1 = (f32[16,1024]{1,0:T(8,128)S(1)}, f32[16,1024]{1,0:T(8,128)S(1)}, u32[]{:S(2)}, u32[]{:S(2)}) collective-permute-start(f32[16,1024]{1,0:T(8,128)S(1)} %max.15), channel_id=1, source_target_pairs={{0,1},{1,0},{2,3},{3,2},{4,5},{5,4},{6,7},{7,6},{8,9},{9,8},{10,11... | collective-permute-start | bytes 196616 | tf_op jit(solution)/shard_map/ppermute | solution.py:329
  15.4 1.0 dynamic-slice_bitcast_fusion
  16.7 1.3 collective-permute-start.3
  17.9 1.1 collective-permute-start.4
  19.1 6.2 %collective-permute-start.14 = (f32[528,128]{1,0:T(8,128)S(1)}, f32[528,128]{1,0:T(8,128)S(1)}, u32[]{:S(2)}, u32[]{:S(2)}) collective-permute-start(f32[528,128]{1,0:T(8,128)S(1)} %pad_maximum_fusion), channel_id=1, source_target_pairs={{0,8},{1,9},{2,10},{3,11},{4,12},{5,13},{6,14},{7,15},{8,0},{9,1},... | collective-permute-start | bytes 811016 | tf_op jit(solution)/shard_map/ppermute | solution.py:329
  25.3 2.4 %chunk.1 = bf16[7,512,128]{2,1,0:T(8,128)(2,1)S(1)} custom-call(s32[1]{0:T(128)} %bitcast.f_ref, f32[16,1024,128]{2,1,0:T(8,128)} %w_ref.7, f32[16,1024]{1,0:T(8,128)S(1)} %maximum_maximum_fusion.scale_ref), custom_call_target="tpu_custom_call" | custom-call | flops 25165824 | bytes 6291456 | tf_op jit(solution)/shard_map/chunk/pallas_call | solution.py:104
  27.7 3.6 %collective-permute-start.13 = (bf16[7,512,128]{2,1,0:T(8,128)(2,1)S(1)}, bf16[7,512,128]{2,1,0:T(8,128)(2,1)S(1)}, u32[]{:S(2)}, u32[]{:S(2)}) collective-permute-start(bf16[7,512,128]{2,1,0:T(8,128)(2,1)S(1)} %chunk.1), channel_id=1, source_target_pairs={{0,8},{1,9},{2,10},{3,11},{4,12},{5,13},{6,14},{7,15},{8,0},{9,1},... | collective-permute-start | bytes 2752520 | tf_op jit(solution)/shard_map/ppermute | solution.py:329
  31.3 3.4 %across_pieces.1 = (bf16[8,64,128]{2,1,0:T(8,128)(2,1)S(1)}, bf16[8,64,128]{2,1,0:T(8,128)(2,1)S(1)}, bf16[8,64,128]{2,1,0:T(8,128)(2,1)S(1)}, bf16[8,64,128]{2,...) custom-call(s32[1]{0:T(128)} %bitcast.f_ref, ...), custom_call_target="tpu_custom_call" | custom-call | flops 25165824 | bytes 6291456 | tf_op jit(solution)/shard_map/across_pieces/pallas_call | solution.py:181
  34.7 2.0 %collective-permute-start.12 = (bf16[8,64,128]{2,1,0:T(8,128)(2,1)S(1)}, bf16[8,64,128]{2,1,0:T(8,128)(2,1)S(1)}, u32[]{:S(2)}, u32[]{:S(2)}) collective-permute-start(bf16[8,64,128]{2,1,0:T(8,128)(2,1)S(1)} %get-tuple-element.49), channel_id=1, source_target_pairs={{0,8},{1,9},{2,10},{3,11},{4,12},{5,13},{6,14},{7,15},{8,0},{9,1},... | collective-permute-start | bytes 393224 | tf_op jit(solution)/shard_map/ppermute | solution.py:329
  36.7 15.5 %collective-permute-done.14.relay_ref = f32[528,128]{1,0:T(8,128)S(1)} collective-permute-done((f32[528,128]{1,0:T(8,128)S(1)}, f32[528,128]{1,0:T(8,128)S(1)}, u32[]{:S(2)}, u32[]{:S(2)}) %collective-permute-start.14) | collective-permute-done | bytes 270368 | tf_op jit(solution)/shard_map/ppermute | solution.py:329
  52.2 1.0 collective-permute-start.15
  53.5 0.9 collective-permute-start.17
  55.0 2.5 %collective-permute-done.16.r2_ref = bf16[2,16,128]{2,1,0:T(8,128)(2,1)S(1)} collective-permute-done((bf16[2,16,128]{2,1,0:T(8,128)(2,1)S(1)}, bf16[2,16,128]{2,1,0:T(8,128)(2,1)S(1)}, u32[]{:S(2)}, u32[]{:S(2)}) %collective-permute-start.16) | collective-permute-done | bytes 8224 | tf_op jit(solution)/shard_map/ppermute | solution.py:355
  57.5 3.8 %plane_pieces.1 = (bf16[19,64,128]{2,1,0:T(8,128)(2,1)S(1)}, bf16[19,64,128]{2,1,0:T(8,128)(2,1)S(1)}, bf16[19,64,128]{2,1,0:T(8,128)(2,1)S(1)}, bf16[19,64,128]...) custom-call(s32[1]{0:T(128)} %bitcast.f_ref, ...), custom_call_target="tpu_custom_call" | custom-call | flops 33554432 | bytes 8388608 | tf_op jit(solution)/shard_map/plane_pieces/pallas_call | solution.py:249
  61.3 11.2 %collective-permute-start.31 = (bf16[19,64,128]{2,1,0:T(8,128)(2,1)S(1)}, bf16[19,64,128]{2,1,0:T(8,128)(2,1)S(1)}, u32[]{:S(2)}, u32[]{:S(2)}) collective-permute-start(bf16[19,64,128]{2,1,0:T(8,128)(2,1)S(1)} %get-tuple-element.64), channel_id=1, source_target_pairs={{0,1},{1,0},{2,3},{3,2},{4,5},{5,4},{6,7},{7,6},{8,9},{9,8},{10,11... | collective-permute-start | bytes 933896 | tf_op jit(solution)/shard_map/ppermute | solution.py:329
  72.5 1.8 %collective-permute-start.30 = (bf16[19,64,128]{2,1,0:T(8,128)(2,1)S(1)}, bf16[19,64,128]{2,1,0:T(8,128)(2,1)S(1)}, u32[]{:S(2)}, u32[]{:S(2)}) collective-permute-start(bf16[19,64,128]{2,1,0:T(8,128)(2,1)S(1)} %get-tuple-element.63), channel_id=1, source_target_pairs={{0,2},{1,3},{2,4},{3,5},{4,6},{5,7},{6,0},{7,1},{8,10},{9,11},{10,... | collective-permute-start | bytes 933896 | tf_op jit(solution)/shard_map/ppermute | solution.py:329
  74.3 5.4 %collective-permute-start.11 = (bf16[8,64,128]{2,1,0:T(8,128)(2,1)S(1)}, bf16[8,64,128]{2,1,0:T(8,128)(2,1)S(1)}, u32[]{:S(2)}, u32[]{:S(2)}) collective-permute-start(bf16[8,64,128]{2,1,0:T(8,128)(2,1)S(1)} %get-tuple-element.48), channel_id=1, source_target_pairs={{0,9},{1,8},{2,11},{3,10},{4,13},{5,12},{6,15},{7,14},{8,1},{9,0},... | collective-permute-start | bytes 393224 | tf_op jit(solution)/shard_map/ppermute | solution.py:329
  79.6 8.3 %collective-permute-done.12.piece_ref = bf16[8,64,128]{2,1,0:T(8,128)(2,1)S(1)} collective-permute-done((bf16[8,64,128]{2,1,0:T(8,128)(2,1)S(1)}, bf16[8,64,128]{2,1,0:T(8,128)(2,1)S(1)}, u32[]{:S(2)}, u32[]{:S(2)}) %collective-permute-start.12) | collective-permute-done | bytes 131104 | tf_op jit(solution)/shard_map/ppermute | solution.py:329
  88.6 6.6 %collective-permute-start.10 = (bf16[8,64,128]{2,1,0:T(8,128)(2,1)S(1)}, bf16[8,64,128]{2,1,0:T(8,128)(2,1)S(1)}, u32[]{:S(2)}, u32[]{:S(2)}) collective-permute-start(bf16[8,64,128]{2,1,0:T(8,128)(2,1)S(1)} %get-tuple-element.47), channel_id=1, source_target_pairs={{0,10},{1,11},{2,12},{3,13},{4,14},{5,15},{6,8},{7,9},{8,2},{9,3},... | collective-permute-start | bytes 393224 | tf_op jit(solution)/shard_map/ppermute | solution.py:329
  95.9 1.7 %collective-permute-start.29 = (bf16[19,64,128]{2,1,0:T(8,128)(2,1)S(1)}, bf16[19,64,128]{2,1,0:T(8,128)(2,1)S(1)}, u32[]{:S(2)}, u32[]{:S(2)}) collective-permute-start(bf16[19,64,128]{2,1,0:T(8,128)(2,1)S(1)} %get-tuple-element.62), channel_id=1, source_target_pairs={{0,3},{1,2},{2,5},{3,4},{4,7},{5,6},{6,1},{7,0},{8,11},{9,10},{10,... | collective-permute-start | bytes 933896 | tf_op jit(solution)/shard_map/ppermute | solution.py:329
  98.3 1.4 collective-permute-start.28
  99.7 4.6 %collective-permute-start.27 = (bf16[19,64,128]{2,1,0:T(8,128)(2,1)S(1)}, bf16[19,64,128]{2,1,0:T(8,128)(2,1)S(1)}, u32[]{:S(2)}, u32[]{:S(2)}) collective-permute-start(bf16[19,64,128]{2,1,0:T(8,128)(2,1)S(1)} %get-tuple-element.60), channel_id=1, source_target_pairs={{0,5},{1,4},{2,7},{3,6},{4,1},{5,0},{6,3},{7,2},{8,13},{9,12},{10,... | collective-permute-start | bytes 933896 | tf_op jit(solution)/shard_map/ppermute | solution.py:329
  104.3 1.1 collective-permute-start.26
  105.5 0.7 split.1
  106.2 13.8 %collective-permute-start.24 = (bf16[7,64,128]{2,1,0:T(8,128)(2,1)S(1)}, bf16[7,64,128]{2,1,0:T(8,128)(2,1)S(1)}, u32[]{:S(2)}, u32[]{:S(2)}) collective-permute-start(bf16[7,64,128]{2,1,0:T(8,128)(2,1)S(1)} %get-tuple-element.57), channel_id=1, source_target_pairs={{0,1},{1,0},{2,3},{3,2},{4,5},{5,4},{6,7},{7,6},{8,9},{9,8},{10,11... | collective-permute-start | bytes 344072 | tf_op jit(solution)/shard_map/ppermute | solution.py:329
  120.0 3.1 %collective-permute-start.23 = (bf16[7,64,128]{2,1,0:T(8,128)(2,1)S(1)}, bf16[7,64,128]{2,1,0:T(8,128)(2,1)S(1)}, u32[]{:S(2)}, u32[]{:S(2)}) collective-permute-start(bf16[7,64,128]{2,1,0:T(8,128)(2,1)S(1)} %get-tuple-element.56), channel_id=1, source_target_pairs={{0,2},{1,3},{2,4},{3,5},{4,6},{5,7},{6,0},{7,1},{8,10},{9,11},{10,... | collective-permute-start | bytes 344072 | tf_op jit(solution)/shard_map/ppermute | solution.py:329
  123.2 0.7 copy-done
  123.9 1.0 collective-permute-start.21
  124.9 5.1 %collective-permute-done.25.piece_ref = bf16[19,64,128]{2,1,0:T(8,128)(2,1)S(1)} collective-permute-done((bf16[19,64,128]{2,1,0:T(8,128)(2,1)S(1)}, bf16[19,64,128]{2,1,0:T(8,128)(2,1)S(1)}, u32[]{:S(2)}, u32[]{:S(2)}) %collective-permute-start.25) | collective-permute-done | bytes 311328 | tf_op jit(solution)/shard_map/ppermute | solution.py:329
  130.1 2.4 %collective-permute-start.20 = (bf16[7,64,128]{2,1,0:T(8,128)(2,1)S(1)}, bf16[7,64,128]{2,1,0:T(8,128)(2,1)S(1)}, u32[]{:S(2)}, u32[]{:S(2)}) collective-permute-start(bf16[7,64,128]{2,1,0:T(8,128)(2,1)S(1)} %get-tuple-element.53), channel_id=1, source_target_pairs={{0,5},{1,4},{2,7},{3,6},{4,1},{5,0},{6,3},{7,2},{8,13},{9,12},{10,... | collective-permute-start | bytes 344072 | tf_op jit(solution)/shard_map/ppermute | solution.py:329
  132.5 0.8 collective-permute-start.18
  133.3 6.6 %collective-permute-start.9 = (bf16[8,64,128]{2,1,0:T(8,128)(2,1)}, bf16[8,64,128]{2,1,0:T(8,128)(2,1)S(1)}, u32[]{:S(2)}, u32[]{:S(2)}) collective-permute-start(bf16[8,64,128]{2,1,0:T(8,128)(2,1)} %get-tuple-element.46), channel_id=1, source_target_pairs={{0,11},{1,10},{2,13},{3,12},{4,15},{5,14},{6,9},{7,8},{8,3},{9,2},... | collective-permute-start | bytes 393224 | tf_op jit(solution)/shard_map/ppermute | solution.py:329
  139.8 1.0 collective-permute-start.8
  140.8 7.1 %collective-permute-start.7 = (bf16[8,64,128]{2,1,0:T(8,128)(2,1)}, bf16[8,64,128]{2,1,0:T(8,128)(2,1)S(1)}, u32[]{:S(2)}, u32[]{:S(2)}) collective-permute-start(bf16[8,64,128]{2,1,0:T(8,128)(2,1)} %get-tuple-element.44), channel_id=1, source_target_pairs={{0,13},{1,12},{2,15},{3,14},{4,9},{5,8},{6,11},{7,10},{8,5},{9,4},... | collective-permute-start | bytes 393224 | tf_op jit(solution)/shard_map/ppermute | solution.py:329
  147.9 4.6 %collective-permute-start.5 = (bf16[8,64,128]{2,1,0:T(8,128)(2,1)}, bf16[8,64,128]{2,1,0:T(8,128)(2,1)S(1)}, u32[]{:S(2)}, u32[]{:S(2)}) collective-permute-start(bf16[8,64,128]{2,1,0:T(8,128)(2,1)} %get-tuple-element.42), channel_id=1, source_target_pairs={{0,15},{1,14},{2,9},{3,8},{4,11},{5,10},{6,13},{7,12},{8,7},{9,6},... | collective-permute-start | bytes 393224 | tf_op jit(solution)/shard_map/ppermute | solution.py:329
  153.2 0.7 place_plane.7
  153.9 0.8 place_plane.8
  154.7 0.8 place_plane.9
  155.5 0.8 place_plane.10
  156.2 0.8 place_plane.11
  157.0 0.8 place_plane.12
  157.8 0.8 place_plane.13
  166.9 0.7 place_far.26._
  167.6 0.7 place_far.27._
  168.3 0.7 place_far.28._
  (72 shorter events, 12.9 us)
Async XLA Ops:
  0.6 10.5 %copy-start.8 = (f32[128,16]{0,1:T(8,128)S(1)}, f32[128,16]{0,1:T(8,128)}, u32[]{:S(2)}) copy-start(f32[128,16]{0,1:T(8,128)} %param.4) | copy-start | bytes 24580
  0.6 10.5 %copy-start.9 = (f32[128]{0:T(128)S(1)}, f32[128]{0:T(128)}, u32[]{:S(2)}) copy-start(f32[128]{0:T(128)} %param.5) | copy-start | bytes 1540
  5.0 7.8 %collective-permute-start = (f32[16,1024]{1,0:T(8,128)S(1)}, f32[16,1024]{1,0:T(8,128)S(1)}, u32[]{:S(2)}, u32[]{:S(2)}) collective-permute-start(f32[16,1024]{1,0:T(8,128)S(1)} %local_maxima.1), channel_id=1, source_target_pairs={{0,8},{1,9},{2,10},{3,11},{4,12},{5,13},{6,14},{7,15},{8,0},{9,1},... | collective-permute-start | bytes 196616 | tf_op jit(solution)/shard_map/ppermute | solution.py:329
  12.8 3.6 %collective-permute-start.1 = (f32[16,1024]{1,0:T(8,128)S(1)}, f32[16,1024]{1,0:T(8,128)S(1)}, u32[]{:S(2)}, u32[]{:S(2)}) collective-permute-start(f32[16,1024]{1,0:T(8,128)S(1)} %max.15), channel_id=1, source_target_pairs={{0,1},{1,0},{2,3},{3,2},{4,5},{5,4},{6,7},{7,6},{8,9},{9,8},{10,11... | collective-permute-start | bytes 196616 | tf_op jit(solution)/shard_map/ppermute | solution.py:329
  16.4 8.9 %collective-permute-start.2 = (f32[16,1024]{1,0:T(8,128)S(1)}, f32[16,1024]{1,0:T(8,128)S(1)}, u32[]{:S(2)}, u32[]{:S(2)}) collective-permute-start(f32[16,1024]{1,0:T(8,128)S(1)} %max.16), channel_id=1, source_target_pairs={{0,2},{1,3},{2,4},{3,5},{4,6},{5,7},{6,0},{7,1},{8,10},{9,11},{10,... | collective-permute-start | bytes 196616 | tf_op jit(solution)/shard_map/ppermute | solution.py:329
  16.7 8.6 %collective-permute-start.3 = (f32[16,1024]{1,0:T(8,128)S(1)}, f32[16,1024]{1,0:T(8,128)S(1)}, u32[]{:S(2)}, u32[]{:S(2)}) collective-permute-start(f32[16,1024]{1,0:T(8,128)S(1)} %max.16), channel_id=1, source_target_pairs={{0,6},{1,7},{2,0},{3,1},{4,2},{5,3},{6,4},{7,5},{8,14},{9,15},{10,... | collective-permute-start | bytes 196616 | tf_op jit(solution)/shard_map/ppermute | solution.py:329
  17.9 7.3 %collective-permute-start.4 = (f32[16,1024]{1,0:T(8,128)S(1)}, f32[16,1024]{1,0:T(8,128)S(1)}, u32[]{:S(2)}, u32[]{:S(2)}) collective-permute-start(f32[16,1024]{1,0:T(8,128)S(1)} %max.16), channel_id=1, source_target_pairs={{0,4},{1,5},{2,6},{3,7},{4,0},{5,1},{6,2},{7,3},{8,12},{9,13},{10,... | collective-permute-start | bytes 196616 | tf_op jit(solution)/shard_map/ppermute | solution.py:329
  19.1 33.1 %collective-permute-start.14 = (f32[528,128]{1,0:T(8,128)S(1)}, f32[528,128]{1,0:T(8,128)S(1)}, u32[]{:S(2)}, u32[]{:S(2)}) collective-permute-start(f32[528,128]{1,0:T(8,128)S(1)} %pad_maximum_fusion), channel_id=1, source_target_pairs={{0,8},{1,9},{2,10},{3,11},{4,12},{5,13},{6,14},{7,15},{8,0},{9,1},... | collective-permute-start | bytes 811016 | tf_op jit(solution)/shard_map/ppermute | solution.py:329
  27.7 77.7 %collective-permute-start.13 = (bf16[7,512,128]{2,1,0:T(8,128)(2,1)S(1)}, bf16[7,512,128]{2,1,0:T(8,128)(2,1)S(1)}, u32[]{:S(2)}, u32[]{:S(2)}) collective-permute-start(bf16[7,512,128]{2,1,0:T(8,128)(2,1)S(1)} %chunk.1), channel_id=1, source_target_pairs={{0,8},{1,9},{2,10},{3,11},{4,12},{5,13},{6,14},{7,15},{8,0},{9,1},... | collective-permute-start | bytes 2752520 | tf_op jit(solution)/shard_map/ppermute | solution.py:329
  34.7 53.2 %collective-permute-start.12 = (bf16[8,64,128]{2,1,0:T(8,128)(2,1)S(1)}, bf16[8,64,128]{2,1,0:T(8,128)(2,1)S(1)}, u32[]{:S(2)}, u32[]{:S(2)}) collective-permute-start(bf16[8,64,128]{2,1,0:T(8,128)(2,1)S(1)} %get-tuple-element.49), channel_id=1, source_target_pairs={{0,8},{1,9},{2,10},{3,11},{4,12},{5,13},{6,14},{7,15},{8,0},{9,1},... | collective-permute-start | bytes 393224 | tf_op jit(solution)/shard_map/ppermute | solution.py:329
  52.2 2.8 %collective-permute-start.15 = (bf16[2,16,128]{2,1,0:T(8,128)(2,1)S(1)}, bf16[2,16,128]{2,1,0:T(8,128)(2,1)S(1)}, u32[]{:S(2)}, u32[]{:S(2)}) collective-permute-start(bf16[2,16,128]{2,1,0:T(8,128)(2,1)S(1)} %pad_maximum_fusion.1.near_ref), channel_id=1, source_target_pairs={{0,16},{16,32},{32,48},{48,0},{1,17},{17,33},{33,49},{49,1},{2,18}... | collective-permute-start | bytes 24584 | tf_op jit(solution)/shard_map/ppermute | solution.py:355
  53.2 4.3 %collective-permute-start.16 = (bf16[2,16,128]{2,1,0:T(8,128)(2,1)S(1)}, bf16[2,16,128]{2,1,0:T(8,128)(2,1)S(1)}, u32[]{:S(2)}, u32[]{:S(2)}) collective-permute-start(bf16[2,16,128]{2,1,0:T(8,128)(2,1)S(1)} %pad_maximum_fusion.1.near_ref), channel_id=1, source_target_pairs={{0,32},{16,48},{32,0},{48,16},{1,33},{17,49},{33,1},{49,17},{2,34}... | collective-permute-start | bytes 24584 | tf_op jit(solution)/shard_map/ppermute | solution.py:355
  53.5 4.0 %collective-permute-start.17 = (bf16[2,16,128]{2,1,0:T(8,128)(2,1)S(1)}, bf16[2,16,128]{2,1,0:T(8,128)(2,1)S(1)}, u32[]{:S(2)}, u32[]{:S(2)}) collective-permute-start(bf16[2,16,128]{2,1,0:T(8,128)(2,1)S(1)} %pad_maximum_fusion.1.near_ref), channel_id=1, source_target_pairs={{0,48},{16,0},{32,16},{48,32},{1,49},{17,1},{33,17},{49,33},{2,50}... | collective-permute-start | bytes 24584 | tf_op jit(solution)/shard_map/ppermute | solution.py:355
  61.3 38.4 %collective-permute-start.31 = (bf16[19,64,128]{2,1,0:T(8,128)(2,1)S(1)}, bf16[19,64,128]{2,1,0:T(8,128)(2,1)S(1)}, u32[]{:S(2)}, u32[]{:S(2)}) collective-permute-start(bf16[19,64,128]{2,1,0:T(8,128)(2,1)S(1)} %get-tuple-element.64), channel_id=1, source_target_pairs={{0,1},{1,0},{2,3},{3,2},{4,5},{5,4},{6,7},{7,6},{8,9},{9,8},{10,11... | collective-permute-start | bytes 933896 | tf_op jit(solution)/shard_map/ppermute | solution.py:329
  72.5 31.8 %collective-permute-start.30 = (bf16[19,64,128]{2,1,0:T(8,128)(2,1)S(1)}, bf16[19,64,128]{2,1,0:T(8,128)(2,1)S(1)}, u32[]{:S(2)}, u32[]{:S(2)}) collective-permute-start(bf16[19,64,128]{2,1,0:T(8,128)(2,1)S(1)} %get-tuple-element.63), channel_id=1, source_target_pairs={{0,2},{1,3},{2,4},{3,5},{4,6},{5,7},{6,0},{7,1},{8,10},{9,11},{10,... | collective-permute-start | bytes 933896 | tf_op jit(solution)/shard_map/ppermute | solution.py:329
  74.3 21.0 %collective-permute-start.11 = (bf16[8,64,128]{2,1,0:T(8,128)(2,1)S(1)}, bf16[8,64,128]{2,1,0:T(8,128)(2,1)S(1)}, u32[]{:S(2)}, u32[]{:S(2)}) collective-permute-start(bf16[8,64,128]{2,1,0:T(8,128)(2,1)S(1)} %get-tuple-element.48), channel_id=1, source_target_pairs={{0,9},{1,8},{2,11},{3,10},{4,13},{5,12},{6,15},{7,14},{8,1},{9,0},... | collective-permute-start | bytes 393224 | tf_op jit(solution)/shard_map/ppermute | solution.py:329
  87.9 0.7 copy-start.2
  88.6 9.0 %collective-permute-start.10 = (bf16[8,64,128]{2,1,0:T(8,128)(2,1)S(1)}, bf16[8,64,128]{2,1,0:T(8,128)(2,1)S(1)}, u32[]{:S(2)}, u32[]{:S(2)}) collective-permute-start(bf16[8,64,128]{2,1,0:T(8,128)(2,1)S(1)} %get-tuple-element.47), channel_id=1, source_target_pairs={{0,10},{1,11},{2,12},{3,13},{4,14},{5,15},{6,8},{7,9},{8,2},{9,3},... | collective-permute-start | bytes 393224 | tf_op jit(solution)/shard_map/ppermute | solution.py:329
  95.2 0.7 copy-start.4
  95.9 10.3 %collective-permute-start.29 = (bf16[19,64,128]{2,1,0:T(8,128)(2,1)S(1)}, bf16[19,64,128]{2,1,0:T(8,128)(2,1)S(1)}, u32[]{:S(2)}, u32[]{:S(2)}) collective-permute-start(bf16[19,64,128]{2,1,0:T(8,128)(2,1)S(1)} %get-tuple-element.62), channel_id=1, source_target_pairs={{0,3},{1,2},{2,5},{3,4},{4,7},{5,6},{6,1},{7,0},{8,11},{9,10},{10,... | collective-permute-start | bytes 933896 | tf_op jit(solution)/shard_map/ppermute | solution.py:329
  97.6 0.6 copy-start.6
  98.3 21.7 %collective-permute-start.28 = (bf16[19,64,128]{2,1,0:T(8,128)(2,1)S(1)}, bf16[19,64,128]{2,1,0:T(8,128)(2,1)S(1)}, u32[]{:S(2)}, u32[]{:S(2)}) collective-permute-start(bf16[19,64,128]{2,1,0:T(8,128)(2,1)S(1)} %get-tuple-element.61), channel_id=1, source_target_pairs={{0,4},{1,5},{2,6},{3,7},{4,0},{5,1},{6,2},{7,3},{8,12},{9,13},{10,... | collective-permute-start | bytes 933896 | tf_op jit(solution)/shard_map/ppermute | solution.py:329
  99.7 23.4 %collective-permute-start.27 = (bf16[19,64,128]{2,1,0:T(8,128)(2,1)S(1)}, bf16[19,64,128]{2,1,0:T(8,128)(2,1)S(1)}, u32[]{:S(2)}, u32[]{:S(2)}) collective-permute-start(bf16[19,64,128]{2,1,0:T(8,128)(2,1)S(1)} %get-tuple-element.60), channel_id=1, source_target_pairs={{0,5},{1,4},{2,7},{3,6},{4,1},{5,0},{6,3},{7,2},{8,13},{9,12},{10,... | collective-permute-start | bytes 933896 | tf_op jit(solution)/shard_map/ppermute | solution.py:329
  104.3 18.9 %collective-permute-start.26 = (bf16[19,64,128]{2,1,0:T(8,128)(2,1)S(1)}, bf16[19,64,128]{2,1,0:T(8,128)(2,1)S(1)}, u32[]{:S(2)}, u32[]{:S(2)}) collective-permute-start(bf16[19,64,128]{2,1,0:T(8,128)(2,1)S(1)} %get-tuple-element.59), channel_id=1, source_target_pairs={{0,6},{1,7},{2,0},{3,1},{4,2},{5,3},{6,4},{7,5},{8,14},{9,15},{10,... | collective-permute-start | bytes 933896 | tf_op jit(solution)/shard_map/ppermute | solution.py:329
  105.5 24.6 %collective-permute-start.25 = (bf16[19,64,128]{2,1,0:T(8,128)(2,1)S(1)}, bf16[19,64,128]{2,1,0:T(8,128)(2,1)S(1)}, u32[]{:S(2)}, u32[]{:S(2)}) collective-permute-start(bf16[19,64,128]{2,1,0:T(8,128)(2,1)S(1)} %get-tuple-element.58), channel_id=1, source_target_pairs={{0,7},{1,6},{2,1},{3,0},{4,3},{5,2},{6,5},{7,4},{8,15},{9,14},{10,... | collective-permute-start | bytes 933896 | tf_op jit(solution)/shard_map/ppermute | solution.py:329
  106.2 26.2 %collective-permute-start.24 = (bf16[7,64,128]{2,1,0:T(8,128)(2,1)S(1)}, bf16[7,64,128]{2,1,0:T(8,128)(2,1)S(1)}, u32[]{:S(2)}, u32[]{:S(2)}) collective-permute-start(bf16[7,64,128]{2,1,0:T(8,128)(2,1)S(1)} %get-tuple-element.57), channel_id=1, source_target_pairs={{0,1},{1,0},{2,3},{3,2},{4,5},{5,4},{6,7},{7,6},{8,9},{9,8},{10,11... | collective-permute-start | bytes 344072 | tf_op jit(solution)/shard_map/ppermute | solution.py:329
  120.0 12.5 %collective-permute-start.23 = (bf16[7,64,128]{2,1,0:T(8,128)(2,1)S(1)}, bf16[7,64,128]{2,1,0:T(8,128)(2,1)S(1)}, u32[]{:S(2)}, u32[]{:S(2)}) collective-permute-start(bf16[7,64,128]{2,1,0:T(8,128)(2,1)S(1)} %get-tuple-element.56), channel_id=1, source_target_pairs={{0,2},{1,3},{2,4},{3,5},{4,6},{5,7},{6,0},{7,1},{8,10},{9,11},{10,... | collective-permute-start | bytes 344072 | tf_op jit(solution)/shard_map/ppermute | solution.py:329
  123.1 10.2 %collective-permute-start.22 = (bf16[7,64,128]{2,1,0:T(8,128)(2,1)S(1)}, bf16[7,64,128]{2,1,0:T(8,128)(2,1)S(1)}, u32[]{:S(2)}, u32[]{:S(2)}) collective-permute-start(bf16[7,64,128]{2,1,0:T(8,128)(2,1)S(1)} %get-tuple-element.55), channel_id=1, source_target_pairs={{0,3},{1,2},{2,5},{3,4},{4,7},{5,6},{6,1},{7,0},{8,11},{9,10},{10,... | collective-permute-start | bytes 344072 | tf_op jit(solution)/shard_map/ppermute | solution.py:329
  123.2 0.7 copy-start
  123.9 15.9 %collective-permute-start.21 = (bf16[7,64,128]{2,1,0:T(8,128)(2,1)S(1)}, bf16[7,64,128]{2,1,0:T(8,128)(2,1)S(1)}, u32[]{:S(2)}, u32[]{:S(2)}) collective-permute-start(bf16[7,64,128]{2,1,0:T(8,128)(2,1)S(1)} %get-tuple-element.54), channel_id=1, source_target_pairs={{0,4},{1,5},{2,6},{3,7},{4,0},{5,1},{6,2},{7,3},{8,12},{9,13},{10,... | collective-permute-start | bytes 344072 | tf_op jit(solution)/shard_map/ppermute | solution.py:329
  130.1 10.7 %collective-permute-start.20 = (bf16[7,64,128]{2,1,0:T(8,128)(2,1)S(1)}, bf16[7,64,128]{2,1,0:T(8,128)(2,1)S(1)}, u32[]{:S(2)}, u32[]{:S(2)}) collective-permute-start(bf16[7,64,128]{2,1,0:T(8,128)(2,1)S(1)} %get-tuple-element.53), channel_id=1, source_target_pairs={{0,5},{1,4},{2,7},{3,6},{4,1},{5,0},{6,3},{7,2},{8,13},{9,12},{10,... | collective-permute-start | bytes 344072 | tf_op jit(solution)/shard_map/ppermute | solution.py:329
  132.4 15.4 %collective-permute-start.19 = (bf16[7,64,128]{2,1,0:T(8,128)(2,1)S(1)}, bf16[7,64,128]{2,1,0:T(8,128)(2,1)S(1)}, u32[]{:S(2)}, u32[]{:S(2)}) collective-permute-start(bf16[7,64,128]{2,1,0:T(8,128)(2,1)S(1)} %get-tuple-element.52), channel_id=1, source_target_pairs={{0,6},{1,7},{2,0},{3,1},{4,2},{5,3},{6,4},{7,5},{8,14},{9,15},{10,... | collective-permute-start | bytes 344072 | tf_op jit(solution)/shard_map/ppermute | solution.py:329
  132.5 15.4 %collective-permute-start.18 = (bf16[7,64,128]{2,1,0:T(8,128)(2,1)S(1)}, bf16[7,64,128]{2,1,0:T(8,128)(2,1)S(1)}, u32[]{:S(2)}, u32[]{:S(2)}) collective-permute-start(bf16[7,64,128]{2,1,0:T(8,128)(2,1)S(1)} %get-tuple-element.51), channel_id=1, source_target_pairs={{0,7},{1,6},{2,1},{3,0},{4,3},{5,2},{6,5},{7,4},{8,15},{9,14},{10,... | collective-permute-start | bytes 344072 | tf_op jit(solution)/shard_map/ppermute | solution.py:329
  133.3 32.9 %collective-permute-start.9 = (bf16[8,64,128]{2,1,0:T(8,128)(2,1)}, bf16[8,64,128]{2,1,0:T(8,128)(2,1)S(1)}, u32[]{:S(2)}, u32[]{:S(2)}) collective-permute-start(bf16[8,64,128]{2,1,0:T(8,128)(2,1)} %get-tuple-element.46), channel_id=1, source_target_pairs={{0,11},{1,10},{2,13},{3,12},{4,15},{5,14},{6,9},{7,8},{8,3},{9,2},... | collective-permute-start | bytes 393224 | tf_op jit(solution)/shard_map/ppermute | solution.py:329
  139.8 27.1 %collective-permute-start.8 = (bf16[8,64,128]{2,1,0:T(8,128)(2,1)}, bf16[8,64,128]{2,1,0:T(8,128)(2,1)S(1)}, u32[]{:S(2)}, u32[]{:S(2)}) collective-permute-start(bf16[8,64,128]{2,1,0:T(8,128)(2,1)} %get-tuple-element.45), channel_id=1, source_target_pairs={{0,12},{1,13},{2,14},{3,15},{4,8},{5,9},{6,10},{7,11},{8,4},{9,5},... | collective-permute-start | bytes 393224 | tf_op jit(solution)/shard_map/ppermute | solution.py:329
  140.8 26.8 %collective-permute-start.7 = (bf16[8,64,128]{2,1,0:T(8,128)(2,1)}, bf16[8,64,128]{2,1,0:T(8,128)(2,1)S(1)}, u32[]{:S(2)}, u32[]{:S(2)}) collective-permute-start(bf16[8,64,128]{2,1,0:T(8,128)(2,1)} %get-tuple-element.44), channel_id=1, source_target_pairs={{0,13},{1,12},{2,15},{3,14},{4,9},{5,8},{6,11},{7,10},{8,5},{9,4},... | collective-permute-start | bytes 393224 | tf_op jit(solution)/shard_map/ppermute | solution.py:329
  147.9 20.4 %collective-permute-start.6 = (bf16[8,64,128]{2,1,0:T(8,128)(2,1)}, bf16[8,64,128]{2,1,0:T(8,128)(2,1)S(1)}, u32[]{:S(2)}, u32[]{:S(2)}) collective-permute-start(bf16[8,64,128]{2,1,0:T(8,128)(2,1)} %get-tuple-element.43), channel_id=1, source_target_pairs={{0,14},{1,15},{2,8},{3,9},{4,10},{5,11},{6,12},{7,13},{8,6},{9,7},... | collective-permute-start | bytes 393224 | tf_op jit(solution)/shard_map/ppermute | solution.py:329
  147.9 21.1 %collective-permute-start.5 = (bf16[8,64,128]{2,1,0:T(8,128)(2,1)}, bf16[8,64,128]{2,1,0:T(8,128)(2,1)S(1)}, u32[]{:S(2)}, u32[]{:S(2)}) collective-permute-start(bf16[8,64,128]{2,1,0:T(8,128)(2,1)} %get-tuple-element.42), channel_id=1, source_target_pairs={{0,15},{1,14},{2,9},{3,8},{4,11},{5,10},{6,13},{7,12},{8,7},{9,6},... | collective-permute-start | bytes 393224 | tf_op jit(solution)/shard_map/ppermute | solution.py:329
  155.5 1.6 copy-start.1
  162.7 0.9 copy-start.3
  163.6 1.0 copy-start.5
  164.6 1.0 copy-start.7

commit v3 on v0

v3 whole, which is shorter than its diff:
```python
import functools

import jax
import jax.numpy as jnp
from jax import lax
from jax.experimental import pallas as pl
from jax.experimental.pallas import tpu as pltpu
from jax.sharding import PartitionSpec as P


RELAY = 7
EARLY = 1
BF16, F32 = jnp.bfloat16, jnp.float32
ANY = pl.BlockSpec(memory_space=pl.ANY)
VMEM = pl.BlockSpec(memory_space=pltpu.VMEM)
SMEM = pl.BlockSpec(memory_space=pltpu.SMEM)


def params(mebibytes):
    return pltpu.CompilerParams(vmem_limit_bytes=mebibytes * 2**20)


def cost(read, written):
    return pl.CostEstimate(flops=(read + written) * 4, bytes_accessed=read + written, transcendentals=0)


def array(*shape, kind=BF16):
    return jax.ShapeDtypeStruct(shape, kind)


def span(start, size):
    return pl.ds(pl.multiple_of(start, size), size)


def lanes(position):
    return span(position * 128, 128)


def route(dz, dx, dc):
    pairs = []
    for f in range(16):
        z, x, c = f // 8, f // 2 % 4, f % 2
        pairs.append((f, (z ^ dz) * 8 + (x + dx) % 4 * 2 + (c ^ dc)))
    return pairs


def send(piece, dz, dx, dc):
    return lax.ppermute(piece, "fsdp", route(dz, dx, dc))


def chip(f, dz, dx):
    z = f // 8 if dz == 0 else 1 - f // 8
    return z * 4 + (f // 2 + dx) % 4


def run(copies):
    for copy in copies:
        copy.start()
    for copy in copies:
        copy.wait()


def parts(experts):
    return (0, RELAY), (RELAY, experts - RELAY - EARLY), (experts - EARLY, EARLY)


def local_kernel(f_ref, w_ref, out_ref, *refs):
    swap_refs, (taken, in_sems, out_sems) = refs[:3], refs[3:]
    blocks, experts = taken.shape[:2]
    away = 1 - f_ref[0] % 2
    reads = []
    for b in range(blocks):
        reads.append(pltpu.make_async_copy(w_ref.at[:, pl.ds(128 * b, 128), :], taken.at[b], in_sems.at[b]))
        reads[-1].start()
    lane = lax.broadcasted_iota(jnp.int32, (128, 128), 1)
    writes = []
    for b in range(blocks):
        reads[b].wait()
        for k, ((first, count), target) in enumerate(zip(parts(experts), swap_refs)):
            rows = taken.at[b, pl.ds(first, count), span(64 * away, 64), :]
            writes.append(
                pltpu.make_async_copy(rows, target.at[:, pl.ds(64 * b, 64), :], out_sems.at[3 * b + k])
            )
            writes[-1].start()
        total = jnp.zeros((128, 128), F32)
        for e in range(experts):
            row = jnp.max(jnp.abs(taken[b, e]), axis=1, keepdims=True)
            total = jnp.where(lane == e, row, total)
        out_ref[:, pl.ds(128 * b, 128)] = total.T[:experts]
    for write in writes:
        write.wait()


def local_maxima(f, w):
    experts, rows, _ = w.shape
    blocks = rows // 128
    return pl.pallas_call(
        local_kernel,
        out_shape=[
            array(experts, rows, kind=F32),
            *(array(count, rows // 2, 128, kind=F32) for _, count in parts(experts)),
        ],
        in_specs=[SMEM, ANY],
        out_specs=[VMEM, ANY, ANY, ANY],
        scratch_shapes=[
            pltpu.VMEM((blocks, experts, 128, 128), F32),
            pltpu.SemaphoreType.DMA((blocks,)),
            pltpu.SemaphoreType.DMA((3 * blocks,)),
        ],
        compiler_params=params(50),
        cost_estimate=cost(8 * 2**20, 4 * 2**20),
        name="local_maxima",
    )(f, w)


def inverse_columns(scale_ref, inverse, slot, block):
    inverse[pl.ds(128 * slot, 128), :] = jnp.concatenate([1.0 / scale_ref[:, lanes(block)]] * 8, axis=0).T


def far_kernel(plan, f_ref, w_ref, theirs_ref, scale_ref, *refs):
    first, count, whole = plan
    outs, (taken, inverse, made, in_sems, out_sems) = refs[:-5], refs[-5:]
    f = f_ref[0]
    core = f % 2
    experts = pl.ds(first, count)
    reads = []
    for dx in range(4):
        q = 4 * (1 - f // 8) + dx if whole else chip(f, 1, dx)
        own = w_ref.at[experts, span(128 * q + 64 * core, 64), :]
        theirs = theirs_ref.at[:, span(64 * q, 64), :]
        for k, rows in enumerate((own, theirs)):
            reads.append(
                pltpu.make_async_copy(rows, taken.at[dx, pl.ds(k * count, count)], in_sems.at[2 * dx + k])
            )
            reads[-1].start()
    writes = []
    for dx in range(4):
        q = 4 * (1 - f // 8) + dx if whole else chip(f, 1, dx)
        inverse_columns(scale_ref, inverse, dx, q)
        columns = inverse[span(128 * dx + 64 * core, 64), :]
        for k in range(2):
            reads[2 * dx + k].wait()
            for e in range(count):
                at, lane = k * count + e, first + e
                made[dx, at] = (taken[dx, at] * columns[:, lane : lane + 1]).astype(BF16)
        target = outs[0].at[:, pl.ds(64 * dx, 64), :] if whole else outs[dx]
        writes.append(pltpu.make_async_copy(made.at[dx], target, out_sems.at[dx]))
        writes[-1].start()
    for write in writes:
        write.wait()


def far_pieces(f, w, theirs, scale, first, count, whole):
    outs = [array(2 * count, 256, 128)] if whole else [array(2 * count, 64, 128)] * 4
    return pl.pallas_call(
        functools.partial(far_kernel, (first, count, whole)),
        out_shape=outs,
        in_specs=[SMEM, ANY, ANY, VMEM],
        out_specs=[ANY] * len(outs),
        scratch_shapes=[
            pltpu.VMEM((4, 2 * count, 64, 128), F32),
            pltpu.VMEM((512, 128), F32),
            pltpu.VMEM((4, 2 * count, 64, 128), BF16),
            pltpu.SemaphoreType.DMA((8,)),
            pltpu.SemaphoreType.DMA((4,)),
        ],
        compiler_params=params(50),
        cost_estimate=cost(2 * 2**20, 2**20),
        name="far_pieces",
    )(f, w, theirs, scale)


def near_kernel(f_ref, y_ref, w_ref, scale_ref, relay_ref, *refs):
    rows_refs, theirs_refs, refs = refs[:4], refs[4:7], refs[7:]
    outs, (final_ref, router_ref), (taken, inverse, made, in_sems, out_sems) = refs[:3], refs[3:5], refs[5:]
    experts = w_ref.shape[0]
    late = experts - EARLY
    f, y = f_ref[0], y_ref[0]
    core = f % 2
    reads = []
    for dx in range(4):
        q = chip(f, 0, dx)
        own = w_ref.at[:, span(128 * q + 64 * core, 64), :]
        rows = [(own, 0, experts)]
        for (first, count), theirs_ref in zip(parts(experts), theirs_refs):
            rows.append((theirs_ref.at[:, span(64 * q, 64), :], experts + first, count))
        for k, (piece, at, size) in enumerate(rows):
            reads.append(pltpu.make_async_copy(piece, taken.at[dx, pl.ds(at, size)], in_sems.at[4 * dx + k]))
            reads[-1].start()
    for dx in range(4):
        q = chip(f, 0, dx)
        inverse_columns(scale_ref, inverse, dx, q)
        columns = inverse[span(128 * dx + 64 * core, 64), :]
        for k in range(4):
            reads[4 * dx + k].wait()
        for k in range(2):
            for e in range(experts):
                at = k * experts + e
                made[dx, at] = (taken[dx, at] * columns[:, e : e + 1]).astype(BF16)
            for j in range(EARLY):
                rows = relay_ref[span(256 * (k * EARLY + j) + 64 * (q % 4), 64), :]
                lane = late + j
                made[dx, 2 * experts + k * EARLY + j] = (rows * columns[:, lane : lane + 1]).astype(BF16)
        for k in range(4):
            for dy, piece in enumerate(rows_refs):
                made[dx, 2 * experts + 2 * EARLY + k, span((y - dy + 4) % 4 * 16, 16), :] = piece[k]
    copies = [pltpu.make_async_copy(made.at[dx], outs[dx - 1], out_sems.at[dx]) for dx in (1, 2, 3)]
    copies += near_copies(f, f // 2, made.at[0], final_ref, router_ref, out_sems, 4)
    run(copies)


def near_copies(f, source, piece, final_ref, router_ref, sems, at):
    experts = final_ref.shape[0]
    core = f % 2
    across = (source + 4) % 8
    early = pl.ds(experts - EARLY, EARLY)
    copies = []
    for k in range(2):
        side = core if k == 0 else 1 - core
        copies.append((piece.at[pl.ds(k * experts, experts)], final_ref.at[:, :, lanes(2 * source + side)]))
        copies.append(
            (
                piece.at[pl.ds(2 * experts + k * EARLY, EARLY)],
                final_ref.at[early, :, lanes(2 * across + side)],
            )
        )
        for j, q in enumerate((source, across)):
            copies.append(
                (piece.at[2 * experts + 2 * EARLY + 2 * k + j], router_ref.at[:, lanes(2 * q + side)])
            )
    return [pltpu.make_async_copy(a, b, sems.at[at + k]) for k, (a, b) in enumerate(copies)]


def near_pieces(f, y, w, scale, relay, rows, theirs):
    experts = w.shape[0]
    blocks = 2 * experts + 2 * EARLY + 4
    return pl.pallas_call(
        near_kernel,
        out_shape=[array(blocks, 64, 128)] * 3 + [array(experts, 64, 2048), array(64, 2048)],
        in_specs=[SMEM, SMEM, ANY] + [VMEM] * 6 + [ANY] * 3,
        out_specs=[ANY] * 5,
        scratch_shapes=[
            pltpu.VMEM((4, 2 * experts, 64, 128), F32),
            pltpu.VMEM((512, 128), F32),
            pltpu.VMEM((4, blocks, 64, 128), BF16),
            pltpu.SemaphoreType.DMA((16,)),
            pltpu.SemaphoreType.DMA((12,)),
        ],
        compiler_params=params(50),
        cost_estimate=cost(5 * 2**20, 3 * 2**20),
        name="near_pieces",
    )(f, y, w, scale, relay, *rows, *theirs)


def split_kernel(f_ref, chunk_ref, _, *refs):
    outs, final_ref, sems = refs[:3], refs[3], refs[4]
    f = f_ref[0]
    copies = []
    for dx in (1, 2, 3):
        rows = chunk_ref.at[:, span(64 * (chip(f, 0, dx) % 4), 64), :]
        copies.append(pltpu.make_async_copy(rows, outs[dx - 1], sems.at[dx - 1]))
    rows = chunk_ref.at[:, span(64 * (chip(f, 0, 0) % 4), 64), :]
    run(copies + far_copies(f, chip(f, 1, 0), 0, rows, final_ref, sems, 3))


def far_copies(f, source, first, piece, final_ref, sems, at):
    count = piece.shape[0] // 2
    copies = []
    for k in range(2):
        side = f % 2 if k == 0 else 1 - f % 2
        target = final_ref.at[pl.ds(first, count), :, lanes(2 * source + side)]
        copies.append(pltpu.make_async_copy(piece.at[pl.ds(k * count, count)], target, sems.at[at + k]))
    return copies


def split(f, chunk, final):
    return pl.pallas_call(
        split_kernel,
        out_shape=[array(chunk.shape[0], 64, 128)] * 3 + [array(*final.shape)],
        in_specs=[SMEM, VMEM, ANY],
        out_specs=[ANY] * 4,
        scratch_shapes=[pltpu.SemaphoreType.DMA((5,))],
        input_output_aliases={2: 3},
        compiler_params=params(50),
        cost_estimate=cost(2**20, 2**20),
        name="split",
    )(f, chunk, final)


def place_far_kernel(dx, first, f_ref, piece_ref, _, final_ref, sems):
    f = f_ref[0]
    run(far_copies(f, chip(f, 1, 4 - dx), first, piece_ref, final_ref, sems, 0))


def place_far(dx, first, f, piece, final):
    return pl.pallas_call(
        functools.partial(place_far_kernel, dx, first),
        out_shape=array(*final.shape),
        in_specs=[SMEM, VMEM, ANY],
        out_specs=ANY,
        scratch_shapes=[pltpu.SemaphoreType.DMA((2,))],
        input_output_aliases={2: 0},
        compiler_params=params(2),
        cost_estimate=cost(2**18, 2**18),
        name="place_far",
    )(f, piece, final)


def place_near_kernel(dx, f_ref, piece_ref, _, __, final_ref, router_ref, sems):
    f = f_ref[0]
    run(near_copies(f, chip(f, 0, 4 - dx), piece_ref, final_ref, router_ref, sems, 0))


def place_near(dx, f, piece, final, router):
    return pl.pallas_call(
        functools.partial(place_near_kernel, dx),
        out_shape=[array(*final.shape), array(*router.shape)],
        in_specs=[SMEM, VMEM, ANY, ANY],
        out_specs=[ANY, ANY],
        scratch_shapes=[pltpu.SemaphoreType.DMA((8,))],
        input_output_aliases={2: 0, 3: 1},
        compiler_params=params(2),
        cost_estimate=cost(2**19, 2**19),
        name="place_near",
    )(f, piece, final, router)


def served(w, router_weight, router_gain):
    experts, _, _ = w.shape
    position = lax.axis_index("fsdp")
    f = position.reshape(1)
    y = lax.axis_index("ep").reshape(1)
    far_plane = 1 - position // 8

    scale, swap, swap_direct, swap_early = local_maxima(f, w)
    theirs_early = send(swap_early, 0, 0, 1)
    peer = send(scale, 1, 0, 0)
    product = router_weight.T * router_gain.reshape(1, -1)
    own = lax.dynamic_slice(
        w.reshape(experts, 8, 2, 64, 128), (experts - EARLY, 4 * far_plane, position % 2, 0, 0), (EARLY, 4, 1, 64, 128)
    )
    other = lax.dynamic_slice(theirs_early, (0, 256 * far_plane, 0), (EARLY, 256, 128))
    early = jnp.concatenate([own.reshape(-1, 128), other.reshape(-1, 128), product])
    relay = send(early, 1, 0, 0)
    theirs = send(swap, 0, 0, 1)
    theirs_direct = send(swap_direct, 0, 0, 1)
    scale = jnp.maximum(scale, peer)
    scale = jnp.maximum(scale, send(scale, 0, 0, 1))
    scale = functools.reduce(jnp.maximum, [scale] + [send(scale, 0, dx, 0) for dx in (1, 3, 2)])

    (chunk,) = far_pieces(f, w, theirs, scale, 0, RELAY, True)
    forward = send(chunk, 1, 0, 0)
    near = jnp.stack([product, relay[2 * EARLY * 256 :]]).astype(BF16)
    near = jnp.concatenate([near, send(near, 0, 0, 1)])
    received = [near]
    for d in (1, 2, 3):
        received.append(lax.ppermute(near, "ep", [(i, (i + d) % 4) for i in range(4)]))
    *pieces, final, router = near_pieces(f, y, w, scale, relay, received, (theirs, theirs_direct, theirs_early))
    plane = [send(piece, 0, k + 1, 0) for k, piece in enumerate(pieces)]
    pieces = far_pieces(f, w, theirs_direct, scale, RELAY, experts - RELAY - EARLY, False)
    across = [send(piece, 1, k, 0) for k, piece in enumerate(pieces)]
    for k in range(3):
        final, router = place_near(k + 1, f, plane[k], final, router)
    *pieces, final = split(f, forward, final)
    relayed = [send(piece, 0, k + 1, 0) for k, piece in enumerate(pieces)]
    for k in range(3):
        final = place_far(k + 1, 0, f, relayed[k], final)
    for k in range(4):
        final = place_far(k, RELAY, f, across[k], final)
    own = lax.dynamic_slice_in_dim(scale, position * 64, 64, axis=1)
    return final, own, router.T


def solution(mesh):
    return jax.shard_map(
        served,
        mesh=mesh,
        in_specs=(
            P(("trial", "ep"), None, "fsdp"),
            P(("trial", "fsdp"), "ep"),
            P(("trial", "fsdp")),
        ),
        out_specs=(P(("trial", "ep"), "fsdp", None), P(("trial", "ep"), "fsdp"), P("trial", None)),
        check_vma=False,
    )
```

time: 195 us -> 147 us (0.75); the launches traced: 194 us -> 144 us
  waiting for transfers between devices: 126 us -> 67.7 us
  Pallas kernels: 0 us -> 22.7 us
  starting transfers between devices: 25.5 us -> 47.7 us
  other arithmetic: 15.3 us -> 0.07 us
  local copies, waits for them, and re-layouts: 17.4 us -> 4.63 us
  blocking collectives: 9.36 us -> 0 us
    all_to_all x3 -> x0, waiting for transfers between devices: 126 us -> none  [the longest x1 96.2 us: shards(): lax.all_to_all(narrow_down, 'fsdp', split_axis=1, concat_axis=2, tiled=True)]
    ppermute x0 -> x24, waiting for transfers between devices: none -> 67.7 us  [the longest x21 64.5 us: send(): return lax.ppermute(piece, 'fsdp', route(dz, dx, dc))]
    ppermute x0 -> x24, starting transfers between devices: none -> 47.7 us  [the longest x21 45.4 us: send(): return lax.ppermute(piece, 'fsdp', route(dz, dx, dc))]
    all_to_all x3 -> x0, starting transfers between devices: 25.5 us -> none  [the longest x2 15.8 us: copy_for_each(): return lax.all_to_all(copies, axis, split_axis=0, concat_axis=0, tiled=True)]
    pallas_call x0 -> x15, Pallas kernels: none -> 22.7 us  [the longest x1 5.39 us: local_maxima(): pl.pallas_call(local_kernel, out_shape=[array(experts, rows, kind=F32), *...]
    all_to_all x2 -> x0, local copies, waits for them, and re-layouts: 14.1 us -> none  [shards(): lax.all_to_all(narrow_down, 'fsdp', split_axis=1, concat_axis=2, tiled=True)]
    convert_element_type x2 -> x0, other arithmetic: 9.63 us -> none  [the longest x1 9.63 us: shards(): (master_down / jnp.expand_dims(scale_down, 2)).astype(jnp.bfloat16)]
    all_gather x1 -> x0, blocking collectives: 9.36 us -> none  [shards(): serve_router = lax.all_gather(row_router, 'ep', axis=1, tiled=True)]
  transfers between devices with their start and end apart: 3 -> 24, of which waited for: 2 -> 14; matrix products, arithmetic and copies ran while one was open for 5% -> 1% of each run, Pallas kernels for 0% -> 11%
where the time goes in v3:
time: 147 us; the launch traced here: 144 us
  waiting for transfers between devices  67.7 us (46%)
  starting transfers between devices  47.7 us (32%)
  Pallas kernels  22.7 us (15%)
  local copies, waits for them, and re-layouts  4.63 us (3%)
    ppermute x21, waiting for transfers between devices, send(): return lax.ppermute(piece, 'fsdp', route(dz, dx, dc))  64.5 us
    ppermute x21, starting transfers between devices, send(): return lax.ppermute(piece, 'fsdp', route(dz, dx, dc))  45.4 us
    pallas_call x1, Pallas kernels, local_maxima(): pl.pallas_call(local_kernel, out_shape=[array(experts, rows, kind=F32), *...  5.39 us
    pallas_call x7, Pallas kernels, place_far(): pl.pallas_call(functools.partial(place_far_kernel, dx, first), out_shape=...  4.98 us
    pallas_call x2, Pallas kernels, far_pieces(): pl.pallas_call(functools.partial(far_kernel, (first, count, whole)), out_...  4.84 us
    pallas_call x1, Pallas kernels, near_pieces(): pl.pallas_call(near_kernel, out_shape=[array(blocks, 64, 128)] * 3 + [arr...  3.98 us
    ppermute x3, waiting for transfers between devices, served(): lax.ppermute(near, 'ep', [(i, (i + d) % 4) for i in range(4)])  3.12 us
    unnamed x12, local copies, waits for them, and re-layouts  3.03 us
  transfers between devices with their start and end apart: 24, of which 14 were waited for; matrix products, arithmetic and copies ran while one was open for 1% of the time, Pallas kernels for 11%

profile of v3, /device:TPU:55, one launch (start us, length us, event | category | flops | bytes accessed | tf_op | source)
XLA Modules:
  0.0 143.8 jit_solution(4787452932403454111)
XLA Ops:
  0.7 5.4 %local_maxima.1 = (f32[16,1024]{1,0:T(8,128)S(1)}, f32[7,512,128]{2,1,0:T(8,128)}, f32[8,512,128]{2,1,0:T(8,128)}, f32[1,512,128]{2,1,0:T(8,128)S(1)}) custom-call(s32[1]{0:T(128)} %bitcast.f_ref, f32[16,1024,128]{2,1,0:T(8,128)} %w_ref.7), custom_call_target="tpu_custom_call" | custom-call | flops 50331648 | bytes 12582912 | tf_op jit(solution)/shard_map/local_maxima/pallas_call | solution.py:97
  6.1 0.8 collective-permute-start.10
  6.9 6.0 %collective-permute-start.1 = (f32[16,1024]{1,0:T(8,128)S(1)}, f32[16,1024]{1,0:T(8,128)S(1)}, u32[]{:S(2)}, u32[]{:S(2)}) collective-permute-start(f32[16,1024]{1,0:T(8,128)S(1)} %get-tuple-element.27), channel_id=1, source_target_pairs={{0,8},{1,9},{2,10},{3,11},{4,12},{5,13},{6,14},{7,15},{8,0},{9,1},... | collective-permute-start | bytes 196616 | tf_op jit(solution)/shard_map/ppermute | solution.py:48
  12.9 0.7 collective-permute-start.12
  13.7 1.3 collective-permute-done.1
  15.0 1.9 %collective-permute-start.2 = (f32[16,1024]{1,0:T(8,128)S(1)}, f32[16,1024]{1,0:T(8,128)S(1)}, u32[]{:S(2)}, u32[]{:S(2)}) collective-permute-start(f32[16,1024]{1,0:T(8,128)S(1)} %max.15), channel_id=1, source_target_pairs={{0,1},{1,0},{2,3},{3,2},{4,5},{5,4},{6,7},{7,6},{8,9},{9,8},{10,11... | collective-permute-start | bytes 196616 | tf_op jit(solution)/shard_map/ppermute | solution.py:48
  16.9 0.9 constant_dynamic-slice_fusion.1
  17.9 1.2 collective-permute-start.5
  19.1 2.7 %collective-permute-start.3 = (f32[16,1024]{1,0:T(8,128)S(1)}, f32[16,1024]{1,0:T(8,128)S(1)}, u32[]{:S(2)}, u32[]{:S(2)}) collective-permute-start(f32[16,1024]{1,0:T(8,128)S(1)} %max.16), channel_id=1, source_target_pairs={{0,2},{1,3},{2,4},{3,5},{4,6},{5,7},{6,0},{7,1},{8,10},{9,11},{10,... | collective-permute-start | bytes 196616 | tf_op jit(solution)/shard_map/ppermute | solution.py:48
  21.8 0.8 collective-permute-done.5
  22.6 6.1 %collective-permute-start.13 = (f32[528,128]{1,0:T(8,128)S(1)}, f32[528,128]{1,0:T(8,128)S(1)}, u32[]{:S(2)}, u32[]{:S(2)}) collective-permute-start(f32[528,128]{1,0:T(8,128)S(1)} %pad_maximum_fusion), channel_id=1, source_target_pairs={{0,8},{1,9},{2,10},{3,11},{4,12},{5,13},{6,14},{7,15},{8,0},{9,1},... | collective-permute-start | bytes 811016 | tf_op jit(solution)/shard_map/ppermute | solution.py:48
  28.7 2.7 %far_pieces.3 = bf16[14,256,128]{2,1,0:T(8,128)(2,1)} custom-call(s32[1]{0:T(128)} %bitcast.f_ref, f32[16,1024,128]{2,1,0:T(8,128)} %w_ref.7, f32[7,512,128]{2,1,0:T(8,128)} %collective-permute-done.10.theirs_ref.refs_4_, f32[16,1024]{1,0:T(8,128)S(1)} %maximum_maximum_fusion.scale_ref), custom_call_target="tpu_custom_call" | custom-call | flops 12582912 | bytes 3145728 | tf_op jit(solution)/shard_map/far_pieces/pallas_call | solution.py:155
  31.4 2.2 %collective-permute-start.11 = (bf16[14,256,128]{2,1,0:T(8,128)(2,1)}, bf16[14,256,128]{2,1,0:T(8,128)(2,1)S(1)}, u32[]{:S(2)}, u32[]{:S(2)}) collective-permute-start(bf16[14,256,128]{2,1,0:T(8,128)(2,1)} %far_pieces.3), channel_id=1, source_target_pairs={{0,8},{1,9},{2,10},{3,11},{4,12},{5,13},{6,14},{7,15},{8,0},{9,1},... | collective-permute-start | bytes 2752520 | tf_op jit(solution)/shard_map/ppermute | solution.py:48
  33.6 13.0 %collective-permute-done.13.relay_ref = f32[528,128]{1,0:T(8,128)S(1)} collective-permute-done((f32[528,128]{1,0:T(8,128)S(1)}, f32[528,128]{1,0:T(8,128)S(1)}, u32[]{:S(2)}, u32[]{:S(2)}) %collective-permute-start.13) | collective-permute-done | bytes 270368 | tf_op jit(solution)/shard_map/ppermute | solution.py:48
  46.6 0.7 copy-done.2
  47.3 5.4 %collective-permute-start.14 = (bf16[2,16,128]{2,1,0:T(8,128)(2,1)S(1)}, bf16[2,16,128]{2,1,0:T(8,128)(2,1)S(1)}, u32[]{:S(2)}, u32[]{:S(2)}) collective-permute-start(bf16[2,16,128]{2,1,0:T(8,128)(2,1)S(1)} %pad_maximum_fusion.2), channel_id=1, source_target_pairs={{0,1},{1,0},{2,3},{3,2},{4,5},{5,4},{6,7},{7,6},{8,9},{9,8},{10,11... | collective-permute-start | bytes 24584 | tf_op jit(solution)/shard_map/ppermute | solution.py:48
  52.7 0.8 collective-permute-done.14
  53.5 1.0 collective-permute-start.15
  54.9 0.9 collective-permute-start.17
  56.4 2.5 %collective-permute-done.16.refs_2_ = bf16[4,16,128]{2,1,0:T(8,128)(2,1)S(1)} collective-permute-done((bf16[4,16,128]{2,1,0:T(8,128)(2,1)S(1)}, bf16[4,16,128]{2,1,0:T(8,128)(2,1)S(1)}, u32[]{:S(2)}, u32[]{:S(2)}) %collective-permute-start.16) | collective-permute-done | bytes 16416 | tf_op jit(solution)/shard_map/ppermute | solution.py:357
  58.9 1.4 copy-done
  60.3 1.0 copy-done.3
  61.2 4.0 %near_pieces.1 = (bf16[38,64,128]{2,1,0:T(8,128)(2,1)S(1)}, bf16[38,64,128]{2,1,0:T(8,128)(2,1)S(1)}, bf16[38,64,128]{2,1,0:T(8,128)(2,1)S(1)}, bf16[16,64,2048]{2,1,0:T(8,128)(2,1)}, bf16[64,2048]{1,0:T(8,128)(2,1)}) custom-call(s32[1]{0:T(128)} %bitcast.f_ref, s32[1]{0:T(128)} %bitcast.1.y_ref, f32[16,1024,128]{2,1,0:T(8,128)} %w_ref.7, ...), custom_call_target="tpu_custom_call" | custom-call | flops 33554432 | bytes 8388608 | tf_op jit(solution)/shard_map/near_pieces/pallas_call | solution.py:237
  65.5 2.1 %collective-permute-start.19 = (bf16[38,64,128]{2,1,0:T(8,128)(2,1)S(1)}, bf16[38,64,128]{2,1,0:T(8,128)(2,1)S(1)}, u32[]{:S(2)}, u32[]{:S(2)}) collective-permute-start(bf16[38,64,128]{2,1,0:T(8,128)(2,1)S(1)} %get-tuple-element.35), channel_id=1, source_target_pairs={{0,4},{1,5},{2,6},{3,7},{4,0},{5,1},{6,2},{7,3},{8,12},{9,13},{10,... | collective-permute-start | bytes 1867784 | tf_op jit(solution)/shard_map/ppermute | solution.py:48
  67.6 11.8 %collective-permute-done.20.piece_ref = bf16[38,64,128]{2,1,0:T(8,128)(2,1)S(1)} collective-permute-done((bf16[38,64,128]{2,1,0:T(8,128)(2,1)S(1)}, bf16[38,64,128]{2,1,0:T(8,128)(2,1)S(1)}, u32[]{:S(2)}, u32[]{:S(2)}) %collective-permute-start.20) | collective-permute-done | bytes 622624 | tf_op jit(solution)/shard_map/ppermute | solution.py:48
  79.4 0.9 place_near.3
  80.9 0.9 place_near.4
  81.7 14.5 %collective-permute-done.18.piece_ref = bf16[38,64,128]{2,1,0:T(8,128)(2,1)S(1)} collective-permute-done((bf16[38,64,128]{2,1,0:T(8,128)(2,1)S(1)}, bf16[38,64,128]{2,1,0:T(8,128)(2,1)S(1)}, u32[]{:S(2)}, u32[]{:S(2)}) %collective-permute-start.18) | collective-permute-done | bytes 622624 | tf_op jit(solution)/shard_map/ppermute | solution.py:48
  96.3 0.9 place_near.5
  97.2 0.9 split.1
  98.1 0.9 collective-permute-start.22
  99.2 2.2 %far_pieces.2 = (bf16[16,64,128]{2,1,0:T(8,128)(2,1)S(1)}, bf16[16,64,128]{2,1,0:T(8,128)(2,1)S(1)}, bf16[16,64,128]{2,1,0:T(8,128)(2,1)S(1)}, bf16[16,64,128]{2,1,0:T(8,128)(2,1)S(1)}) custom-call(s32[1]{0:T(128)} %bitcast.f_ref, f32[16,1024,128]{2,1,0:T(8,128)} %w_ref.7, f32[8,512,128]{2,1,0:T(8,128)S(1)} %copy-done.1, ...), custom_call_target="tpu_custom_call" | custom-call | flops 12582912 | bytes 3145728 | tf_op jit(solution)/shard_map/far_pieces/pallas_call | solution.py:155
  101.3 5.1 %collective-permute-start.9 = (bf16[16,64,128]{2,1,0:T(8,128)(2,1)S(1)}, bf16[16,64,128]{2,1,0:T(8,128)(2,1)S(1)}, u32[]{:S(2)}, u32[]{:S(2)}) collective-permute-start(bf16[16,64,128]{2,1,0:T(8,128)(2,1)S(1)} %get-tuple-element.31), channel_id=1, source_target_pairs={{0,8},{1,9},{2,10},{3,11},{4,12},{5,13},{6,14},{7,15},{8,0},{9,1},... | collective-permute-start | bytes 786440 | tf_op jit(solution)/shard_map/ppermute | solution.py:48
  106.5 2.3 %collective-permute-start.8 = (bf16[16,64,128]{2,1,0:T(8,128)(2,1)S(1)}, bf16[16,64,128]{2,1,0:T(8,128)(2,1)S(1)}, u32[]{:S(2)}, u32[]{:S(2)}) collective-permute-start(bf16[16,64,128]{2,1,0:T(8,128)(2,1)S(1)} %get-tuple-element.30), channel_id=1, source_target_pairs={{0,10},{1,11},{2,12},{3,13},{4,14},{5,15},{6,8},{7,9},{8,2},{9,3},... | collective-permute-start | bytes 786440 | tf_op jit(solution)/shard_map/ppermute | solution.py:48
  108.7 5.6 %collective-permute-start.7 = (bf16[16,64,128]{2,1,0:T(8,128)(2,1)S(1)}, bf16[16,64,128]{2,1,0:T(8,128)(2,1)S(1)}, u32[]{:S(2)}, u32[]{:S(2)}) collective-permute-start(bf16[16,64,128]{2,1,0:T(8,128)(2,1)S(1)} %get-tuple-element.29), channel_id=1, source_target_pairs={{0,12},{1,13},{2,14},{3,15},{4,8},{5,9},{6,10},{7,11},{8,4},{9,5},... | collective-permute-start | bytes 786440 | tf_op jit(solution)/shard_map/ppermute | solution.py:48
  114.3 1.9 %collective-permute-start.21 = (bf16[14,64,128]{2,1,0:T(8,128)(2,1)S(1)}, bf16[14,64,128]{2,1,0:T(8,128)(2,1)S(1)}, u32[]{:S(2)}, u32[]{:S(2)}) collective-permute-start(bf16[14,64,128]{2,1,0:T(8,128)(2,1)S(1)} %get-tuple-element.44), channel_id=1, source_target_pairs={{0,6},{1,7},{2,0},{3,1},{4,2},{5,3},{6,4},{7,5},{8,14},{9,15},{10,... | collective-permute-start | bytes 688136 | tf_op jit(solution)/shard_map/ppermute | solution.py:48
  116.9 0.7 place_far.7._
  117.6 0.7 place_far.8._
  118.3 2.4 %collective-permute-done.21.piece_ref = bf16[14,64,128]{2,1,0:T(8,128)(2,1)S(1)} collective-permute-done((bf16[14,64,128]{2,1,0:T(8,128)(2,1)S(1)}, bf16[14,64,128]{2,1,0:T(8,128)(2,1)S(1)}, u32[]{:S(2)}, u32[]{:S(2)}) %collective-permute-start.21) | collective-permute-done | bytes 229408 | tf_op jit(solution)/shard_map/ppermute | solution.py:48
  120.8 0.7 place_far.9._
  121.5 4.3 %collective-permute-done.9.piece_ref = bf16[16,64,128]{2,1,0:T(8,128)(2,1)S(1)} collective-permute-done((bf16[16,64,128]{2,1,0:T(8,128)(2,1)S(1)}, bf16[16,64,128]{2,1,0:T(8,128)(2,1)S(1)}, u32[]{:S(2)}, u32[]{:S(2)}) %collective-permute-start.9) | collective-permute-done | bytes 262176 | tf_op jit(solution)/shard_map/ppermute | solution.py:48
  125.8 0.7 place_far.10._
  126.5 4.5 %collective-permute-done.8.piece_ref = bf16[16,64,128]{2,1,0:T(8,128)(2,1)S(1)} collective-permute-done((bf16[16,64,128]{2,1,0:T(8,128)(2,1)S(1)}, bf16[16,64,128]{2,1,0:T(8,128)(2,1)S(1)}, u32[]{:S(2)}, u32[]{:S(2)}) %collective-permute-start.8) | collective-permute-done | bytes 262176 | tf_op jit(solution)/shard_map/ppermute | solution.py:48
  131.0 0.7 place_far.11._
  131.7 5.6 %collective-permute-done.7.piece_ref = bf16[16,64,128]{2,1,0:T(8,128)(2,1)S(1)} collective-permute-done((bf16[16,64,128]{2,1,0:T(8,128)(2,1)S(1)}, bf16[16,64,128]{2,1,0:T(8,128)(2,1)S(1)}, u32[]{:S(2)}, u32[]{:S(2)}) %collective-permute-start.7) | collective-permute-done | bytes 262176 | tf_op jit(solution)/shard_map/ppermute | solution.py:48
  137.4 0.7 place_far.12._
  138.1 4.8 %collective-permute-done.6.piece_ref = bf16[16,64,128]{2,1,0:T(8,128)(2,1)S(1)} collective-permute-done((bf16[16,64,128]{2,1,0:T(8,128)(2,1)S(1)}, bf16[16,64,128]{2,1,0:T(8,128)(2,1)S(1)}, u32[]{:S(2)}, u32[]{:S(2)}) %collective-permute-start.6) | collective-permute-done | bytes 262176 | tf_op jit(solution)/shard_map/ppermute | solution.py:48
  142.9 0.7 place_far.13
  (38 shorter events, 2.9 us)
Async XLA Ops:
  0.6 13.0 %copy-start.4 = (f32[128,16]{0,1:T(8,128)S(1)}, f32[128,16]{0,1:T(8,128)}, u32[]{:S(2)}) copy-start(f32[128,16]{0,1:T(8,128)} %param.4) | copy-start | bytes 24580
  0.6 13.0 %copy-start.5 = (f32[128]{0:T(128)S(1)}, f32[128]{0:T(128)}, u32[]{:S(2)}) copy-start(f32[128]{0:T(128)} %param.5) | copy-start | bytes 1540
  6.1 22.6 %collective-permute-start.10 = (f32[7,512,128]{2,1,0:T(8,128)}, f32[7,512,128]{2,1,0:T(8,128)}, u32[]{:S(2)}, u32[]{:S(2)}) collective-permute-start(f32[7,512,128]{2,1,0:T(8,128)} %get-tuple-element.32), channel_id=1, source_target_pairs={{0,1},{1,0},{2,3},{3,2},{4,5},{5,4},{6,7},{7,6},{8,9},{9,8},{10,11... | collective-permute-start | bytes 5505032 | tf_op jit(solution)/shard_map/ppermute | solution.py:48
  6.8 52.1 %collective-permute-start = (f32[8,512,128]{2,1,0:T(8,128)}, f32[8,512,128]{2,1,0:T(8,128)S(1)}, u32[]{:S(2)}, u32[]{:S(2)}) collective-permute-start(f32[8,512,128]{2,1,0:T(8,128)} %get-tuple-element.26), channel_id=1, source_target_pairs={{0,1},{1,0},{2,3},{3,2},{4,5},{5,4},{6,7},{7,6},{8,9},{9,8},{10,11... | collective-permute-start | bytes 6291464 | tf_op jit(solution)/shard_map/ppermute | solution.py:48
  6.9 8.1 %collective-permute-start.1 = (f32[16,1024]{1,0:T(8,128)S(1)}, f32[16,1024]{1,0:T(8,128)S(1)}, u32[]{:S(2)}, u32[]{:S(2)}) collective-permute-start(f32[16,1024]{1,0:T(8,128)S(1)} %get-tuple-element.27), channel_id=1, source_target_pairs={{0,8},{1,9},{2,10},{3,11},{4,12},{5,13},{6,14},{7,15},{8,0},{9,1},... | collective-permute-start | bytes 196616 | tf_op jit(solution)/shard_map/ppermute | solution.py:48
  12.9 6.2 %collective-permute-start.12 = (f32[1,512,128]{2,1,0:T(8,128)S(1)}, f32[1,512,128]{2,1,0:T(8,128)S(1)}, u32[]{:S(2)}, u32[]{:S(2)}) collective-permute-start(f32[1,512,128]{2,1,0:T(8,128)S(1)} %get-tuple-element.33), channel_id=1, source_target_pairs={{0,1},{1,0},{2,3},{3,2},{4,5},{5,4},{6,7},{7,6},{8,9},{9,8},{10,11... | collective-permute-start | bytes 786440 | tf_op jit(solution)/shard_map/ppermute | solution.py:48
  15.0 2.9 %collective-permute-start.2 = (f32[16,1024]{1,0:T(8,128)S(1)}, f32[16,1024]{1,0:T(8,128)S(1)}, u32[]{:S(2)}, u32[]{:S(2)}) collective-permute-start(f32[16,1024]{1,0:T(8,128)S(1)} %max.15), channel_id=1, source_target_pairs={{0,1},{1,0},{2,3},{3,2},{4,5},{5,4},{6,7},{7,6},{8,9},{9,8},{10,11... | collective-permute-start | bytes 196616 | tf_op jit(solution)/shard_map/ppermute | solution.py:48
  17.9 4.7 %collective-permute-start.5 = (f32[16,1024]{1,0:T(8,128)S(1)}, f32[16,1024]{1,0:T(8,128)S(1)}, u32[]{:S(2)}, u32[]{:S(2)}) collective-permute-start(f32[16,1024]{1,0:T(8,128)S(1)} %max.16), channel_id=1, source_target_pairs={{0,4},{1,5},{2,6},{3,7},{4,0},{5,1},{6,2},{7,3},{8,12},{9,13},{10,... | collective-permute-start | bytes 196616 | tf_op jit(solution)/shard_map/ppermute | solution.py:48
  19.1 9.6 %collective-permute-start.4 = (f32[16,1024]{1,0:T(8,128)S(1)}, f32[16,1024]{1,0:T(8,128)S(1)}, u32[]{:S(2)}, u32[]{:S(2)}) collective-permute-start(f32[16,1024]{1,0:T(8,128)S(1)} %max.16), channel_id=1, source_target_pairs={{0,6},{1,7},{2,0},{3,1},{4,2},{5,3},{6,4},{7,5},{8,14},{9,15},{10,... | collective-permute-start | bytes 196616 | tf_op jit(solution)/shard_map/ppermute | solution.py:48
  19.1 9.6 %collective-permute-start.3 = (f32[16,1024]{1,0:T(8,128)S(1)}, f32[16,1024]{1,0:T(8,128)S(1)}, u32[]{:S(2)}, u32[]{:S(2)}) collective-permute-start(f32[16,1024]{1,0:T(8,128)S(1)} %max.16), channel_id=1, source_target_pairs={{0,2},{1,3},{2,4},{3,5},{4,6},{5,7},{6,0},{7,1},{8,10},{9,11},{10,... | collective-permute-start | bytes 196616 | tf_op jit(solution)/shard_map/ppermute | solution.py:48
  22.6 24.0 %collective-permute-start.13 = (f32[528,128]{1,0:T(8,128)S(1)}, f32[528,128]{1,0:T(8,128)S(1)}, u32[]{:S(2)}, u32[]{:S(2)}) collective-permute-start(f32[528,128]{1,0:T(8,128)S(1)} %pad_maximum_fusion), channel_id=1, source_target_pairs={{0,8},{1,9},{2,10},{3,11},{4,12},{5,13},{6,14},{7,15},{8,0},{9,1},... | collective-permute-start | bytes 811016 | tf_op jit(solution)/shard_map/ppermute | solution.py:48
  31.4 65.8 %collective-permute-start.11 = (bf16[14,256,128]{2,1,0:T(8,128)(2,1)}, bf16[14,256,128]{2,1,0:T(8,128)(2,1)S(1)}, u32[]{:S(2)}, u32[]{:S(2)}) collective-permute-start(bf16[14,256,128]{2,1,0:T(8,128)(2,1)} %far_pieces.3), channel_id=1, source_target_pairs={{0,8},{1,9},{2,10},{3,11},{4,12},{5,13},{6,14},{7,15},{8,0},{9,1},... | collective-permute-start | bytes 2752520 | tf_op jit(solution)/shard_map/ppermute | solution.py:48
  46.6 0.7 copy-start.2
  47.3 6.2 %collective-permute-start.14 = (bf16[2,16,128]{2,1,0:T(8,128)(2,1)S(1)}, bf16[2,16,128]{2,1,0:T(8,128)(2,1)S(1)}, u32[]{:S(2)}, u32[]{:S(2)}) collective-permute-start(bf16[2,16,128]{2,1,0:T(8,128)(2,1)S(1)} %pad_maximum_fusion.2), channel_id=1, source_target_pairs={{0,1},{1,0},{2,3},{3,2},{4,5},{5,4},{6,7},{7,6},{8,9},{9,8},{10,11... | collective-permute-start | bytes 24584 | tf_op jit(solution)/shard_map/ppermute | solution.py:48
  53.5 2.9 %collective-permute-start.15 = (bf16[4,16,128]{2,1,0:T(8,128)(2,1)S(1)}, bf16[4,16,128]{2,1,0:T(8,128)(2,1)S(1)}, u32[]{:S(2)}, u32[]{:S(2)}) collective-permute-start(bf16[4,16,128]{2,1,0:T(8,128)(2,1)S(1)} %pad_maximum_fusion.1.refs_0_), channel_id=1, source_target_pairs={{0,16},{16,32},{32,48},{48,0},{1,17},{17,33},{33,49},{49,1},{2,18}... | collective-permute-start | bytes 49160 | tf_op jit(solution)/shard_map/ppermute | solution.py:357
  54.5 4.4 %collective-permute-start.16 = (bf16[4,16,128]{2,1,0:T(8,128)(2,1)S(1)}, bf16[4,16,128]{2,1,0:T(8,128)(2,1)S(1)}, u32[]{:S(2)}, u32[]{:S(2)}) collective-permute-start(bf16[4,16,128]{2,1,0:T(8,128)(2,1)S(1)} %pad_maximum_fusion.1.refs_0_), channel_id=1, source_target_pairs={{0,32},{16,48},{32,0},{48,16},{1,33},{17,49},{33,1},{49,17},{2,34}... | collective-permute-start | bytes 49160 | tf_op jit(solution)/shard_map/ppermute | solution.py:357
  54.9 4.0 %collective-permute-start.17 = (bf16[4,16,128]{2,1,0:T(8,128)(2,1)S(1)}, bf16[4,16,128]{2,1,0:T(8,128)(2,1)S(1)}, u32[]{:S(2)}, u32[]{:S(2)}) collective-permute-start(bf16[4,16,128]{2,1,0:T(8,128)(2,1)S(1)} %pad_maximum_fusion.1.refs_0_), channel_id=1, source_target_pairs={{0,48},{16,0},{32,16},{48,32},{1,49},{17,1},{33,17},{49,33},{2,50}... | collective-permute-start | bytes 49160 | tf_op jit(solution)/shard_map/ppermute | solution.py:357
  58.9 1.4 copy-start
  60.3 1.0 copy-start.3
  65.2 14.2 %collective-permute-start.20 = (bf16[38,64,128]{2,1,0:T(8,128)(2,1)S(1)}, bf16[38,64,128]{2,1,0:T(8,128)(2,1)S(1)}, u32[]{:S(2)}, u32[]{:S(2)}) collective-permute-start(bf16[38,64,128]{2,1,0:T(8,128)(2,1)S(1)} %get-tuple-element.36), channel_id=1, source_target_pairs={{0,2},{1,3},{2,4},{3,5},{4,6},{5,7},{6,0},{7,1},{8,10},{9,11},{10,... | collective-permute-start | bytes 1867784 | tf_op jit(solution)/shard_map/ppermute | solution.py:48
  65.5 15.4 %collective-permute-start.19 = (bf16[38,64,128]{2,1,0:T(8,128)(2,1)S(1)}, bf16[38,64,128]{2,1,0:T(8,128)(2,1)S(1)}, u32[]{:S(2)}, u32[]{:S(2)}) collective-permute-start(bf16[38,64,128]{2,1,0:T(8,128)(2,1)S(1)} %get-tuple-element.35), channel_id=1, source_target_pairs={{0,4},{1,5},{2,6},{3,7},{4,0},{5,1},{6,2},{7,3},{8,12},{9,13},{10,... | collective-permute-start | bytes 1867784 | tf_op jit(solution)/shard_map/ppermute | solution.py:48
  67.6 28.7 %collective-permute-start.18 = (bf16[38,64,128]{2,1,0:T(8,128)(2,1)S(1)}, bf16[38,64,128]{2,1,0:T(8,128)(2,1)S(1)}, u32[]{:S(2)}, u32[]{:S(2)}) collective-permute-start(bf16[38,64,128]{2,1,0:T(8,128)(2,1)S(1)} %get-tuple-element.34), channel_id=1, source_target_pairs={{0,6},{1,7},{2,0},{3,1},{4,2},{5,3},{6,4},{7,5},{8,14},{9,15},{10,... | collective-permute-start | bytes 1867784 | tf_op jit(solution)/shard_map/ppermute | solution.py:48
  96.3 2.9 %copy-start.1 = (f32[8,512,128]{2,1,0:T(8,128)S(1)}, f32[8,512,128]{2,1,0:T(8,128)}, u32[]{:S(2)}) copy-start(f32[8,512,128]{2,1,0:T(8,128)} %copy-done) | copy-start | bytes 6291460
  98.1 16.2 %collective-permute-start.22 = (bf16[14,64,128]{2,1,0:T(8,128)(2,1)S(1)}, bf16[14,64,128]{2,1,0:T(8,128)(2,1)S(1)}, u32[]{:S(2)}, u32[]{:S(2)}) collective-permute-start(bf16[14,64,128]{2,1,0:T(8,128)(2,1)S(1)} %get-tuple-element.45), channel_id=1, source_target_pairs={{0,4},{1,5},{2,6},{3,7},{4,0},{5,1},{6,2},{7,3},{8,12},{9,13},{10,... | collective-permute-start | bytes 688136 | tf_op jit(solution)/shard_map/ppermute | solution.py:48
  98.9 15.4 %collective-permute-start.23 = (bf16[14,64,128]{2,1,0:T(8,128)(2,1)S(1)}, bf16[14,64,128]{2,1,0:T(8,128)(2,1)S(1)}, u32[]{:S(2)}, u32[]{:S(2)}) collective-permute-start(bf16[14,64,128]{2,1,0:T(8,128)(2,1)S(1)} %get-tuple-element.46), channel_id=1, source_target_pairs={{0,2},{1,3},{2,4},{3,5},{4,6},{5,7},{6,0},{7,1},{8,10},{9,11},{10,... | collective-permute-start | bytes 688136 | tf_op jit(solution)/shard_map/ppermute | solution.py:48
  101.3 24.4 %collective-permute-start.9 = (bf16[16,64,128]{2,1,0:T(8,128)(2,1)S(1)}, bf16[16,64,128]{2,1,0:T(8,128)(2,1)S(1)}, u32[]{:S(2)}, u32[]{:S(2)}) collective-permute-start(bf16[16,64,128]{2,1,0:T(8,128)(2,1)S(1)} %get-tuple-element.31), channel_id=1, source_target_pairs={{0,8},{1,9},{2,10},{3,11},{4,12},{5,13},{6,14},{7,15},{8,0},{9,1},... | collective-permute-start | bytes 786440 | tf_op jit(solution)/shard_map/ppermute | solution.py:48
  106.5 24.6 %collective-permute-start.8 = (bf16[16,64,128]{2,1,0:T(8,128)(2,1)S(1)}, bf16[16,64,128]{2,1,0:T(8,128)(2,1)S(1)}, u32[]{:S(2)}, u32[]{:S(2)}) collective-permute-start(bf16[16,64,128]{2,1,0:T(8,128)(2,1)S(1)} %get-tuple-element.30), channel_id=1, source_target_pairs={{0,10},{1,11},{2,12},{3,13},{4,14},{5,15},{6,8},{7,9},{8,2},{9,3},... | collective-permute-start | bytes 786440 | tf_op jit(solution)/shard_map/ppermute | solution.py:48
  108.7 28.6 %collective-permute-start.7 = (bf16[16,64,128]{2,1,0:T(8,128)(2,1)S(1)}, bf16[16,64,128]{2,1,0:T(8,128)(2,1)S(1)}, u32[]{:S(2)}, u32[]{:S(2)}) collective-permute-start(bf16[16,64,128]{2,1,0:T(8,128)(2,1)S(1)} %get-tuple-element.29), channel_id=1, source_target_pairs={{0,12},{1,13},{2,14},{3,15},{4,8},{5,9},{6,10},{7,11},{8,4},{9,5},... | collective-permute-start | bytes 786440 | tf_op jit(solution)/shard_map/ppermute | solution.py:48
  114.3 28.6 %collective-permute-start.6 = (bf16[16,64,128]{2,1,0:T(8,128)(2,1)S(1)}, bf16[16,64,128]{2,1,0:T(8,128)(2,1)S(1)}, u32[]{:S(2)}, u32[]{:S(2)}) collective-permute-start(bf16[16,64,128]{2,1,0:T(8,128)(2,1)S(1)} %get-tuple-element.28), channel_id=1, source_target_pairs={{0,14},{1,15},{2,8},{3,9},{4,10},{5,11},{6,12},{7,13},{8,6},{9,7},... | collective-permute-start | bytes 786440 | tf_op jit(solution)/shard_map/ppermute | solution.py:48
  114.3 6.5 %collective-permute-start.21 = (bf16[14,64,128]{2,1,0:T(8,128)(2,1)S(1)}, bf16[14,64,128]{2,1,0:T(8,128)(2,1)S(1)}, u32[]{:S(2)}, u32[]{:S(2)}) collective-permute-start(bf16[14,64,128]{2,1,0:T(8,128)(2,1)S(1)} %get-tuple-element.44), channel_id=1, source_target_pairs={{0,6},{1,7},{2,0},{3,1},{4,2},{5,3},{6,4},{7,5},{8,14},{9,15},{10,... | collective-permute-start | bytes 688136 | tf_op jit(solution)/shard_map/ppermute | solution.py:48

commit v4 on v3

--- a/solution.py
+++ b/solution.py
@@ -8,7 +8,7 @@
 from jax.sharding import PartitionSpec as P
 
 
-RELAY = 7
+RELAY = 4
 EARLY = 1
 BF16, F32 = jnp.bfloat16, jnp.float32
 ANY = pl.BlockSpec(memory_space=pl.ANY)
@@ -65,7 +65,7 @@
 
 
 def local_kernel(f_ref, w_ref, out_ref, *refs):
-    swap_refs, (taken, in_sems, out_sems) = refs[:3], refs[3:]
+    swap_refs, (taken, in_sems, out_sems) = refs[:2], refs[2:]
     blocks, experts = taken.shape[:2]
     away = 1 - f_ref[0] % 2
     reads = []
@@ -76,10 +76,10 @@
     writes = []
     for b in range(blocks):
         reads[b].wait()
-        for k, ((first, count), target) in enumerate(zip(parts(experts), swap_refs)):
+        for k, ((first, count), target) in enumerate(zip(parts(experts)[::2], swap_refs)):
             rows = taken.at[b, pl.ds(first, count), span(64 * away, 64), :]
             writes.append(
-                pltpu.make_async_copy(rows, target.at[:, pl.ds(64 * b, 64), :], out_sems.at[3 * b + k])
+                pltpu.make_async_copy(rows, target.at[:, pl.ds(64 * b, 64), :], out_sems.at[2 * b + k])
             )
             writes[-1].start()
         total = jnp.zeros((128, 128), F32)
@@ -98,18 +98,53 @@
         local_kernel,
         out_shape=[
             array(experts, rows, kind=F32),
-            *(array(count, rows // 2, 128, kind=F32) for _, count in parts(experts)),
+            *(array(count, rows // 2, 128, kind=F32) for _, count in parts(experts)[::2]),
         ],
         in_specs=[SMEM, ANY],
-        out_specs=[VMEM, ANY, ANY, ANY],
+        out_specs=[VMEM, ANY, ANY],
         scratch_shapes=[
             pltpu.VMEM((blocks, experts, 128, 128), F32),
             pltpu.SemaphoreType.DMA((blocks,)),
-            pltpu.SemaphoreType.DMA((3 * blocks,)),
+            pltpu.SemaphoreType.DMA((2 * blocks,)),
         ],
-        compiler_params=params(50),
+        compiler_params=params(46),
         cost_estimate=cost(8 * 2**20, 4 * 2**20),
         name="local_maxima",
+    )(f, w)
+
+
+def swap_kernel(first, f_ref, w_ref, out_ref, taken, in_sems, out_sems):
+    blocks, count = taken.shape[:2]
+    away = 1 - f_ref[0] % 2
+    reads, writes = [], []
+    for b in range(blocks):
+        rows = w_ref.at[pl.ds(first, count), span(128 * b + 64 * away, 64), :]
+        reads.append(pltpu.make_async_copy(rows, taken.at[b], in_sems.at[b]))
+        reads[-1].start()
+    for b in range(blocks):
+        reads[b].wait()
+        writes.append(pltpu.make_async_copy(taken.at[b], out_ref.at[:, pl.ds(64 * b, 64), :], out_sems.at[b]))
+        writes[-1].start()
+    for write in writes:
+        write.wait()
+
+
+def swap_rows(f, w, first, count):
+    rows = w.shape[1]
+    blocks = rows // 128
+    return pl.pallas_call(
+        functools.partial(swap_kernel, first),
+        out_shape=array(count, rows // 2, 128, kind=F32),
+        in_specs=[SMEM, ANY],
+        out_specs=ANY,
+        scratch_shapes=[
+            pltpu.VMEM((blocks, count, 64, 128), F32),
+            pltpu.SemaphoreType.DMA((blocks,)),
+            pltpu.SemaphoreType.DMA((blocks,)),
+        ],
+        compiler_params=params(46),
+        cost_estimate=cost(3 * 2**20, 3 * 2**20),
+        name="swap_rows",
     )(f, w)
 
 
@@ -164,18 +199,18 @@
             pltpu.SemaphoreType.DMA((8,)),
             pltpu.SemaphoreType.DMA((4,)),
         ],
-        compiler_params=params(50),
+        compiler_params=params(46),
         cost_estimate=cost(2 * 2**20, 2**20),
         name="far_pieces",
     )(f, w, theirs, scale)
 
 
-def near_kernel(f_ref, y_ref, w_ref, scale_ref, relay_ref, *refs):
-    rows_refs, theirs_refs, refs = refs[:4], refs[4:7], refs[7:]
-    outs, (final_ref, router_ref), (taken, inverse, made, in_sems, out_sems) = refs[:3], refs[3:5], refs[5:]
+def near_kernel(f_ref, w_ref, scale_ref, relay_ref, *refs):
+    theirs_refs, outs, final_ref, refs = refs[:3], refs[3:6], refs[6], refs[7:]
+    taken, relay, inverse, made, in_sems, out_sems = refs
     experts = w_ref.shape[0]
     late = experts - EARLY
-    f, y = f_ref[0], y_ref[0]
+    f = f_ref[0]
     core = f % 2
     reads = []
     for dx in range(4):
@@ -187,7 +222,10 @@
         for k, (piece, at, size) in enumerate(rows):
             reads.append(pltpu.make_async_copy(piece, taken.at[dx, pl.ds(at, size)], in_sems.at[4 * dx + k]))
             reads[-1].start()
-    for dx in range(4):
+    relayed = pltpu.make_async_copy(relay_ref, relay, in_sems.at[16])
+    relayed.start()
+    writes = []
+    for dx in (1, 2, 3, 0):
         q = chip(f, 0, dx)
         inverse_columns(scale_ref, inverse, dx, q)
         columns = inverse[span(128 * dx + 64 * core, 64), :]
@@ -197,70 +235,90 @@
             for e in range(experts):
                 at = k * experts + e
                 made[dx, at] = (taken[dx, at] * columns[:, e : e + 1]).astype(BF16)
+        if dx == 1:
+            relayed.wait()
+        for k in range(2):
             for j in range(EARLY):
-                rows = relay_ref[span(256 * (k * EARLY + j) + 64 * (q % 4), 64), :]
+                rows = relay[span(256 * (k * EARLY + j) + 64 * (q % 4), 64), :]
                 lane = late + j
                 made[dx, 2 * experts + k * EARLY + j] = (rows * columns[:, lane : lane + 1]).astype(BF16)
-        for k in range(4):
-            for dy, piece in enumerate(rows_refs):
-                made[dx, 2 * experts + 2 * EARLY + k, span((y - dy + 4) % 4 * 16, 16), :] = piece[k]
-    copies = [pltpu.make_async_copy(made.at[dx], outs[dx - 1], out_sems.at[dx]) for dx in (1, 2, 3)]
-    copies += near_copies(f, f // 2, made.at[0], final_ref, router_ref, out_sems, 4)
-    run(copies)
-
-
-def near_copies(f, source, piece, final_ref, router_ref, sems, at):
+        if dx:
+            copies = [pltpu.make_async_copy(made.at[dx], outs[dx - 1], out_sems.at[dx])]
+        else:
+            copies = near_copies(f, f // 2, made.at[0], final_ref, out_sems, 4)
+        for copy in copies:
+            copy.start()
+        writes += copies
+    for write in writes:
+        write.wait()
+
+
+def near_copies(f, source, piece, final_ref, sems, at):
     experts = final_ref.shape[0]
-    core = f % 2
     across = (source + 4) % 8
-    early = pl.ds(experts - EARLY, EARLY)
     copies = []
     for k in range(2):
-        side = core if k == 0 else 1 - core
+        side = f % 2 if k == 0 else 1 - f % 2
         copies.append((piece.at[pl.ds(k * experts, experts)], final_ref.at[:, :, lanes(2 * source + side)]))
         copies.append(
             (
                 piece.at[pl.ds(2 * experts + k * EARLY, EARLY)],
-                final_ref.at[early, :, lanes(2 * across + side)],
+                final_ref.at[pl.ds(experts - EARLY, EARLY), :, lanes(2 * across + side)],
             )
         )
-        for j, q in enumerate((source, across)):
-            copies.append(
-                (piece.at[2 * experts + 2 * EARLY + 2 * k + j], router_ref.at[:, lanes(2 * q + side)])
-            )
     return [pltpu.make_async_copy(a, b, sems.at[at + k]) for k, (a, b) in enumerate(copies)]
 
 
-def near_pieces(f, y, w, scale, relay, rows, theirs):
+def near_pieces(f, w, scale, relay, theirs):
     experts = w.shape[0]
-    blocks = 2 * experts + 2 * EARLY + 4
+    blocks = 2 * experts + 2 * EARLY
     return pl.pallas_call(
         near_kernel,
-        out_shape=[array(blocks, 64, 128)] * 3 + [array(experts, 64, 2048), array(64, 2048)],
-        in_specs=[SMEM, SMEM, ANY] + [VMEM] * 6 + [ANY] * 3,
-        out_specs=[ANY] * 5,
+        out_shape=[array(blocks, 64, 128)] * 3 + [array(experts, 64, 2048)],
+        in_specs=[SMEM, ANY, VMEM] + [ANY] * 4,
+        out_specs=[ANY] * 4,
         scratch_shapes=[
             pltpu.VMEM((4, 2 * experts, 64, 128), F32),
+            pltpu.VMEM(relay.shape, F32),
             pltpu.VMEM((512, 128), F32),
             pltpu.VMEM((4, blocks, 64, 128), BF16),
-            pltpu.SemaphoreType.DMA((16,)),
-            pltpu.SemaphoreType.DMA((12,)),
+            pltpu.SemaphoreType.DMA((17,)),
+            pltpu.SemaphoreType.DMA((8,)),
         ],
-        compiler_params=params(50),
+        compiler_params=params(46),
         cost_estimate=cost(5 * 2**20, 3 * 2**20),
         name="near_pieces",
-    )(f, y, w, scale, relay, *rows, *theirs)
-
-
-def split_kernel(f_ref, chunk_ref, _, *refs):
-    outs, final_ref, sems = refs[:3], refs[3], refs[4]
-    f = f_ref[0]
+    )(f, w, scale, relay, *theirs)
+
+
+def split_kernel(f_ref, y_ref, chunk_ref, *refs):
+    rows_refs, outs, final_ref, router_ref, made, sems = refs[:4], refs[5:8], refs[8], refs[9], refs[10], refs[11]
+    f, y = f_ref[0], y_ref[0]
+    count = chunk_ref.shape[0]
     copies = []
     for dx in (1, 2, 3):
         rows = chunk_ref.at[:, span(64 * (chip(f, 0, dx) % 4), 64), :]
-        copies.append(pltpu.make_async_copy(rows, outs[dx - 1], sems.at[dx - 1]))
+        copies.append(pltpu.make_async_copy(rows, outs[dx - 1].at[pl.ds(0, count)], sems.at[dx]))
     rows = chunk_ref.at[:, span(64 * (chip(f, 0, 0) % 4), 64), :]
-    run(copies + far_copies(f, chip(f, 1, 0), 0, rows, final_ref, sems, 3))
+    copies += far_copies(f, chip(f, 1, 0), 0, rows, final_ref, sems, 4)
+    for copy in copies:
+        copy.start()
+    for k in range(4):
+        for dy, piece in enumerate(rows_refs):
+            made[k, span((y - dy + 4) % 4 * 16, 16), :] = piece[k]
+    more = [pltpu.make_async_copy(made, outs[dx - 1].at[pl.ds(count, 4)], sems.at[5 + dx]) for dx in (1, 2, 3)]
+    run(more + router_copies(f, f // 2, made, router_ref, sems, 9))
+    for copy in copies:
+        copy.wait()
+
+
+def router_copies(f, source, piece, router_ref, sems, at):
+    copies = []
+    for k in range(4):
+        side = f % 2 if k < 2 else 1 - f % 2
+        q = source if k % 2 == 0 else (source + 4) % 8
+        copies.append(pltpu.make_async_copy(piece.at[k], router_ref.at[:, lanes(2 * q + side)], sems.at[at + k]))
+    return copies
 
 
 def far_copies(f, source, first, piece, final_ref, sems, at):
@@ -273,18 +331,19 @@
     return copies
 
 
-def split(f, chunk, final):
+def split(f, y, chunk, rows, final):
+    count = chunk.shape[0]
     return pl.pallas_call(
         split_kernel,
-        out_shape=[array(chunk.shape[0], 64, 128)] * 3 + [array(*final.shape)],
-        in_specs=[SMEM, VMEM, ANY],
-        out_specs=[ANY] * 4,
-        scratch_shapes=[pltpu.SemaphoreType.DMA((5,))],
-        input_output_aliases={2: 3},
-        compiler_params=params(50),
+        out_shape=[array(count + 4, 64, 128)] * 3 + [array(*final.shape), array(64, 2048)],
+        in_specs=[SMEM, SMEM] + [VMEM] * 5 + [ANY],
+        out_specs=[ANY] * 5,
+        scratch_shapes=[pltpu.VMEM((4, 64, 128), BF16), pltpu.SemaphoreType.DMA((13,))],
+        input_output_aliases={7: 3},
+        compiler_params=params(46),
         cost_estimate=cost(2**20, 2**20),
         name="split",
-    )(f, chunk, final)
+    )(f, y, chunk, *rows, final)
 
 
 def place_far_kernel(dx, first, f_ref, piece_ref, _, final_ref, sems):
@@ -306,22 +365,43 @@
     )(f, piece, final)
 
 
-def place_near_kernel(dx, f_ref, piece_ref, _, __, final_ref, router_ref, sems):
+def place_near_kernel(dx, f_ref, piece_ref, _, final_ref, sems):
     f = f_ref[0]
-    run(near_copies(f, chip(f, 0, 4 - dx), piece_ref, final_ref, router_ref, sems, 0))
-
-
-def place_near(dx, f, piece, final, router):
+    run(near_copies(f, chip(f, 0, 4 - dx), piece_ref, final_ref, sems, 0))
+
+
+def place_near(dx, f, piece, final):
     return pl.pallas_call(
         functools.partial(place_near_kernel, dx),
+        out_shape=array(*final.shape),
+        in_specs=[SMEM, VMEM, ANY],
+        out_specs=ANY,
+        scratch_shapes=[pltpu.SemaphoreType.DMA((4,))],
+        input_output_aliases={2: 0},
+        compiler_params=params(2),
+        cost_estimate=cost(2**19, 2**19),
+        name="place_near",
+    )(f, piece, final)
+
+
+def place_relayed_kernel(dx, f_ref, piece_ref, _, __, final_ref, router_ref, sems):
+    f = f_ref[0]
+    count = piece_ref.shape[0] - 4
+    copies = far_copies(f, chip(f, 1, 4 - dx), 0, piece_ref.at[pl.ds(0, count)], final_ref, sems, 0)
+    run(copies + router_copies(f, chip(f, 0, 4 - dx), piece_ref.at[pl.ds(count, 4)], router_ref, sems, 2))
+
+
+def place_relayed(dx, f, piece, final, router):
+    return pl.pallas_call(
+        functools.partial(place_relayed_kernel, dx),
         out_shape=[array(*final.shape), array(*router.shape)],
         in_specs=[SMEM, VMEM, ANY, ANY],
         out_specs=[ANY, ANY],
-        scratch_shapes=[pltpu.SemaphoreType.DMA((8,))],
+        scratch_shapes=[pltpu.SemaphoreType.DMA((6,))],
         input_output_aliases={2: 0, 3: 1},
         compiler_params=params(2),
-        cost_estimate=cost(2**19, 2**19),
-        name="place_near",
+        cost_estimate=cost(2**18, 2**18),
+        name="place_relayed",
     )(f, piece, final, router)
 
 
@@ -332,7 +412,7 @@
     y = lax.axis_index("ep").reshape(1)
     far_plane = 1 - position // 8
 
-    scale, swap, swap_direct, swap_early = local_maxima(f, w)
+    scale, swap, swap_early = local_maxima(f, w)
     theirs_early = send(swap_early, 0, 0, 1)
     peer = send(scale, 1, 0, 0)
     product = router_weight.T * router_gain.reshape(1, -1)
@@ -343,28 +423,30 @@
     early = jnp.concatenate([own.reshape(-1, 128), other.reshape(-1, 128), product])
     relay = send(early, 1, 0, 0)
     theirs = send(swap, 0, 0, 1)
-    theirs_direct = send(swap_direct, 0, 0, 1)
     scale = jnp.maximum(scale, peer)
     scale = jnp.maximum(scale, send(scale, 0, 0, 1))
     scale = functools.reduce(jnp.maximum, [scale] + [send(scale, 0, dx, 0) for dx in (1, 3, 2)])
+    direct = experts - RELAY - EARLY
+    swap_direct = swap_rows(f, w, RELAY, direct)
+    theirs_direct = send(swap_direct, 0, 0, 1)
 
     (chunk,) = far_pieces(f, w, theirs, scale, 0, RELAY, True)
     forward = send(chunk, 1, 0, 0)
+    *pieces, final = near_pieces(f, w, scale, relay, (theirs, theirs_direct, theirs_early))
+    plane = [send(piece, 0, k + 1, 0) for k, piece in enumerate(pieces)]
+    pieces = far_pieces(f, w, theirs_direct, scale, RELAY, direct, False)
+    across = [send(piece, 1, k, 0) for k, piece in enumerate(pieces)]
     near = jnp.stack([product, relay[2 * EARLY * 256 :]]).astype(BF16)
     near = jnp.concatenate([near, send(near, 0, 0, 1)])
     received = [near]
     for d in (1, 2, 3):
         received.append(lax.ppermute(near, "ep", [(i, (i + d) % 4) for i in range(4)]))
-    *pieces, final, router = near_pieces(f, y, w, scale, relay, received, (theirs, theirs_direct, theirs_early))
-    plane = [send(piece, 0, k + 1, 0) for k, piece in enumerate(pieces)]
-    pieces = far_pieces(f, w, theirs_direct, scale, RELAY, experts - RELAY - EARLY, False)
-    across = [send(piece, 1, k, 0) for k, piece in enumerate(pieces)]
-    for k in range(3):
-        final, router = place_near(k + 1, f, plane[k], final, router)
-    *pieces, final = split(f, forward, final)
+    *pieces, final, router = split(f, y, forward, received, final)
     relayed = [send(piece, 0, k + 1, 0) for k, piece in enumerate(pieces)]
     for k in range(3):
-        final = place_far(k + 1, 0, f, relayed[k], final)
+        final = place_near(k + 1, f, plane[k], final)
+    for k in range(3):
+        final, router = place_relayed(k + 1, f, relayed[k], final, router)
     for k in range(4):
         final = place_far(k, RELAY, f, across[k], final)
     own = lax.dynamic_slice_in_dim(scale, position * 64, 64, axis=1)

time: 147 us -> 146 us (level); the launches traced: 144 us -> 144 us
  waiting for transfers between devices: 67.7 us -> 53.2 us
  starting transfers between devices: 47.7 us -> 58.5 us
  Pallas kernels: 22.7 us -> 28.3 us
    ppermute x21, waiting for transfers between devices: 64.5 us -> 45.9 us  [send(): return lax.ppermute(piece, 'fsdp', route(dz, dx, dc))]
    ppermute x21, starting transfers between devices: 45.4 us -> 55.6 us  [send(): return lax.ppermute(piece, 'fsdp', route(dz, dx, dc))]
    pallas_call x4 -> x8, Pallas kernels: 3.51 us -> 11.5 us  [the longest x3 4.62 us: place_near(): pl.pallas_call(functools.partial(place_near_kernel, dx), out_shape=array(...]
    ppermute x3, waiting for transfers between devices: 3.12 us -> 7.29 us  [served(): lax.ppermute(near, 'ep', [(i, (i + d) % 4) for i in range(4)])]
    pallas_call x7 -> x4, Pallas kernels: 4.98 us -> 3.01 us  [place_far(): pl.pallas_call(functools.partial(place_far_kernel, dx, first), out_shape=...]
  transfers between devices with their start and end apart: 24 -> 24, of which waited for: 14 -> 12; matrix products, arithmetic and copies ran while one was open for 1% -> 1% of each run, Pallas kernels for 11% -> 17%
where the time goes in v4:
time: 146 us; the launch traced here: 144 us
  starting transfers between devices  58.5 us (40%)
  waiting for transfers between devices  53.2 us (36%)
  Pallas kernels  28.3 us (19%)
  local copies, waits for them, and re-layouts  3.19 us (2%)
    ppermute x21, starting transfers between devices, send(): return lax.ppermute(piece, 'fsdp', route(dz, dx, dc))  55.6 us
    ppermute x21, waiting for transfers between devices, send(): return lax.ppermute(piece, 'fsdp', route(dz, dx, dc))  45.9 us
    ppermute x3, waiting for transfers between devices, served(): lax.ppermute(near, 'ep', [(i, (i + d) % 4) for i in range(4)])  7.29 us
    pallas_call x2, Pallas kernels, far_pieces(): pl.pallas_call(functools.partial(far_kernel, (first, count, whole)), out_...  5.42 us
    pallas_call x1, Pallas kernels, local_maxima(): pl.pallas_call(local_kernel, out_shape=[array(experts, rows, kind=F32), *...  4.86 us
    pallas_call x3, Pallas kernels, place_near(): pl.pallas_call(functools.partial(place_near_kernel, dx), out_shape=array(...  4.62 us
    pallas_call x1, Pallas kernels, near_pieces(): pl.pallas_call(near_kernel, out_shape=[array(blocks, 64, 128)] * 3 + [arr...  3.45 us
    pallas_call x4, Pallas kernels, place_far(): pl.pallas_call(functools.partial(place_far_kernel, dx, first), out_shape=...  3.01 us
  transfers between devices with their start and end apart: 24, of which 12 were waited for; matrix products, arithmetic and copies ran while one was open for 1% of the time, Pallas kernels for 17%

profile of v4, /device:TPU:55, one launch (start us, length us, event | category | flops | bytes accessed | tf_op | source)
XLA Modules:
  0.0 144.4 jit_solution(6882892560430457157)
XLA Ops:
  0.6 2.7 %swap_rows.1 = f32[11,512,128]{2,1,0:T(8,128)} custom-call(s32[1]{0:T(128)} %bitcast.f_ref, f32[16,1024,128]{2,1,0:T(8,128)} %w_ref.9), custom_call_target="tpu_custom_call" | custom-call | flops 25165824 | bytes 6291456 | tf_op jit(solution)/shard_map/swap_rows/pallas_call | solution.py:135
  3.4 0.8 collective-permute-start
  4.1 4.9 %local_maxima.1 = (f32[16,1024]{1,0:T(8,128)S(1)}, f32[4,512,128]{2,1,0:T(8,128)}, f32[1,512,128]{2,1,0:T(8,128)S(1)}) custom-call(s32[1]{0:T(128)} %bitcast.f_ref, f32[16,1024,128]{2,1,0:T(8,128)} %w_ref.9), custom_call_target="tpu_custom_call" | custom-call | flops 50331648 | bytes 12582912 | tf_op jit(solution)/shard_map/local_maxima/pallas_call | solution.py:97
  9.1 6.1 %collective-permute-start.1 = (f32[16,1024]{1,0:T(8,128)S(1)}, f32[16,1024]{1,0:T(8,128)S(1)}, u32[]{:S(2)}, u32[]{:S(2)}) collective-permute-start(f32[16,1024]{1,0:T(8,128)S(1)} %get-tuple-element.25), channel_id=1, source_target_pairs={{0,8},{1,9},{2,10},{3,11},{4,12},{5,13},{6,14},{7,15},{8,0},{9,1},... | collective-permute-start | bytes 196616 | tf_op jit(solution)/shard_map/ppermute | solution.py:48
  15.2 0.7 collective-permute-start.12
  15.9 1.3 collective-permute-done.1
  17.3 1.9 %collective-permute-start.2 = (f32[16,1024]{1,0:T(8,128)S(1)}, f32[16,1024]{1,0:T(8,128)S(1)}, u32[]{:S(2)}, u32[]{:S(2)}) collective-permute-start(f32[16,1024]{1,0:T(8,128)S(1)} %max.15), channel_id=1, source_target_pairs={{0,1},{1,0},{2,3},{3,2},{4,5},{5,4},{6,7},{7,6},{8,9},{9,8},{10,11... | collective-permute-start | bytes 196616 | tf_op jit(solution)/shard_map/ppermute | solution.py:48
  19.2 0.9 constant_dynamic-slice_fusion.1
  20.2 1.2 collective-permute-start.5
  21.4 2.7 %collective-permute-start.3 = (f32[16,1024]{1,0:T(8,128)S(1)}, f32[16,1024]{1,0:T(8,128)S(1)}, u32[]{:S(2)}, u32[]{:S(2)}) collective-permute-start(f32[16,1024]{1,0:T(8,128)S(1)} %max.16), channel_id=1, source_target_pairs={{0,2},{1,3},{2,4},{3,5},{4,6},{5,7},{6,0},{7,1},{8,10},{9,11},{10,... | collective-permute-start | bytes 196616 | tf_op jit(solution)/shard_map/ppermute | solution.py:48
  24.1 0.8 collective-permute-done.5
  24.9 6.1 %collective-permute-start.13 = (f32[528,128]{1,0:T(8,128)S(1)}, f32[528,128]{1,0:T(8,128)S(1)}, u32[]{:S(2)}, u32[]{:S(2)}) collective-permute-start(f32[528,128]{1,0:T(8,128)S(1)} %pad_maximum_fusion), channel_id=1, source_target_pairs={{0,8},{1,9},{2,10},{3,11},{4,12},{5,13},{6,14},{7,15},{8,0},{9,1},... | collective-permute-start | bytes 811016 | tf_op jit(solution)/shard_map/ppermute | solution.py:48
  31.0 2.5 %far_pieces.3 = bf16[8,256,128]{2,1,0:T(8,128)(2,1)} custom-call(s32[1]{0:T(128)} %bitcast.f_ref, f32[16,1024,128]{2,1,0:T(8,128)} %w_ref.9, f32[4,512,128]{2,1,0:T(8,128)} %collective-permute-done.10.theirs_ref.refs_0_, f32[16,1024]{1,0:T(8,128)S(1)} %maximum_maximum_fusion.scale_ref), custom_call_target="tpu_custom_call" | custom-call | flops 12582912 | bytes 3145728 | tf_op jit(solution)/shard_map/far_pieces/pallas_call | solution.py:190
  33.5 2.2 %collective-permute-start.11 = (bf16[8,256,128]{2,1,0:T(8,128)(2,1)}, bf16[8,256,128]{2,1,0:T(8,128)(2,1)}, u32[]{:S(2)}, u32[]{:S(2)}) collective-permute-start(bf16[8,256,128]{2,1,0:T(8,128)(2,1)} %far_pieces.3), channel_id=1, source_target_pairs={{0,8},{1,9},{2,10},{3,11},{4,12},{5,13},{6,14},{7,15},{8,0},{9,1},... | collective-permute-start | bytes 1572872 | tf_op jit(solution)/shard_map/ppermute | solution.py:48
  35.6 14.9 %collective-permute-done.13.relay_ref = f32[528,128]{1,0:T(8,128)S(1)} collective-permute-done((f32[528,128]{1,0:T(8,128)S(1)}, f32[528,128]{1,0:T(8,128)S(1)}, u32[]{:S(2)}, u32[]{:S(2)}) %collective-permute-start.13) | collective-permute-done | bytes 270368 | tf_op jit(solution)/shard_map/ppermute | solution.py:48
  50.5 3.4 %near_pieces.1 = (bf16[34,64,128]{2,1,0:T(8,128)(2,1)}, bf16[34,64,128]{2,1,0:T(8,128)(2,1)}, bf16[34,64,128]{2,1,0:T(8,128)(2,1)}, bf16[16,64,2048]{2,1,0:T(8,128)(2,1)}) custom-call(s32[1]{0:T(128)} %bitcast.f_ref, f32[16,1024,128]{2,1,0:T(8,128)} %w_ref.9, f32[16,1024]{1,0:T(8,128)S(1)} %maximum_maximum_fusion.scale_ref, ...), custom_call_target="tpu_custom_call" | custom-call | flops 33554432 | bytes 8388608 | tf_op jit(solution)/shard_map/near_pieces/pallas_call | solution.py:275
  54.6 0.8 collective-permute-start.22
  55.4 1.9 %collective-permute-start.23 = (bf16[34,64,128]{2,1,0:T(8,128)(2,1)}, bf16[34,64,128]{2,1,0:T(8,128)(2,1)}, u32[]{:S(2)}, u32[]{:S(2)}) collective-permute-start(bf16[34,64,128]{2,1,0:T(8,128)(2,1)} %get-tuple-element.38), channel_id=1, source_target_pairs={{0,2},{1,3},{2,4},{3,5},{4,6},{5,7},{6,0},{7,1},{8,10},{9,11},{10,... | collective-permute-start | bytes 1671176 | tf_op jit(solution)/shard_map/ppermute | solution.py:48
  57.3 6.4 %collective-permute-start.14 = (bf16[2,16,128]{2,1,0:T(8,128)(2,1)S(1)}, bf16[2,16,128]{2,1,0:T(8,128)(2,1)S(1)}, u32[]{:S(2)}, u32[]{:S(2)}) collective-permute-start(bf16[2,16,128]{2,1,0:T(8,128)(2,1)S(1)} %pad_maximum_fusion.2), channel_id=1, source_target_pairs={{0,1},{1,0},{2,3},{3,2},{4,5},{5,4},{6,7},{7,6},{8,9},{9,8},{10,11... | collective-permute-start | bytes 24584 | tf_op jit(solution)/shard_map/ppermute | solution.py:48
  63.7 0.8 collective-permute-done.14
  64.7 2.7 %collective-permute-done.17.refs_3_ = bf16[4,16,128]{2,1,0:T(8,128)(2,1)S(1)} collective-permute-done((bf16[4,16,128]{2,1,0:T(8,128)(2,1)S(1)}, bf16[4,16,128]{2,1,0:T(8,128)(2,1)S(1)}, u32[]{:S(2)}, u32[]{:S(2)}) %collective-permute-start.17) | collective-permute-done | bytes 16416 | tf_op jit(solution)/shard_map/ppermute | solution.py:443
  67.4 0.8 collective-permute-start.16
  68.2 3.6 %collective-permute-done.16.refs_2_ = bf16[4,16,128]{2,1,0:T(8,128)(2,1)S(1)} collective-permute-done((bf16[4,16,128]{2,1,0:T(8,128)(2,1)S(1)}, bf16[4,16,128]{2,1,0:T(8,128)(2,1)S(1)}, u32[]{:S(2)}, u32[]{:S(2)}) %collective-permute-start.16) | collective-permute-done | bytes 16416 | tf_op jit(solution)/shard_map/ppermute | solution.py:443
  71.8 1.9 %collective-permute-start.15 = (bf16[4,16,128]{2,1,0:T(8,128)(2,1)S(1)}, bf16[4,16,128]{2,1,0:T(8,128)(2,1)}, u32[]{:S(2)}, u32[]{:S(2)}) collective-permute-start(bf16[4,16,128]{2,1,0:T(8,128)(2,1)S(1)} %pad_maximum_fusion.1.refs_0_), channel_id=1, source_target_pairs={{0,16},{16,32},{32,48},{48,0},{1,17},{17,33},{33,49},{49,1},{2,18}... | collective-permute-start | bytes 49160 | tf_op jit(solution)/shard_map/ppermute | solution.py:443
  73.7 1.0 collective-permute-done.15.refs_1_
  74.7 2.1 %split.1 = (bf16[12,64,128]{2,1,0:T(8,128)(2,1)S(1)}, bf16[12,64,128]{2,1,0:T(8,128)(2,1)S(1)}, bf16[12,64,128]{2,1,0:T(8,128)(2,1)}, bf16[16,64,2048]{2,1,0:T(8,128)(2,1)}, bf16[64,2048]{1,0:T(8,128)(2,1)}) custom-call(s32[1]{0:T(128)} %bitcast.f_ref, s32[1]{0:T(128)} %bitcast.1.y_ref, ...), custom_call_target="tpu_custom_call", output_to_operand_aliasing={{3}: (7, {})} | custom-call | flops 8388608 | bytes 2097152 | tf_op jit(solution)/shard_map/split/pallas_call | solution.py:336
  76.8 1.5 %collective-permute-start.19 = (bf16[12,64,128]{2,1,0:T(8,128)(2,1)S(1)}, bf16[12,64,128]{2,1,0:T(8,128)(2,1)S(1)}, u32[]{:S(2)}, u32[]{:S(2)}) collective-permute-start(bf16[12,64,128]{2,1,0:T(8,128)(2,1)S(1)} %get-tuple-element.34), channel_id=1, source_target_pairs={{0,4},{1,5},{2,6},{3,7},{4,0},{5,1},{6,2},{7,3},{8,12},{9,13},{10,... | collective-permute-start | bytes 589832 | tf_op jit(solution)/shard_map/ppermute | solution.py:48
  78.3 1.1 collective-permute-start.20
  79.4 2.9 %far_pieces.2 = (bf16[22,64,128]{2,1,0:T(8,128)(2,1)}, bf16[22,64,128]{2,1,0:T(8,128)(2,1)}, bf16[22,64,128]{2,1,0:T(8,128)(2,1)}, bf16[22,64,128]{2,1,0:T(8,128)(2,1)}) custom-call(s32[1]{0:T(128)} %bitcast.f_ref, f32[16,1024,128]{2,1,0:T(8,128)} %w_ref.9, f32[11,512,128]{2,1,0:T(8,128)S(1)} %collective-permute-done.theirs_ref.refs_1_, ...), custom_call_target="tpu_custom_call" | custom-call | flops 12582912 | bytes 3145728 | tf_op jit(solution)/shard_map/far_pieces/pallas_call | solution.py:190
  82.9 0.7 copy-done
  83.6 5.1 %collective-permute-start.9 = (bf16[22,64,128]{2,1,0:T(8,128)(2,1)}, bf16[22,64,128]{2,1,0:T(8,128)(2,1)S(1)}, u32[]{:S(2)}, u32[]{:S(2)}) collective-permute-start(bf16[22,64,128]{2,1,0:T(8,128)(2,1)} %get-tuple-element.29), channel_id=1, source_target_pairs={{0,8},{1,9},{2,10},{3,11},{4,12},{5,13},{6,14},{7,15},{8,0},{9,1},... | collective-permute-start | bytes 1081352 | tf_op jit(solution)/shard_map/ppermute | solution.py:48
  89.9 9.1 %collective-permute-start.8 = (bf16[22,64,128]{2,1,0:T(8,128)(2,1)}, bf16[22,64,128]{2,1,0:T(8,128)(2,1)S(1)}, u32[]{:S(2)}, u32[]{:S(2)}) collective-permute-start(bf16[22,64,128]{2,1,0:T(8,128)(2,1)} %get-tuple-element.28), channel_id=1, source_target_pairs={{0,10},{1,11},{2,12},{3,13},{4,14},{5,15},{6,8},{7,9},{8,2},{9,3},... | collective-permute-start | bytes 1081352 | tf_op jit(solution)/shard_map/ppermute | solution.py:48
  99.0 3.4 %collective-permute-start.6 = (bf16[22,64,128]{2,1,0:T(8,128)(2,1)}, bf16[22,64,128]{2,1,0:T(8,128)(2,1)S(1)}, u32[]{:S(2)}, u32[]{:S(2)}) collective-permute-start(bf16[22,64,128]{2,1,0:T(8,128)(2,1)} %get-tuple-element.26), channel_id=1, source_target_pairs={{0,14},{1,15},{2,8},{3,9},{4,10},{5,11},{6,12},{7,13},{8,6},{9,7},... | collective-permute-start | bytes 1081352 | tf_op jit(solution)/shard_map/ppermute | solution.py:48
  102.4 4.0 %collective-permute-start.18 = (bf16[12,64,128]{2,1,0:T(8,128)(2,1)}, bf16[12,64,128]{2,1,0:T(8,128)(2,1)S(1)}, u32[]{:S(2)}, u32[]{:S(2)}) collective-permute-start(bf16[12,64,128]{2,1,0:T(8,128)(2,1)} %get-tuple-element.33), channel_id=1, source_target_pairs={{0,6},{1,7},{2,0},{3,1},{4,2},{5,3},{6,4},{7,5},{8,14},{9,15},{10,... | collective-permute-start | bytes 589832 | tf_op jit(solution)/shard_map/ppermute | solution.py:48
  106.5 0.7 constant_dynamic-slice_fusion
  107.1 1.9 %place_near.3._ = bf16[16,64,2048]{2,1,0:T(8,128)(2,1)} custom-call(s32[1]{0:T(128)} %bitcast.f_ref, bf16[34,64,128]{2,1,0:T(8,128)(2,1)} %collective-permute-done.23.piece_ref, bf16[16,64,2048]{2,1,0:T(8,128)(2,1)} %get-tuple-element.39._), custom_call_target="tpu_custom_call", output_to_operand_aliasing={{}: (2, {})} | custom-call | flops 4194304 | bytes 1048576 | tf_op jit(solution)/shard_map/place_near/pallas_call | solution.py:374
  109.0 1.9 %place_near.4._ = bf16[16,64,2048]{2,1,0:T(8,128)(2,1)} custom-call(s32[1]{0:T(128)} %bitcast.f_ref, bf16[34,64,128]{2,1,0:T(8,128)(2,1)} %collective-permute-done.22.piece_ref, bf16[16,64,2048]{2,1,0:T(8,128)(2,1)} %place_near.3._), custom_call_target="tpu_custom_call", output_to_operand_aliasing={{}: (2, {})} | custom-call | flops 4194304 | bytes 1048576 | tf_op jit(solution)/shard_map/place_near/pallas_call | solution.py:374
  110.9 0.9 place_near.5._
  112.0 0.7 place_relayed.3
  112.7 0.7 place_relayed.4
  113.5 0.7 place_relayed.5
  114.2 0.8 place_far.4._
  115.0 12.1 %collective-permute-done.8.piece_ref = bf16[22,64,128]{2,1,0:T(8,128)(2,1)S(1)} collective-permute-done((bf16[22,64,128]{2,1,0:T(8,128)(2,1)}, bf16[22,64,128]{2,1,0:T(8,128)(2,1)S(1)}, u32[]{:S(2)}, u32[]{:S(2)}) %collective-permute-start.8) | collective-permute-done | bytes 360480 | tf_op jit(solution)/shard_map/ppermute | solution.py:48
  127.1 0.7 place_far.5._
  127.8 6.6 %collective-permute-done.7.piece_ref = bf16[22,64,128]{2,1,0:T(8,128)(2,1)S(1)} collective-permute-done((bf16[22,64,128]{2,1,0:T(8,128)(2,1)}, bf16[22,64,128]{2,1,0:T(8,128)(2,1)S(1)}, u32[]{:S(2)}, u32[]{:S(2)}) %collective-permute-start.7) | collective-permute-done | bytes 360480 | tf_op jit(solution)/shard_map/ppermute | solution.py:48
  134.5 0.7 place_far.6._
  135.2 8.2 %collective-permute-done.6.piece_ref = bf16[22,64,128]{2,1,0:T(8,128)(2,1)S(1)} collective-permute-done((bf16[22,64,128]{2,1,0:T(8,128)(2,1)}, bf16[22,64,128]{2,1,0:T(8,128)(2,1)S(1)}, u32[]{:S(2)}, u32[]{:S(2)}) %collective-permute-start.6) | collective-permute-done | bytes 360480 | tf_op jit(solution)/shard_map/ppermute | solution.py:48
  143.5 0.7 place_far.7
  (39 shorter events, 3.1 us)
Async XLA Ops:
  3.3 12.5 %copy-start.4 = (f32[128,16]{0,1:T(8,128)S(1)}, f32[128,16]{0,1:T(8,128)}, u32[]{:S(2)}) copy-start(f32[128,16]{0,1:T(8,128)} %param.4) | copy-start | bytes 24580
  3.4 12.5 %copy-start.5 = (f32[128]{0:T(128)S(1)}, f32[128]{0:T(128)}, u32[]{:S(2)}) copy-start(f32[128]{0:T(128)} %param.5) | copy-start | bytes 1540
  3.4 47.1 %collective-permute-start = (f32[11,512,128]{2,1,0:T(8,128)}, f32[11,512,128]{2,1,0:T(8,128)S(1)}, u32[]{:S(2)}, u32[]{:S(2)}) collective-permute-start(f32[11,512,128]{2,1,0:T(8,128)} %swap_rows.1), channel_id=1, source_target_pairs={{0,1},{1,0},{2,3},{3,2},{4,5},{5,4},{6,7},{7,6},{8,9},{9,8},{10,11... | collective-permute-start | bytes 8650760 | tf_op jit(solution)/shard_map/ppermute | solution.py:48
  9.0 22.0 %collective-permute-start.10 = (f32[4,512,128]{2,1,0:T(8,128)}, f32[4,512,128]{2,1,0:T(8,128)}, u32[]{:S(2)}, u32[]{:S(2)}) collective-permute-start(f32[4,512,128]{2,1,0:T(8,128)} %get-tuple-element.30), channel_id=1, source_target_pairs={{0,1},{1,0},{2,3},{3,2},{4,5},{5,4},{6,7},{7,6},{8,9},{9,8},{10,11... | collective-permute-start | bytes 3145736 | tf_op jit(solution)/shard_map/ppermute | solution.py:48
  9.1 8.2 %collective-permute-start.1 = (f32[16,1024]{1,0:T(8,128)S(1)}, f32[16,1024]{1,0:T(8,128)S(1)}, u32[]{:S(2)}, u32[]{:S(2)}) collective-permute-start(f32[16,1024]{1,0:T(8,128)S(1)} %get-tuple-element.25), channel_id=1, source_target_pairs={{0,8},{1,9},{2,10},{3,11},{4,12},{5,13},{6,14},{7,15},{8,0},{9,1},... | collective-permute-start | bytes 196616 | tf_op jit(solution)/shard_map/ppermute | solution.py:48
  15.2 6.2 %collective-permute-start.12 = (f32[1,512,128]{2,1,0:T(8,128)S(1)}, f32[1,512,128]{2,1,0:T(8,128)S(1)}, u32[]{:S(2)}, u32[]{:S(2)}) collective-permute-start(f32[1,512,128]{2,1,0:T(8,128)S(1)} %get-tuple-element.31), channel_id=1, source_target_pairs={{0,1},{1,0},{2,3},{3,2},{4,5},{5,4},{6,7},{7,6},{8,9},{9,8},{10,11... | collective-permute-start | bytes 786440 | tf_op jit(solution)/shard_map/ppermute | solution.py:48
  17.3 2.9 %collective-permute-start.2 = (f32[16,1024]{1,0:T(8,128)S(1)}, f32[16,1024]{1,0:T(8,128)S(1)}, u32[]{:S(2)}, u32[]{:S(2)}) collective-permute-start(f32[16,1024]{1,0:T(8,128)S(1)} %max.15), channel_id=1, source_target_pairs={{0,1},{1,0},{2,3},{3,2},{4,5},{5,4},{6,7},{7,6},{8,9},{9,8},{10,11... | collective-permute-start | bytes 196616 | tf_op jit(solution)/shard_map/ppermute | solution.py:48
  20.2 4.7 %collective-permute-start.5 = (f32[16,1024]{1,0:T(8,128)S(1)}, f32[16,1024]{1,0:T(8,128)S(1)}, u32[]{:S(2)}, u32[]{:S(2)}) collective-permute-start(f32[16,1024]{1,0:T(8,128)S(1)} %max.16), channel_id=1, source_target_pairs={{0,4},{1,5},{2,6},{3,7},{4,0},{5,1},{6,2},{7,3},{8,12},{9,13},{10,... | collective-permute-start | bytes 196616 | tf_op jit(solution)/shard_map/ppermute | solution.py:48
  21.4 9.6 %collective-permute-start.4 = (f32[16,1024]{1,0:T(8,128)S(1)}, f32[16,1024]{1,0:T(8,128)S(1)}, u32[]{:S(2)}, u32[]{:S(2)}) collective-permute-start(f32[16,1024]{1,0:T(8,128)S(1)} %max.16), channel_id=1, source_target_pairs={{0,6},{1,7},{2,0},{3,1},{4,2},{5,3},{6,4},{7,5},{8,14},{9,15},{10,... | collective-permute-start | bytes 196616 | tf_op jit(solution)/shard_map/ppermute | solution.py:48
  21.4 9.6 %collective-permute-start.3 = (f32[16,1024]{1,0:T(8,128)S(1)}, f32[16,1024]{1,0:T(8,128)S(1)}, u32[]{:S(2)}, u32[]{:S(2)}) collective-permute-start(f32[16,1024]{1,0:T(8,128)S(1)} %max.16), channel_id=1, source_target_pairs={{0,2},{1,3},{2,4},{3,5},{4,6},{5,7},{6,0},{7,1},{8,10},{9,11},{10,... | collective-permute-start | bytes 196616 | tf_op jit(solution)/shard_map/ppermute | solution.py:48
  24.9 25.6 %collective-permute-start.13 = (f32[528,128]{1,0:T(8,128)S(1)}, f32[528,128]{1,0:T(8,128)S(1)}, u32[]{:S(2)}, u32[]{:S(2)}) collective-permute-start(f32[528,128]{1,0:T(8,128)S(1)} %pad_maximum_fusion), channel_id=1, source_target_pairs={{0,8},{1,9},{2,10},{3,11},{4,12},{5,13},{6,14},{7,15},{8,0},{9,1},... | collective-permute-start | bytes 811016 | tf_op jit(solution)/shard_map/ppermute | solution.py:48
  33.5 41.2 %collective-permute-start.11 = (bf16[8,256,128]{2,1,0:T(8,128)(2,1)}, bf16[8,256,128]{2,1,0:T(8,128)(2,1)}, u32[]{:S(2)}, u32[]{:S(2)}) collective-permute-start(bf16[8,256,128]{2,1,0:T(8,128)(2,1)} %far_pieces.3), channel_id=1, source_target_pairs={{0,8},{1,9},{2,10},{3,11},{4,12},{5,13},{6,14},{7,15},{8,0},{9,1},... | collective-permute-start | bytes 1572872 | tf_op jit(solution)/shard_map/ppermute | solution.py:48
  53.9 45.1 %collective-permute-start.21 = (bf16[34,64,128]{2,1,0:T(8,128)(2,1)}, bf16[34,64,128]{2,1,0:T(8,128)(2,1)S(1)}, u32[]{:S(2)}, u32[]{:S(2)}) collective-permute-start(bf16[34,64,128]{2,1,0:T(8,128)(2,1)} %get-tuple-element.36), channel_id=1, source_target_pairs={{0,6},{1,7},{2,0},{3,1},{4,2},{5,3},{6,4},{7,5},{8,14},{9,15},{10,... | collective-permute-start | bytes 1671176 | tf_op jit(solution)/shard_map/ppermute | solution.py:48
  54.6 44.4 %collective-permute-start.22 = (bf16[34,64,128]{2,1,0:T(8,128)(2,1)}, bf16[34,64,128]{2,1,0:T(8,128)(2,1)}, u32[]{:S(2)}, u32[]{:S(2)}) collective-permute-start(bf16[34,64,128]{2,1,0:T(8,128)(2,1)} %get-tuple-element.37), channel_id=1, source_target_pairs={{0,4},{1,5},{2,6},{3,7},{4,0},{5,1},{6,2},{7,3},{8,12},{9,13},{10,... | collective-permute-start | bytes 1671176 | tf_op jit(solution)/shard_map/ppermute | solution.py:48
  55.4 47.0 %collective-permute-start.23 = (bf16[34,64,128]{2,1,0:T(8,128)(2,1)}, bf16[34,64,128]{2,1,0:T(8,128)(2,1)}, u32[]{:S(2)}, u32[]{:S(2)}) collective-permute-start(bf16[34,64,128]{2,1,0:T(8,128)(2,1)} %get-tuple-element.38), channel_id=1, source_target_pairs={{0,2},{1,3},{2,4},{3,5},{4,6},{5,7},{6,0},{7,1},{8,10},{9,11},{10,... | collective-permute-start | bytes 1671176 | tf_op jit(solution)/shard_map/ppermute | solution.py:48
  57.3 7.2 %collective-permute-start.14 = (bf16[2,16,128]{2,1,0:T(8,128)(2,1)S(1)}, bf16[2,16,128]{2,1,0:T(8,128)(2,1)S(1)}, u32[]{:S(2)}, u32[]{:S(2)}) collective-permute-start(bf16[2,16,128]{2,1,0:T(8,128)(2,1)S(1)} %pad_maximum_fusion.2), channel_id=1, source_target_pairs={{0,1},{1,0},{2,3},{3,2},{4,5},{5,4},{6,7},{7,6},{8,9},{9,8},{10,11... | collective-permute-start | bytes 24584 | tf_op jit(solution)/shard_map/ppermute | solution.py:48
  64.5 2.9 %collective-permute-start.17 = (bf16[4,16,128]{2,1,0:T(8,128)(2,1)S(1)}, bf16[4,16,128]{2,1,0:T(8,128)(2,1)S(1)}, u32[]{:S(2)}, u32[]{:S(2)}) collective-permute-start(bf16[4,16,128]{2,1,0:T(8,128)(2,1)S(1)} %pad_maximum_fusion.1.refs_0_), channel_id=1, source_target_pairs={{0,48},{16,0},{32,16},{48,32},{1,49},{17,1},{33,17},{49,33},{2,50}... | collective-permute-start | bytes 49160 | tf_op jit(solution)/shard_map/ppermute | solution.py:443
  67.4 4.4 %collective-permute-start.16 = (bf16[4,16,128]{2,1,0:T(8,128)(2,1)S(1)}, bf16[4,16,128]{2,1,0:T(8,128)(2,1)S(1)}, u32[]{:S(2)}, u32[]{:S(2)}) collective-permute-start(bf16[4,16,128]{2,1,0:T(8,128)(2,1)S(1)} %pad_maximum_fusion.1.refs_0_), channel_id=1, source_target_pairs={{0,32},{16,48},{32,0},{48,16},{1,33},{17,49},{33,1},{49,17},{2,34}... | collective-permute-start | bytes 49160 | tf_op jit(solution)/shard_map/ppermute | solution.py:443
  71.8 2.9 %collective-permute-start.15 = (bf16[4,16,128]{2,1,0:T(8,128)(2,1)S(1)}, bf16[4,16,128]{2,1,0:T(8,128)(2,1)}, u32[]{:S(2)}, u32[]{:S(2)}) collective-permute-start(bf16[4,16,128]{2,1,0:T(8,128)(2,1)S(1)} %pad_maximum_fusion.1.refs_0_), channel_id=1, source_target_pairs={{0,16},{16,32},{32,48},{48,0},{1,17},{17,33},{33,49},{49,1},{2,18}... | collective-permute-start | bytes 49160 | tf_op jit(solution)/shard_map/ppermute | solution.py:443
  76.8 6.1 %collective-permute-start.19 = (bf16[12,64,128]{2,1,0:T(8,128)(2,1)S(1)}, bf16[12,64,128]{2,1,0:T(8,128)(2,1)S(1)}, u32[]{:S(2)}, u32[]{:S(2)}) collective-permute-start(bf16[12,64,128]{2,1,0:T(8,128)(2,1)S(1)} %get-tuple-element.34), channel_id=1, source_target_pairs={{0,4},{1,5},{2,6},{3,7},{4,0},{5,1},{6,2},{7,3},{8,12},{9,13},{10,... | collective-permute-start | bytes 589832 | tf_op jit(solution)/shard_map/ppermute | solution.py:48
  78.3 11.0 %collective-permute-start.20 = (bf16[12,64,128]{2,1,0:T(8,128)(2,1)S(1)}, bf16[12,64,128]{2,1,0:T(8,128)(2,1)S(1)}, u32[]{:S(2)}, u32[]{:S(2)}) collective-permute-start(bf16[12,64,128]{2,1,0:T(8,128)(2,1)S(1)} %get-tuple-element.35), channel_id=1, source_target_pairs={{0,2},{1,3},{2,4},{3,5},{4,6},{5,7},{6,0},{7,1},{8,10},{9,11},{10,... | collective-permute-start | bytes 589832 | tf_op jit(solution)/shard_map/ppermute | solution.py:48
  82.9 0.7 copy-start
  83.6 30.7 %collective-permute-start.9 = (bf16[22,64,128]{2,1,0:T(8,128)(2,1)}, bf16[22,64,128]{2,1,0:T(8,128)(2,1)S(1)}, u32[]{:S(2)}, u32[]{:S(2)}) collective-permute-start(bf16[22,64,128]{2,1,0:T(8,128)(2,1)} %get-tuple-element.29), channel_id=1, source_target_pairs={{0,8},{1,9},{2,10},{3,11},{4,12},{5,13},{6,14},{7,15},{8,0},{9,1},... | collective-permute-start | bytes 1081352 | tf_op jit(solution)/shard_map/ppermute | solution.py:48
  89.2 0.7 copy-start.2
  89.9 37.2 %collective-permute-start.8 = (bf16[22,64,128]{2,1,0:T(8,128)(2,1)}, bf16[22,64,128]{2,1,0:T(8,128)(2,1)S(1)}, u32[]{:S(2)}, u32[]{:S(2)}) collective-permute-start(bf16[22,64,128]{2,1,0:T(8,128)(2,1)} %get-tuple-element.28), channel_id=1, source_target_pairs={{0,10},{1,11},{2,12},{3,13},{4,14},{5,15},{6,8},{7,9},{8,2},{9,3},... | collective-permute-start | bytes 1081352 | tf_op jit(solution)/shard_map/ppermute | solution.py:48
  99.0 35.5 %collective-permute-start.7 = (bf16[22,64,128]{2,1,0:T(8,128)(2,1)}, bf16[22,64,128]{2,1,0:T(8,128)(2,1)S(1)}, u32[]{:S(2)}, u32[]{:S(2)}) collective-permute-start(bf16[22,64,128]{2,1,0:T(8,128)(2,1)} %get-tuple-element.27), channel_id=1, source_target_pairs={{0,12},{1,13},{2,14},{3,15},{4,8},{5,9},{6,10},{7,11},{8,4},{9,5},... | collective-permute-start | bytes 1081352 | tf_op jit(solution)/shard_map/ppermute | solution.py:48
  99.0 44.5 %collective-permute-start.6 = (bf16[22,64,128]{2,1,0:T(8,128)(2,1)}, bf16[22,64,128]{2,1,0:T(8,128)(2,1)S(1)}, u32[]{:S(2)}, u32[]{:S(2)}) collective-permute-start(bf16[22,64,128]{2,1,0:T(8,128)(2,1)} %get-tuple-element.26), channel_id=1, source_target_pairs={{0,14},{1,15},{2,8},{3,9},{4,10},{5,11},{6,12},{7,13},{8,6},{9,7},... | collective-permute-start | bytes 1081352 | tf_op jit(solution)/shard_map/ppermute | solution.py:48
  102.4 11.0 %collective-permute-start.18 = (bf16[12,64,128]{2,1,0:T(8,128)(2,1)}, bf16[12,64,128]{2,1,0:T(8,128)(2,1)S(1)}, u32[]{:S(2)}, u32[]{:S(2)}) collective-permute-start(bf16[12,64,128]{2,1,0:T(8,128)(2,1)} %get-tuple-element.33), channel_id=1, source_target_pairs={{0,6},{1,7},{2,0},{3,1},{4,2},{5,3},{6,4},{7,5},{8,14},{9,15},{10,... | collective-permute-start | bytes 589832 | tf_op jit(solution)/shard_map/ppermute | solution.py:48
  110.9 1.0 copy-start.3
  111.8 1.0 copy-start.1

commit v5 on v4

--- a/solution.py
+++ b/solution.py
@@ -8,8 +8,8 @@
 from jax.sharding import PartitionSpec as P
 
 
-RELAY = 4
-EARLY = 1
+RELAY = 5
+EARLY = 2
 BF16, F32 = jnp.bfloat16, jnp.float32
 ANY = pl.BlockSpec(memory_space=pl.ANY)
 VMEM = pl.BlockSpec(memory_space=pltpu.VMEM)
@@ -60,33 +60,33 @@
         copy.wait()
 
 
-def parts(experts):
-    return (0, RELAY), (RELAY, experts - RELAY - EARLY), (experts - EARLY, EARLY)
-
-
-def local_kernel(f_ref, w_ref, out_ref, *refs):
-    swap_refs, (taken, in_sems, out_sems) = refs[:2], refs[2:]
+def local_kernel(f_ref, w_ref, mine_ref, theirs_ref, swap_ref, taken, in_sems, out_sems):
     blocks, experts = taken.shape[:2]
-    away = 1 - f_ref[0] % 2
+    core = f_ref[0] % 2
     reads = []
     for b in range(blocks):
         reads.append(pltpu.make_async_copy(w_ref.at[:, pl.ds(128 * b, 128), :], taken.at[b], in_sems.at[b]))
         reads[-1].start()
     lane = lax.broadcasted_iota(jnp.int32, (128, 128), 1)
-    writes = []
+    low = lax.broadcasted_iota(jnp.int32, (experts, 128), 1) < 64
+    writes, rows = [], []
     for b in range(blocks):
         reads[b].wait()
-        for k, ((first, count), target) in enumerate(zip(parts(experts)[::2], swap_refs)):
-            rows = taken.at[b, pl.ds(first, count), span(64 * away, 64), :]
-            writes.append(
-                pltpu.make_async_copy(rows, target.at[:, pl.ds(64 * b, 64), :], out_sems.at[2 * b + k])
-            )
-            writes[-1].start()
+        piece = taken.at[b, pl.ds(0, RELAY), span(64 * (1 - core), 64), :]
+        writes.append(pltpu.make_async_copy(piece, swap_ref.at[:, pl.ds(64 * b, 64), :], out_sems.at[b]))
+        writes[-1].start()
         total = jnp.zeros((128, 128), F32)
         for e in range(experts):
             row = jnp.max(jnp.abs(taken[b, e]), axis=1, keepdims=True)
             total = jnp.where(lane == e, row, total)
-        out_ref[:, pl.ds(128 * b, 128)] = total.T[:experts]
+        rows.append(total.T[:experts])
+        if b % 2:
+            first, second = rows[-2:]
+            south = jnp.where(low, first, pltpu.roll(second, 64, 1))
+            north = jnp.where(low, pltpu.roll(first, 64, 1), second)
+            at = pl.ds(64 * (b - 1), 128)
+            mine_ref[:, at] = jnp.where(core == 0, south, north)
+            theirs_ref[:, at] = jnp.where(core == 0, north, south)
     for write in writes:
         write.wait()
 
@@ -97,15 +97,16 @@
     return pl.pallas_call(
         local_kernel,
         out_shape=[
-            array(experts, rows, kind=F32),
-            *(array(count, rows // 2, 128, kind=F32) for _, count in parts(experts)[::2]),
+            array(experts, rows // 2, kind=F32),
+            array(experts, rows // 2, kind=F32),
+            array(RELAY, rows // 2, 128, kind=F32),
         ],
         in_specs=[SMEM, ANY],
-        out_specs=[VMEM, ANY, ANY],
+        out_specs=[VMEM, VMEM, ANY],
         scratch_shapes=[
             pltpu.VMEM((blocks, experts, 128, 128), F32),
             pltpu.SemaphoreType.DMA((blocks,)),
-            pltpu.SemaphoreType.DMA((2 * blocks,)),
+            pltpu.SemaphoreType.DMA((blocks,)),
         ],
         compiler_params=params(46),
         cost_estimate=cost(8 * 2**20, 4 * 2**20),
@@ -148,8 +149,10 @@
     )(f, w)
 
 
-def inverse_columns(scale_ref, inverse, slot, block):
-    inverse[pl.ds(128 * slot, 128), :] = jnp.concatenate([1.0 / scale_ref[:, lanes(block)]] * 8, axis=0).T
+def inverse_columns(scale_ref, inverse):
+    for b in range(4):
+        block = 1.0 / scale_ref[:, pl.ds(128 * b, 128)]
+        inverse[pl.ds(128 * b, 128), :] = jnp.concatenate([block] * 8, axis=0).T
 
 
 def far_kernel(plan, f_ref, w_ref, theirs_ref, scale_ref, *refs):
@@ -162,17 +165,17 @@
     for dx in range(4):
         q = 4 * (1 - f // 8) + dx if whole else chip(f, 1, dx)
         own = w_ref.at[experts, span(128 * q + 64 * core, 64), :]
-        theirs = theirs_ref.at[:, span(64 * q, 64), :]
+        theirs = theirs_ref.at[pl.ds(0, count), span(64 * q, 64), :]
         for k, rows in enumerate((own, theirs)):
             reads.append(
                 pltpu.make_async_copy(rows, taken.at[dx, pl.ds(k * count, count)], in_sems.at[2 * dx + k])
             )
             reads[-1].start()
+    inverse_columns(scale_ref, inverse)
     writes = []
     for dx in range(4):
         q = 4 * (1 - f // 8) + dx if whole else chip(f, 1, dx)
-        inverse_columns(scale_ref, inverse, dx, q)
-        columns = inverse[span(128 * dx + 64 * core, 64), :]
+        columns = inverse[span(64 * q, 64), :]
         for k in range(2):
             reads[2 * dx + k].wait()
             for e in range(count):
@@ -205,9 +208,9 @@
     )(f, w, theirs, scale)
 
 
-def near_kernel(f_ref, w_ref, scale_ref, relay_ref, *refs):
-    theirs_refs, outs, final_ref, refs = refs[:3], refs[3:6], refs[6], refs[7:]
-    taken, relay, inverse, made, in_sems, out_sems = refs
+def near_kernel(f_ref, w_ref, scale_ref, *refs):
+    early_refs, (across_ref, theirs_ref, rest_ref), refs = refs[:EARLY], refs[EARLY : EARLY + 3], refs[EARLY + 3 :]
+    outs, final_ref, (taken, relay, inverse, made, in_sems, out_sems) = refs[:3], refs[3], refs[4:]
     experts = w_ref.shape[0]
     late = experts - EARLY
     f = f_ref[0]
@@ -215,28 +218,38 @@
     reads = []
     for dx in range(4):
         q = chip(f, 0, dx)
-        own = w_ref.at[:, span(128 * q + 64 * core, 64), :]
-        rows = [(own, 0, experts)]
-        for (first, count), theirs_ref in zip(parts(experts), theirs_refs):
-            rows.append((theirs_ref.at[:, span(64 * q, 64), :], experts + first, count))
-        for k, (piece, at, size) in enumerate(rows):
-            reads.append(pltpu.make_async_copy(piece, taken.at[dx, pl.ds(at, size)], in_sems.at[4 * dx + k]))
+        for k, (piece, at, size) in enumerate(
+            (
+                (w_ref.at[:, span(128 * q + 64 * core, 64), :], 0, experts),
+                (theirs_ref.at[:, span(64 * q, 64), :], experts, RELAY),
+                (rest_ref.at[:, span(64 * q, 64), :], experts + RELAY, experts - RELAY),
+            )
+        ):
+            reads.append(pltpu.make_async_copy(piece, taken.at[dx, pl.ds(at, size)], in_sems.at[3 * dx + k]))
             reads[-1].start()
-    relayed = pltpu.make_async_copy(relay_ref, relay, in_sems.at[16])
-    relayed.start()
+    half = 256 * EARLY
+    relayed = [pltpu.make_async_copy(across_ref, relay.at[pl.ds(half, half)], in_sems.at[12])]
+    for j, early_ref in enumerate(early_refs):
+        for k in range(4):
+            rows = early_ref.at[span(128 * k + 64 * core, 64), :]
+            target = relay.at[pl.ds(256 * j + 64 * k, 64)]
+            relayed.append(pltpu.make_async_copy(rows, target, in_sems.at[13 + 4 * j + k]))
+    for copy in relayed:
+        copy.start()
+    inverse_columns(scale_ref, inverse)
     writes = []
     for dx in (1, 2, 3, 0):
         q = chip(f, 0, dx)
-        inverse_columns(scale_ref, inverse, dx, q)
-        columns = inverse[span(128 * dx + 64 * core, 64), :]
-        for k in range(4):
-            reads[4 * dx + k].wait()
+        columns = inverse[span(64 * q, 64), :]
+        for k in range(3):
+            reads[3 * dx + k].wait()
         for k in range(2):
             for e in range(experts):
                 at = k * experts + e
                 made[dx, at] = (taken[dx, at] * columns[:, e : e + 1]).astype(BF16)
         if dx == 1:
-            relayed.wait()
+            for copy in relayed:
+                copy.wait()
         for k in range(2):
             for j in range(EARLY):
                 rows = relay[span(256 * (k * EARLY + j) + 64 * (q % 4), 64), :]
@@ -269,26 +282,26 @@
     return [pltpu.make_async_copy(a, b, sems.at[at + k]) for k, (a, b) in enumerate(copies)]
 
 
-def near_pieces(f, w, scale, relay, theirs):
+def near_pieces(f, w, scale, early, across, theirs, rest):
     experts = w.shape[0]
     blocks = 2 * experts + 2 * EARLY
     return pl.pallas_call(
         near_kernel,
         out_shape=[array(blocks, 64, 128)] * 3 + [array(experts, 64, 2048)],
-        in_specs=[SMEM, ANY, VMEM] + [ANY] * 4,
+        in_specs=[SMEM, ANY, VMEM] + [ANY] * (EARLY + 3),
         out_specs=[ANY] * 4,
         scratch_shapes=[
             pltpu.VMEM((4, 2 * experts, 64, 128), F32),
-            pltpu.VMEM(relay.shape, F32),
+            pltpu.VMEM((512 * EARLY, 128), F32),
             pltpu.VMEM((512, 128), F32),
             pltpu.VMEM((4, blocks, 64, 128), BF16),
-            pltpu.SemaphoreType.DMA((17,)),
+            pltpu.SemaphoreType.DMA((13 + 4 * EARLY,)),
             pltpu.SemaphoreType.DMA((8,)),
         ],
         compiler_params=params(46),
         cost_estimate=cost(5 * 2**20, 3 * 2**20),
         name="near_pieces",
-    )(f, w, scale, relay, *theirs)
+    )(f, w, scale, *early, across, theirs, rest)
 
 
 def split_kernel(f_ref, y_ref, chunk_ref, *refs):
@@ -407,36 +420,38 @@
 
 def served(w, router_weight, router_gain):
     experts, _, _ = w.shape
+    late, direct = experts - EARLY, experts - RELAY - EARLY
     position = lax.axis_index("fsdp")
     f = position.reshape(1)
     y = lax.axis_index("ep").reshape(1)
-    far_plane = 1 - position // 8
-
-    scale, swap, swap_early = local_maxima(f, w)
-    theirs_early = send(swap_early, 0, 0, 1)
+    far_plane, core = 1 - position // 8, position % 2
+
+    soon = lax.dynamic_slice(w, (experts - 1, 512 * far_plane, 0), (1, 512, 128)).reshape(512, 128)
+    soon = send(soon, 1, 0, 0)
+    scale, scale_theirs, swap = local_maxima(f, w)
+    scale = jnp.maximum(scale, send(scale_theirs, 0, 0, 1))
     peer = send(scale, 1, 0, 0)
     product = router_weight.T * router_gain.reshape(1, -1)
-    own = lax.dynamic_slice(
-        w.reshape(experts, 8, 2, 64, 128), (experts - EARLY, 4 * far_plane, position % 2, 0, 0), (EARLY, 4, 1, 64, 128)
-    )
-    other = lax.dynamic_slice(theirs_early, (0, 256 * far_plane, 0), (EARLY, 256, 128))
-    early = jnp.concatenate([own.reshape(-1, 128), other.reshape(-1, 128), product])
-    relay = send(early, 1, 0, 0)
+    early = lax.dynamic_slice(w, (late, 512 * far_plane, 0), (EARLY - 1, 512, 128))
+    early = jnp.concatenate([early.reshape(-1, 128), product])
+    early = send(early, 1, 0, 0)
     theirs = send(swap, 0, 0, 1)
     scale = jnp.maximum(scale, peer)
-    scale = jnp.maximum(scale, send(scale, 0, 0, 1))
     scale = functools.reduce(jnp.maximum, [scale] + [send(scale, 0, dx, 0) for dx in (1, 3, 2)])
-    direct = experts - RELAY - EARLY
-    swap_direct = swap_rows(f, w, RELAY, direct)
-    theirs_direct = send(swap_direct, 0, 0, 1)
+    swap_rest = swap_rows(f, w, RELAY, experts - RELAY)
+    rest = send(swap_rest, 0, 0, 1)
 
     (chunk,) = far_pieces(f, w, theirs, scale, 0, RELAY, True)
     forward = send(chunk, 1, 0, 0)
-    *pieces, final = near_pieces(f, w, scale, relay, (theirs, theirs_direct, theirs_early))
+    relay = [early[512 * j : 512 * (j + 1)] for j in range(EARLY - 1)] + [soon]
+    turned = jnp.stack(relay).reshape(EARLY, 4, 2, 64, 128)
+    turned = lax.dynamic_slice_in_dim(turned, 1 - core, 1, axis=2).reshape(EARLY * 256, 128)
+    turned = send(turned, 0, 0, 1)
+    *pieces, final = near_pieces(f, w, scale, [early] + [soon], turned, theirs, rest)
     plane = [send(piece, 0, k + 1, 0) for k, piece in enumerate(pieces)]
-    pieces = far_pieces(f, w, theirs_direct, scale, RELAY, direct, False)
+    pieces = far_pieces(f, w, rest, scale, RELAY, direct, False)
     across = [send(piece, 1, k, 0) for k, piece in enumerate(pieces)]
-    near = jnp.stack([product, relay[2 * EARLY * 256 :]]).astype(BF16)
+    near = jnp.stack([product, early[-16:]]).astype(BF16)
     near = jnp.concatenate([near, send(near, 0, 0, 1)])
     received = [near]
     for d in (1, 2, 3):
@@ -449,7 +464,7 @@
         final, router = place_relayed(k + 1, f, relayed[k], final, router)
     for k in range(4):
         final = place_far(k, RELAY, f, across[k], final)
-    own = lax.dynamic_slice_in_dim(scale, position * 64, 64, axis=1)
+    own = lax.dynamic_slice_in_dim(scale, position // 2 * 64, 64, axis=1)
     return final, own, router.T
 
 

time: 146 us -> 153 us (1.048)
  the two profiles are of different devices: /device:TPU:55 before, /device:TPU:72 now
where the time goes in v5:
time: 153 us
  waiting for transfers between devices  67.8 us (44%)
  starting transfers between devices  52.1 us (34%)
  Pallas kernels  28.7 us (19%)
  local copies, waits for them, and re-layouts  2.47 us (2%)
    ppermute x22, waiting for transfers between devices, send(): return lax.ppermute(piece, 'fsdp', route(dz, dx, dc))  60.6 us
    ppermute x22, starting transfers between devices, send(): return lax.ppermute(piece, 'fsdp', route(dz, dx, dc))  46.6 us
    ppermute x3, waiting for transfers between devices, served(): lax.ppermute(near, 'ep', [(i, (i + d) % 4) for i in range(4)])  7.19 us
    pallas_call x3, Pallas kernels, place_near(): pl.pallas_call(functools.partial(place_near_kernel, dx), out_shape=array(...  5.7 us
    ppermute x3, starting transfers between devices, served(): lax.ppermute(near, 'ep', [(i, (i + d) % 4) for i in range(4)])  5.53 us
    pallas_call x1, Pallas kernels, local_maxima(): pl.pallas_call(local_kernel, out_shape=[array(experts, rows // 2, kind=F3...  4.95 us
    pallas_call x2, Pallas kernels, far_pieces(): pl.pallas_call(functools.partial(far_kernel, (first, count, whole)), out_...  4.81 us
    pallas_call x1, Pallas kernels, near_pieces(): pl.pallas_call(near_kernel, out_shape=[array(blocks, 64, 128)] * 3 + [arr...  3.29 us
  transfers between devices with their start and end apart: 25, of which 14 were waited for; matrix products, arithmetic and copies ran while one was open for 2% of the time, Pallas kernels for 17%

profile of v5, /device:TPU:72, one launch (start us, length us, event | category | flops | bytes accessed | tf_op | source)
XLA Modules:
  0.0 152.9 jit_solution(6724845093464740019)
XLA Ops:
  0.6 2.7 %swap_rows.1 = f32[11,512,128]{2,1,0:T(8,128)} custom-call(s32[1]{0:T(128)} %bitcast.f_ref, f32[16,1024,128]{2,1,0:T(8,128)} %w_ref.9), custom_call_target="tpu_custom_call" | custom-call | flops 25165824 | bytes 6291456 | tf_op jit(solution)/shard_map/swap_rows/pallas_call | solution.py:136
  3.5 5.0 %local_maxima.1 = (f32[16,512]{1,0:T(8,128)S(1)}, f32[16,512]{1,0:T(8,128)S(1)}, f32[5,512,128]{2,1,0:T(8,128)}) custom-call(s32[1]{0:T(128)} %bitcast.f_ref, f32[16,1024,128]{2,1,0:T(8,128)} %w_ref.9), custom_call_target="tpu_custom_call" | custom-call | flops 50331648 | bytes 12582912 | tf_op jit(solution)/shard_map/local_maxima/pallas_call | solution.py:97
  9.0 1.8 %dynamic-slice_bitcast_fusion = (f32[512,128]{1,0:T(8,128)}, f32[512,128]{1,0:T(8,128)S(1)}) fusion(f32[16,1024,128]{2,1,0:T(8,128)} %w_ref.9, s32[]{:T(128)S(6)} %select_n.25), kind=kLoop, calls=%fused_computation.4 | loop fusion | bytes 1048580 | tf_op jit(solution)/shard_map/reshape | solution.py:429
  10.8 0.7 pad_maximum_fusion
  11.5 5.4 %collective-permute-start.12 = (f32[528,128]{1,0:T(8,128)}, f32[528,128]{1,0:T(8,128)S(1)}, u32[]{:S(2)}, u32[]{:S(2)}) collective-permute-start(f32[528,128]{1,0:T(8,128)} %pad_maximum_fusion), channel_id=1, source_target_pairs={{0,8},{1,9},{2,10},{3,11},{4,12},{5,13},{6,14},{7,15},{8,0},{9,1},... | collective-permute-start | bytes 811016 | tf_op jit(solution)/shard_map/ppermute | solution.py:48
  17.4 1.2 collective-permute-done.1
  18.7 5.4 %collective-permute-start.2 = (f32[16,512]{1,0:T(8,128)S(1)}, f32[16,512]{1,0:T(8,128)S(1)}, u32[]{:S(2)}, u32[]{:S(2)}) collective-permute-start(f32[16,512]{1,0:T(8,128)S(1)} %max.15), channel_id=1, source_target_pairs={{0,8},{1,9},{2,10},{3,11},{4,12},{5,13},{6,14},{7,15},{8,0},{9,1},... | collective-permute-start | bytes 98312 | tf_op jit(solution)/shard_map/ppermute | solution.py:48
  24.0 18.6 %collective-permute-done.2 = f32[16,512]{1,0:T(8,128)S(1)} collective-permute-done((f32[16,512]{1,0:T(8,128)S(1)}, f32[16,512]{1,0:T(8,128)S(1)}, u32[]{:S(2)}, u32[]{:S(2)}) %collective-permute-start.2) | collective-permute-done | bytes 32800 | tf_op jit(solution)/shard_map/ppermute | solution.py:48
  42.6 3.0 %collective-permute-start.5 = (f32[16,512]{1,0:T(8,128)S(1)}, f32[16,512]{1,0:T(8,128)S(1)}, u32[]{:S(2)}, u32[]{:S(2)}) collective-permute-start(f32[16,512]{1,0:T(8,128)S(1)} %max.16), channel_id=1, source_target_pairs={{0,4},{1,5},{2,6},{3,7},{4,0},{5,1},{6,2},{7,3},{8,12},{9,13},{10,... | collective-permute-start | bytes 98312 | tf_op jit(solution)/shard_map/ppermute | solution.py:48
  45.7 1.1 collective-permute-start.4
  46.8 1.0 collective-permute-start.3
  48.2 1.4 collective-permute-done.4
  49.6 2.5 %collective-permute-done.3 = f32[16,512]{1,0:T(8,128)S(1)} collective-permute-done((f32[16,512]{1,0:T(8,128)S(1)}, f32[16,512]{1,0:T(8,128)S(1)}, u32[]{:S(2)}, u32[]{:S(2)}) %collective-permute-start.3) | collective-permute-done | bytes 32800 | tf_op jit(solution)/shard_map/ppermute | solution.py:48
  52.1 2.3 %far_pieces.3 = bf16[10,256,128]{2,1,0:T(8,128)(2,1)} custom-call(s32[1]{0:T(128)} %bitcast.f_ref, f32[16,1024,128]{2,1,0:T(8,128)} %w_ref.9, f32[5,512,128]{2,1,0:T(8,128)} %collective-permute-done.10.theirs_ref.refs_3_, f32[16,512]{1,0:T(8,128)S(1)} %maximum_maximum_fusion.scale_ref), custom_call_target="tpu_custom_call" | custom-call | flops 12582912 | bytes 3145728 | tf_op jit(solution)/shard_map/far_pieces/pallas_call | solution.py:193
  54.4 5.2 %collective-permute-start.11 = (bf16[10,256,128]{2,1,0:T(8,128)(2,1)}, bf16[10,256,128]{2,1,0:T(8,128)(2,1)}, u32[]{:S(2)}, u32[]{:S(2)}) collective-permute-start(bf16[10,256,128]{2,1,0:T(8,128)(2,1)} %far_pieces.3), channel_id=1, source_target_pairs={{0,8},{1,9},{2,10},{3,11},{4,12},{5,13},{6,14},{7,15},{8,0},{9,1},... | collective-permute-start | bytes 1966088 | tf_op jit(solution)/shard_map/ppermute | solution.py:48
  59.6 3.3 %near_pieces.1 = (bf16[36,64,128]{2,1,0:T(8,128)(2,1)}, bf16[36,64,128]{2,1,0:T(8,128)(2,1)}, bf16[36,64,128]{2,1,0:T(8,128)(2,1)}, bf16[16,64,2048]{2,1,0:T(8,128)(2,1)}) custom-call(s32[1]{0:T(128)} %bitcast.f_ref, f32[16,1024,128]{2,1,0:T(8,128)} %w_ref.9, f32[16,512]{1,0:T(8,128)S(1)} %maximum_maximum_fusion.scale_ref, ...), custom_call_target="tpu_custom_call" | custom-call | flops 33554432 | bytes 8388608 | tf_op jit(solution)/shard_map/near_pieces/pallas_call | solution.py:288
  62.9 1.7 %collective-permute-start.23 = (bf16[36,64,128]{2,1,0:T(8,128)(2,1)}, bf16[36,64,128]{2,1,0:T(8,128)(2,1)}, u32[]{:S(2)}, u32[]{:S(2)}) collective-permute-start(bf16[36,64,128]{2,1,0:T(8,128)(2,1)} %get-tuple-element.37), channel_id=1, source_target_pairs={{0,4},{1,5},{2,6},{3,7},{4,0},{5,1},{6,2},{7,3},{8,12},{9,13},{10,... | collective-permute-start | bytes 1769480 | tf_op jit(solution)/shard_map/ppermute | solution.py:48
  65.0 1.2 collective-permute-done.13
  66.6 3.3 %collective-permute-done.16.refs_3_ = bf16[4,16,128]{2,1,0:T(8,128)(2,1)S(1)} collective-permute-done((bf16[4,16,128]{2,1,0:T(8,128)(2,1)S(1)}, bf16[4,16,128]{2,1,0:T(8,128)(2,1)S(1)}, u32[]{:S(2)}, u32[]{:S(2)}) %collective-permute-start.16) | collective-permute-done | bytes 16416 | tf_op jit(solution)/shard_map/ppermute | solution.py:458
  69.9 3.5 %collective-permute-start.15 = (bf16[4,16,128]{2,1,0:T(8,128)(2,1)S(1)}, bf16[4,16,128]{2,1,0:T(8,128)(2,1)S(1)}, u32[]{:S(2)}, u32[]{:S(2)}) collective-permute-start(bf16[4,16,128]{2,1,0:T(8,128)(2,1)S(1)} %pad_maximum_fusion.1.refs_0_), channel_id=1, source_target_pairs={{0,32},{16,48},{32,0},{48,16},{1,33},{17,49},{33,1},{49,17},{2,34}... | collective-permute-start | bytes 49160 | tf_op jit(solution)/shard_map/ppermute | solution.py:458
  73.4 1.7 %collective-permute-done.15.refs_2_ = bf16[4,16,128]{2,1,0:T(8,128)(2,1)S(1)} collective-permute-done((bf16[4,16,128]{2,1,0:T(8,128)(2,1)S(1)}, bf16[4,16,128]{2,1,0:T(8,128)(2,1)S(1)}, u32[]{:S(2)}, u32[]{:S(2)}) %collective-permute-start.15) | collective-permute-done | bytes 16416 | tf_op jit(solution)/shard_map/ppermute | solution.py:458
  75.1 1.6 %collective-permute-start.14 = (bf16[4,16,128]{2,1,0:T(8,128)(2,1)S(1)}, bf16[4,16,128]{2,1,0:T(8,128)(2,1)S(1)}, u32[]{:S(2)}, u32[]{:S(2)}) collective-permute-start(bf16[4,16,128]{2,1,0:T(8,128)(2,1)S(1)} %pad_maximum_fusion.1.refs_0_), channel_id=1, source_target_pairs={{0,16},{16,32},{32,48},{48,0},{1,17},{17,33},{33,49},{49,1},{2,18}... | collective-permute-start | bytes 49160 | tf_op jit(solution)/shard_map/ppermute | solution.py:458
  76.7 2.2 %collective-permute-done.14.refs_1_ = bf16[4,16,128]{2,1,0:T(8,128)(2,1)S(1)} collective-permute-done((bf16[4,16,128]{2,1,0:T(8,128)(2,1)S(1)}, bf16[4,16,128]{2,1,0:T(8,128)(2,1)S(1)}, u32[]{:S(2)}, u32[]{:S(2)}) %collective-permute-start.14) | collective-permute-done | bytes 16416 | tf_op jit(solution)/shard_map/ppermute | solution.py:458
  78.9 7.0 %collective-permute-done.11.chunk_ref = bf16[10,256,128]{2,1,0:T(8,128)(2,1)} collective-permute-done((bf16[10,256,128]{2,1,0:T(8,128)(2,1)}, bf16[10,256,128]{2,1,0:T(8,128)(2,1)}, u32[]{:S(2)}, u32[]{:S(2)}) %collective-permute-start.11) | collective-permute-done | bytes 655392 | tf_op jit(solution)/shard_map/ppermute | solution.py:48
  85.9 2.1 %split.1 = (bf16[14,64,128]{2,1,0:T(8,128)(2,1)S(1)}, bf16[14,64,128]{2,1,0:T(8,128)(2,1)S(1)}, bf16[14,64,128]{2,1,0:T(8,128)(2,1)}, bf16[16,64,2048]{2,1,0:T(8,128)(2,1)}, bf16[64,2048]{1,0:T(8,128)(2,1)}) custom-call(s32[1]{0:T(128)} %bitcast.f_ref, s32[1]{0:T(128)} %bitcast.1.y_ref, ...), custom_call_target="tpu_custom_call", output_to_operand_aliasing={{3}: (7, {})} | custom-call | flops 8388608 | bytes 2097152 | tf_op jit(solution)/shard_map/split/pallas_call | solution.py:349
  88.0 3.0 %collective-permute-start.20 = (bf16[14,64,128]{2,1,0:T(8,128)(2,1)S(1)}, bf16[14,64,128]{2,1,0:T(8,128)(2,1)S(1)}, u32[]{:S(2)}, u32[]{:S(2)}) collective-permute-start(bf16[14,64,128]{2,1,0:T(8,128)(2,1)S(1)} %get-tuple-element.34), channel_id=1, source_target_pairs={{0,4},{1,5},{2,6},{3,7},{4,0},{5,1},{6,2},{7,3},{8,12},{9,13},{10,... | collective-permute-start | bytes 688136 | tf_op jit(solution)/shard_map/ppermute | solution.py:48
  91.0 0.6 collective-permute-start.21
  91.7 2.5 %far_pieces.2 = (bf16[18,64,128]{2,1,0:T(8,128)(2,1)}, bf16[18,64,128]{2,1,0:T(8,128)(2,1)}, bf16[18,64,128]{2,1,0:T(8,128)(2,1)}, bf16[18,64,128]{2,1,0:T(8,128)(2,1)}) custom-call(s32[1]{0:T(128)} %bitcast.f_ref, f32[16,1024,128]{2,1,0:T(8,128)} %w_ref.9, f32[11,512,128]{2,1,0:T(8,128)S(1)} %collective-permute-done.theirs_ref.refs_4_, ...), custom_call_target="tpu_custom_call" | custom-call | flops 12582912 | bytes 3145728 | tf_op jit(solution)/shard_map/far_pieces/pallas_call | solution.py:193
  94.2 3.9 %collective-permute-done.20.piece_ref = bf16[14,64,128]{2,1,0:T(8,128)(2,1)S(1)} collective-permute-done((bf16[14,64,128]{2,1,0:T(8,128)(2,1)S(1)}, bf16[14,64,128]{2,1,0:T(8,128)(2,1)S(1)}, u32[]{:S(2)}, u32[]{:S(2)}) %collective-permute-start.20) | collective-permute-done | bytes 229408 | tf_op jit(solution)/shard_map/ppermute | solution.py:48
  98.1 5.4 %collective-permute-start.9 = (bf16[18,64,128]{2,1,0:T(8,128)(2,1)}, bf16[18,64,128]{2,1,0:T(8,128)(2,1)S(1)}, u32[]{:S(2)}, u32[]{:S(2)}) collective-permute-start(bf16[18,64,128]{2,1,0:T(8,128)(2,1)} %get-tuple-element.30), channel_id=1, source_target_pairs={{0,8},{1,9},{2,10},{3,11},{4,12},{5,13},{6,14},{7,15},{8,0},{9,1},... | collective-permute-start | bytes 884744 | tf_op jit(solution)/shard_map/ppermute | solution.py:48
  103.5 4.2 %collective-permute-start.8 = (bf16[18,64,128]{2,1,0:T(8,128)(2,1)}, bf16[18,64,128]{2,1,0:T(8,128)(2,1)S(1)}, u32[]{:S(2)}, u32[]{:S(2)}) collective-permute-start(bf16[18,64,128]{2,1,0:T(8,128)(2,1)} %get-tuple-element.29), channel_id=1, source_target_pairs={{0,10},{1,11},{2,12},{3,13},{4,14},{5,15},{6,8},{7,9},{8,2},{9,3},... | collective-permute-start | bytes 884744 | tf_op jit(solution)/shard_map/ppermute | solution.py:48
  107.7 2.8 %collective-permute-start.7 = (bf16[18,64,128]{2,1,0:T(8,128)(2,1)}, bf16[18,64,128]{2,1,0:T(8,128)(2,1)S(1)}, u32[]{:S(2)}, u32[]{:S(2)}) collective-permute-start(bf16[18,64,128]{2,1,0:T(8,128)(2,1)} %get-tuple-element.28), channel_id=1, source_target_pairs={{0,12},{1,13},{2,14},{3,15},{4,8},{5,9},{6,10},{7,11},{8,4},{9,5},... | collective-permute-start | bytes 884744 | tf_op jit(solution)/shard_map/ppermute | solution.py:48
  110.5 5.5 %collective-permute-start.6 = (bf16[18,64,128]{2,1,0:T(8,128)(2,1)}, bf16[18,64,128]{2,1,0:T(8,128)(2,1)S(1)}, u32[]{:S(2)}, u32[]{:S(2)}) collective-permute-start(bf16[18,64,128]{2,1,0:T(8,128)(2,1)} %get-tuple-element.27), channel_id=1, source_target_pairs={{0,14},{1,15},{2,8},{3,9},{4,10},{5,11},{6,12},{7,13},{8,6},{9,7},... | collective-permute-start | bytes 884744 | tf_op jit(solution)/shard_map/ppermute | solution.py:48
  116.0 0.6 collective-permute-start.19
  116.6 0.7 constant_dynamic-slice_fusion
  117.3 1.9 %place_near.3._ = bf16[16,64,2048]{2,1,0:T(8,128)(2,1)} custom-call(s32[1]{0:T(128)} %bitcast.f_ref, bf16[36,64,128]{2,1,0:T(8,128)(2,1)} %collective-permute-done.24.piece_ref, bf16[16,64,2048]{2,1,0:T(8,128)(2,1)} %get-tuple-element.39._), custom_call_target="tpu_custom_call", output_to_operand_aliasing={{}: (2, {})} | custom-call | flops 4194304 | bytes 1048576 | tf_op jit(solution)/shard_map/place_near/pallas_call | solution.py:387
  119.2 1.9 %place_near.4._ = bf16[16,64,2048]{2,1,0:T(8,128)(2,1)} custom-call(s32[1]{0:T(128)} %bitcast.f_ref, bf16[36,64,128]{2,1,0:T(8,128)(2,1)} %collective-permute-done.23.piece_ref, bf16[16,64,2048]{2,1,0:T(8,128)(2,1)} %place_near.3._), custom_call_target="tpu_custom_call", output_to_operand_aliasing={{}: (2, {})} | custom-call | flops 4194304 | bytes 1048576 | tf_op jit(solution)/shard_map/place_near/pallas_call | solution.py:387
  121.1 1.9 %place_near.5._ = bf16[16,64,2048]{2,1,0:T(8,128)(2,1)} custom-call(s32[1]{0:T(128)} %bitcast.f_ref, bf16[36,64,128]{2,1,0:T(8,128)(2,1)} %collective-permute-done.22.piece_ref, bf16[16,64,2048]{2,1,0:T(8,128)(2,1)} %place_near.4._), custom_call_target="tpu_custom_call", output_to_operand_aliasing={{}: (2, {})} | custom-call | flops 4194304 | bytes 1048576 | tf_op jit(solution)/shard_map/place_near/pallas_call | solution.py:387
  123.0 0.7 place_relayed.3
  123.8 0.7 place_relayed.4
  124.6 0.7 place_relayed.5
  125.4 0.7 place_far.4._
  126.1 13.6 %collective-permute-done.8.piece_ref = bf16[18,64,128]{2,1,0:T(8,128)(2,1)S(1)} collective-permute-done((bf16[18,64,128]{2,1,0:T(8,128)(2,1)}, bf16[18,64,128]{2,1,0:T(8,128)(2,1)S(1)}, u32[]{:S(2)}, u32[]{:S(2)}) %collective-permute-start.8) | collective-permute-done | bytes 294944 | tf_op jit(solution)/shard_map/ppermute | solution.py:48
  139.7 0.7 place_far.5._
  140.4 7.9 %collective-permute-done.7.piece_ref = bf16[18,64,128]{2,1,0:T(8,128)(2,1)S(1)} collective-permute-done((bf16[18,64,128]{2,1,0:T(8,128)(2,1)}, bf16[18,64,128]{2,1,0:T(8,128)(2,1)S(1)}, u32[]{:S(2)}, u32[]{:S(2)}) %collective-permute-start.7) | collective-permute-done | bytes 294944 | tf_op jit(solution)/shard_map/ppermute | solution.py:48
  148.4 0.7 place_far.6._
  149.1 2.9 %collective-permute-done.6.piece_ref = bf16[18,64,128]{2,1,0:T(8,128)(2,1)S(1)} collective-permute-done((bf16[18,64,128]{2,1,0:T(8,128)(2,1)}, bf16[18,64,128]{2,1,0:T(8,128)(2,1)S(1)}, u32[]{:S(2)}, u32[]{:S(2)}) %collective-permute-start.6) | collective-permute-done | bytes 294944 | tf_op jit(solution)/shard_map/ppermute | solution.py:48
  152.0 0.7 place_far.7
  (34 shorter events, 2.5 us)
Async XLA Ops:
  3.3 7.4 %copy-start = (f32[128,16]{0,1:T(8,128)S(1)}, f32[128,16]{0,1:T(8,128)}, u32[]{:S(2)}) copy-start(f32[128,16]{0,1:T(8,128)} %param.4) | copy-start | bytes 24580
  3.4 7.4 %copy-start.1 = (f32[128]{0:T(128)S(1)}, f32[128]{0:T(128)}, u32[]{:S(2)}) copy-start(f32[128]{0:T(128)} %param.5) | copy-start | bytes 1540
  3.4 56.2 %collective-permute-start = (f32[11,512,128]{2,1,0:T(8,128)}, f32[11,512,128]{2,1,0:T(8,128)S(1)}, u32[]{:S(2)}, u32[]{:S(2)}) collective-permute-start(f32[11,512,128]{2,1,0:T(8,128)} %swap_rows.1), channel_id=1, source_target_pairs={{0,1},{1,0},{2,3},{3,2},{4,5},{5,4},{6,7},{7,6},{8,9},{9,8},{10,11... | collective-permute-start | bytes 8650760 | tf_op jit(solution)/shard_map/ppermute | solution.py:48
  8.4 43.6 %collective-permute-start.10 = (f32[5,512,128]{2,1,0:T(8,128)}, f32[5,512,128]{2,1,0:T(8,128)}, u32[]{:S(2)}, u32[]{:S(2)}) collective-permute-start(f32[5,512,128]{2,1,0:T(8,128)} %get-tuple-element.31), channel_id=1, source_target_pairs={{0,1},{1,0},{2,3},{3,2},{4,5},{5,4},{6,7},{7,6},{8,9},{9,8},{10,11... | collective-permute-start | bytes 3932168 | tf_op jit(solution)/shard_map/ppermute | solution.py:48
  11.5 34.2 %collective-permute-start.12 = (f32[528,128]{1,0:T(8,128)}, f32[528,128]{1,0:T(8,128)S(1)}, u32[]{:S(2)}, u32[]{:S(2)}) collective-permute-start(f32[528,128]{1,0:T(8,128)} %pad_maximum_fusion), channel_id=1, source_target_pairs={{0,8},{1,9},{2,10},{3,11},{4,12},{5,13},{6,14},{7,15},{8,0},{9,1},... | collective-permute-start | bytes 811016 | tf_op jit(solution)/shard_map/ppermute | solution.py:48
  16.9 29.9 %collective-permute-start.17 = (f32[512,128]{1,0:T(8,128)}, f32[512,128]{1,0:T(8,128)S(1)}, u32[]{:S(2)}, u32[]{:S(2)}) collective-permute-start(f32[512,128]{1,0:T(8,128)} %get-tuple-element.49), channel_id=1, source_target_pairs={{0,8},{1,9},{2,10},{3,11},{4,12},{5,13},{6,14},{7,15},{8,0},{9,1},... | collective-permute-start | bytes 786440 | tf_op jit(solution)/shard_map/ppermute | solution.py:48
  17.4 1.2 collective-permute-start.1
  18.7 24.0 %collective-permute-start.2 = (f32[16,512]{1,0:T(8,128)S(1)}, f32[16,512]{1,0:T(8,128)S(1)}, u32[]{:S(2)}, u32[]{:S(2)}) collective-permute-start(f32[16,512]{1,0:T(8,128)S(1)} %max.15), channel_id=1, source_target_pairs={{0,8},{1,9},{2,10},{3,11},{4,12},{5,13},{6,14},{7,15},{8,0},{9,1},... | collective-permute-start | bytes 98312 | tf_op jit(solution)/shard_map/ppermute | solution.py:48
  42.6 5.5 %collective-permute-start.5 = (f32[16,512]{1,0:T(8,128)S(1)}, f32[16,512]{1,0:T(8,128)S(1)}, u32[]{:S(2)}, u32[]{:S(2)}) collective-permute-start(f32[16,512]{1,0:T(8,128)S(1)} %max.16), channel_id=1, source_target_pairs={{0,4},{1,5},{2,6},{3,7},{4,0},{5,1},{6,2},{7,3},{8,12},{9,13},{10,... | collective-permute-start | bytes 98312 | tf_op jit(solution)/shard_map/ppermute | solution.py:48
  45.7 3.9 %collective-permute-start.4 = (f32[16,512]{1,0:T(8,128)S(1)}, f32[16,512]{1,0:T(8,128)S(1)}, u32[]{:S(2)}, u32[]{:S(2)}) collective-permute-start(f32[16,512]{1,0:T(8,128)S(1)} %max.16), channel_id=1, source_target_pairs={{0,6},{1,7},{2,0},{3,1},{4,2},{5,3},{6,4},{7,5},{8,14},{9,15},{10,... | collective-permute-start | bytes 98312 | tf_op jit(solution)/shard_map/ppermute | solution.py:48
  46.8 5.2 %collective-permute-start.3 = (f32[16,512]{1,0:T(8,128)S(1)}, f32[16,512]{1,0:T(8,128)S(1)}, u32[]{:S(2)}, u32[]{:S(2)}) collective-permute-start(f32[16,512]{1,0:T(8,128)S(1)} %max.16), channel_id=1, source_target_pairs={{0,2},{1,3},{2,4},{3,5},{4,6},{5,7},{6,0},{7,1},{8,10},{9,11},{10,... | collective-permute-start | bytes 98312 | tf_op jit(solution)/shard_map/ppermute | solution.py:48
  48.2 11.4 %collective-permute-start.18 = (f32[512,128]{1,0:T(8,128)S(1)}, f32[512,128]{1,0:T(8,128)S(1)}, u32[]{:S(2)}, u32[]{:S(2)}) collective-permute-start(f32[512,128]{1,0:T(8,128)S(1)} %bitcast.20), channel_id=1, source_target_pairs={{0,1},{1,0},{2,3},{3,2},{4,5},{5,4},{6,7},{7,6},{8,9},{9,8},{10,11... | collective-permute-start | bytes 786440 | tf_op jit(solution)/shard_map/ppermute | solution.py:48
  54.4 31.5 %collective-permute-start.11 = (bf16[10,256,128]{2,1,0:T(8,128)(2,1)}, bf16[10,256,128]{2,1,0:T(8,128)(2,1)}, u32[]{:S(2)}, u32[]{:S(2)}) collective-permute-start(bf16[10,256,128]{2,1,0:T(8,128)(2,1)} %far_pieces.3), channel_id=1, source_target_pairs={{0,8},{1,9},{2,10},{3,11},{4,12},{5,13},{6,14},{7,15},{8,0},{9,1},... | collective-permute-start | bytes 1966088 | tf_op jit(solution)/shard_map/ppermute | solution.py:48
  62.9 44.9 %collective-permute-start.22 = (bf16[36,64,128]{2,1,0:T(8,128)(2,1)}, bf16[36,64,128]{2,1,0:T(8,128)(2,1)}, u32[]{:S(2)}, u32[]{:S(2)}) collective-permute-start(bf16[36,64,128]{2,1,0:T(8,128)(2,1)} %get-tuple-element.36), channel_id=1, source_target_pairs={{0,6},{1,7},{2,0},{3,1},{4,2},{5,3},{6,4},{7,5},{8,14},{9,15},{10,... | collective-permute-start | bytes 1769480 | tf_op jit(solution)/shard_map/ppermute | solution.py:48
  62.9 47.6 %collective-permute-start.23 = (bf16[36,64,128]{2,1,0:T(8,128)(2,1)}, bf16[36,64,128]{2,1,0:T(8,128)(2,1)}, u32[]{:S(2)}, u32[]{:S(2)}) collective-permute-start(bf16[36,64,128]{2,1,0:T(8,128)(2,1)} %get-tuple-element.37), channel_id=1, source_target_pairs={{0,4},{1,5},{2,6},{3,7},{4,0},{5,1},{6,2},{7,3},{8,12},{9,13},{10,... | collective-permute-start | bytes 1769480 | tf_op jit(solution)/shard_map/ppermute | solution.py:48
  64.7 51.4 %collective-permute-start.24 = (bf16[36,64,128]{2,1,0:T(8,128)(2,1)}, bf16[36,64,128]{2,1,0:T(8,128)(2,1)}, u32[]{:S(2)}, u32[]{:S(2)}) collective-permute-start(bf16[36,64,128]{2,1,0:T(8,128)(2,1)} %get-tuple-element.38), channel_id=1, source_target_pairs={{0,2},{1,3},{2,4},{3,5},{4,6},{5,7},{6,0},{7,1},{8,10},{9,11},{10,... | collective-permute-start | bytes 1769480 | tf_op jit(solution)/shard_map/ppermute | solution.py:48
  65.0 1.2 collective-permute-start.13
  66.1 3.7 %collective-permute-start.16 = (bf16[4,16,128]{2,1,0:T(8,128)(2,1)S(1)}, bf16[4,16,128]{2,1,0:T(8,128)(2,1)S(1)}, u32[]{:S(2)}, u32[]{:S(2)}) collective-permute-start(bf16[4,16,128]{2,1,0:T(8,128)(2,1)S(1)} %pad_maximum_fusion.1.refs_0_), channel_id=1, source_target_pairs={{0,48},{16,0},{32,16},{48,32},{1,49},{17,1},{33,17},{49,33},{2,50}... | collective-permute-start | bytes 49160 | tf_op jit(solution)/shard_map/ppermute | solution.py:458
  69.9 5.2 %collective-permute-start.15 = (bf16[4,16,128]{2,1,0:T(8,128)(2,1)S(1)}, bf16[4,16,128]{2,1,0:T(8,128)(2,1)S(1)}, u32[]{:S(2)}, u32[]{:S(2)}) collective-permute-start(bf16[4,16,128]{2,1,0:T(8,128)(2,1)S(1)} %pad_maximum_fusion.1.refs_0_), channel_id=1, source_target_pairs={{0,32},{16,48},{32,0},{48,16},{1,33},{17,49},{33,1},{49,17},{2,34}... | collective-permute-start | bytes 49160 | tf_op jit(solution)/shard_map/ppermute | solution.py:458
  75.1 3.7 %collective-permute-start.14 = (bf16[4,16,128]{2,1,0:T(8,128)(2,1)S(1)}, bf16[4,16,128]{2,1,0:T(8,128)(2,1)S(1)}, u32[]{:S(2)}, u32[]{:S(2)}) collective-permute-start(bf16[4,16,128]{2,1,0:T(8,128)(2,1)S(1)} %pad_maximum_fusion.1.refs_0_), channel_id=1, source_target_pairs={{0,16},{16,32},{32,48},{48,0},{1,17},{17,33},{33,49},{49,1},{2,18}... | collective-permute-start | bytes 49160 | tf_op jit(solution)/shard_map/ppermute | solution.py:458
  88.0 10.1 %collective-permute-start.20 = (bf16[14,64,128]{2,1,0:T(8,128)(2,1)S(1)}, bf16[14,64,128]{2,1,0:T(8,128)(2,1)S(1)}, u32[]{:S(2)}, u32[]{:S(2)}) collective-permute-start(bf16[14,64,128]{2,1,0:T(8,128)(2,1)S(1)} %get-tuple-element.34), channel_id=1, source_target_pairs={{0,4},{1,5},{2,6},{3,7},{4,0},{5,1},{6,2},{7,3},{8,12},{9,13},{10,... | collective-permute-start | bytes 688136 | tf_op jit(solution)/shard_map/ppermute | solution.py:48
  91.0 12.5 %collective-permute-start.21 = (bf16[14,64,128]{2,1,0:T(8,128)(2,1)S(1)}, bf16[14,64,128]{2,1,0:T(8,128)(2,1)S(1)}, u32[]{:S(2)}, u32[]{:S(2)}) collective-permute-start(bf16[14,64,128]{2,1,0:T(8,128)(2,1)S(1)} %get-tuple-element.35), channel_id=1, source_target_pairs={{0,2},{1,3},{2,4},{3,5},{4,6},{5,7},{6,0},{7,1},{8,10},{9,11},{10,... | collective-permute-start | bytes 688136 | tf_op jit(solution)/shard_map/ppermute | solution.py:48
  98.1 27.3 %collective-permute-start.9 = (bf16[18,64,128]{2,1,0:T(8,128)(2,1)}, bf16[18,64,128]{2,1,0:T(8,128)(2,1)S(1)}, u32[]{:S(2)}, u32[]{:S(2)}) collective-permute-start(bf16[18,64,128]{2,1,0:T(8,128)(2,1)} %get-tuple-element.30), channel_id=1, source_target_pairs={{0,8},{1,9},{2,10},{3,11},{4,12},{5,13},{6,14},{7,15},{8,0},{9,1},... | collective-permute-start | bytes 884744 | tf_op jit(solution)/shard_map/ppermute | solution.py:48
  103.5 36.2 %collective-permute-start.8 = (bf16[18,64,128]{2,1,0:T(8,128)(2,1)}, bf16[18,64,128]{2,1,0:T(8,128)(2,1)S(1)}, u32[]{:S(2)}, u32[]{:S(2)}) collective-permute-start(bf16[18,64,128]{2,1,0:T(8,128)(2,1)} %get-tuple-element.29), channel_id=1, source_target_pairs={{0,10},{1,11},{2,12},{3,13},{4,14},{5,15},{6,8},{7,9},{8,2},{9,3},... | collective-permute-start | bytes 884744 | tf_op jit(solution)/shard_map/ppermute | solution.py:48
  107.7 40.6 %collective-permute-start.7 = (bf16[18,64,128]{2,1,0:T(8,128)(2,1)}, bf16[18,64,128]{2,1,0:T(8,128)(2,1)S(1)}, u32[]{:S(2)}, u32[]{:S(2)}) collective-permute-start(bf16[18,64,128]{2,1,0:T(8,128)(2,1)} %get-tuple-element.28), channel_id=1, source_target_pairs={{0,12},{1,13},{2,14},{3,15},{4,8},{5,9},{6,10},{7,11},{8,4},{9,5},... | collective-permute-start | bytes 884744 | tf_op jit(solution)/shard_map/ppermute | solution.py:48
  110.5 41.5 %collective-permute-start.6 = (bf16[18,64,128]{2,1,0:T(8,128)(2,1)}, bf16[18,64,128]{2,1,0:T(8,128)(2,1)S(1)}, u32[]{:S(2)}, u32[]{:S(2)}) collective-permute-start(bf16[18,64,128]{2,1,0:T(8,128)(2,1)} %get-tuple-element.27), channel_id=1, source_target_pairs={{0,14},{1,15},{2,8},{3,9},{4,10},{5,11},{6,12},{7,13},{8,6},{9,7},... | collective-permute-start | bytes 884744 | tf_op jit(solution)/shard_map/ppermute | solution.py:48
  116.0 8.5 %collective-permute-start.19 = (bf16[14,64,128]{2,1,0:T(8,128)(2,1)}, bf16[14,64,128]{2,1,0:T(8,128)(2,1)S(1)}, u32[]{:S(2)}, u32[]{:S(2)}) collective-permute-start(bf16[14,64,128]{2,1,0:T(8,128)(2,1)} %get-tuple-element.33), channel_id=1, source_target_pairs={{0,6},{1,7},{2,0},{3,1},{4,2},{5,3},{6,4},{7,5},{8,14},{9,15},{10,... | collective-permute-start | bytes 688136 | tf_op jit(solution)/shard_map/ppermute | solution.py:48
